TPU v7x, 512 devices: a whole 4x4x16 slice. The times are simulated.
512 devices in a mesh: expert: 8 (over y, core), dp: 16 (over z), tensor: 4 (over x).
Axes of the slice: x: 4, y: 4, z: 16, core: 2. Of those that a mesh axis runs over, the one named last changes fastest.
Arguments:
- tokens: bfloat16 [2048, 4096], P(('expert', 'dp')), may hold values from -6 to 6
- expert_ids: int32 [2048, 2], P(('expert', 'dp')), may hold values from 0 to 7, all different within a row; in each aligned block of 16 rows (0 to 15, 16 to 31, ...) at most 6 rows name the same one
- route_weight: float32 [2048, 2], P(('expert', 'dp')), may hold values from 0.2 to 1
- gate_weight: bfloat16 [8, 4096, 8192], P('expert', None, ('dp', 'tensor')), may hold values from -0.09375 to 0.09375
- up_weight: bfloat16 [8, 4096, 8192], P('expert', None, ('dp', 'tensor')), may hold values from -0.09375 to 0.09375
- down_weight: bfloat16 [8, 8192, 4096], P('expert', 'dp', 'tensor'), may hold values from -0.125 to 0.125
- past_layers: bfloat16 [8, 2048, 4096], P(None, ('expert', 'dp'), 'tensor'), may hold values from -6 to 6
- dwa_weight: float32 [9], replicated, may hold values from 0.3 to 1.2
Outputs:
- mixed: bfloat16 [2048, 4096], P(('expert', 'dp'), 'tensor')
Inputs may be any that keep to these rules, and one draw needn't show every extreme that they name: `expert_ids`: each row names 2 different experts. In each aligned block of 16 rows (the rows of one device) no expert is named more than 6 times; in some blocks one expert is named exactly 6 times.
All inputs are finite; a program needn't handle non-finite values.
Results may differ from a plain program's by a relative error of at most 0.009.
Values may be sent and summed in bfloat16 or wider, within the bound.
No kernel may reach another device: no remote copies, remote signals or barrier semaphores. Data moves between devices by JAX's collectives and lax.ppermute only.
A program may use at most 64 MiB of HBM per device.

v0:
```python
import jax
import jax.numpy as jnp
from jax import lax
from jax.sharding import PartitionSpec as P


def from_everyone(shard, axis):
    count = lax.axis_size(axis)
    return lax.all_to_all(
        jnp.broadcast_to(shard[None], (count, *shard.shape)), axis, 0, 0, tiled=True
    )


def joined_along(tiles, dim):
    dims = list(tiles.shape[1:])
    dims[dim] *= tiles.shape[0]
    return jnp.moveaxis(tiles, 0, dim).reshape(dims)


def gathered_copies(shard, axis, dim):
    tiles = from_everyone(shard, axis)
    return joined_along(tiles, dim)


def assignment_slots(expert_ids, experts, capacity):
    flat_ids = expert_ids.reshape(-1)
    matches = (flat_ids[:, None] == jnp.arange(experts, dtype=jnp.int32)[None, :]).astype(jnp.int32)
    earlier = jnp.cumsum(matches, axis=0) - matches
    slot_ids = jnp.sum(earlier * matches, axis=1)
    return flat_ids * capacity + slot_ids


def selector(expert_ids, experts, capacity):
    targets = assignment_slots(expert_ids, experts, capacity)
    matched = targets[None, :] == jnp.arange(experts * capacity, dtype=jnp.int32)[:, None]
    chosen = matched.reshape(experts * capacity, expert_ids.shape[0], expert_ids.shape[1])
    return jnp.sum(chosen.astype(jnp.float32), axis=2).astype(jnp.bfloat16)


def per_device(
    tokens, expert_ids, route_weight, gate_weight, up_weight, down_weight, past_layers, dwa_weight
):
    experts = lax.axis_size("expert")
    tok_rows, feature_width = tokens.shape
    chosen_count = expert_ids.shape[1]
    capacity = min(tok_rows, 3 * chosen_count * tok_rows // (2 * experts))
    w_gate = gate_weight[0]
    w_up = up_weight[0]
    w_down = down_weight[0]
    targets = assignment_slots(expert_ids, experts, capacity)
    selected = selector(expert_ids, experts, capacity)
    packed = jnp.dot(selected, tokens, preferred_element_type=jnp.float32).astype(jnp.bfloat16)
    packed = packed.reshape(experts, capacity, feature_width)
    arrived = lax.all_to_all(packed, "expert", split_axis=0, concat_axis=0, tiled=True)
    block_rows = lax.all_gather(
        arrived.reshape(experts * capacity, feature_width), "dp", axis=0, tiled=True
    )
    gate = jnp.dot(block_rows, w_gate, preferred_element_type=jnp.float32)
    up = jnp.dot(block_rows, w_up, preferred_element_type=jnp.float32)
    hidden = (jax.nn.silu(gate) * up).astype(jnp.bfloat16)
    hidden_wide = gathered_copies(hidden, "tensor", 1)
    expert_out = lax.psum_scatter(
        jnp.dot(hidden_wide, w_down, preferred_element_type=jnp.float32),
        "dp",
        scatter_dimension=0,
        tiled=True,
    ).astype(jnp.bfloat16)
    quarter = expert_out.shape[1]
    returned_rows = lax.all_to_all(
        expert_out.reshape(experts, capacity, quarter),
        "expert",
        split_axis=0,
        concat_axis=0,
        tiled=True,
    )
    returned_rows = returned_rows.reshape(experts * capacity, quarter)
    fetched = returned_rows[targets].astype(jnp.float32).reshape(tok_rows, chosen_count, quarter)
    shares = route_weight / jnp.sum(route_weight, axis=1, keepdims=True)
    expert_mix = jnp.sum(fetched * shares[:, :, None], axis=1)
    first_column = lax.axis_index("tensor") * quarter
    residual = lax.dynamic_slice_in_dim(tokens, first_column, quarter, 1).astype(jnp.float32)
    current = residual + expert_mix
    depth = past_layers.shape[0]
    history = jnp.einsum("j,jtd->td", dwa_weight[:depth], past_layers.astype(jnp.float32))
    return (dwa_weight[depth] * current + history).astype(jnp.bfloat16)


def solution(mesh):
    return jax.shard_map(
        per_device,
        mesh=mesh,
        in_specs=(
            P(("expert", "dp"), None),
            P(("expert", "dp"), None),
            P(("expert", "dp"), None),
            P("expert", None, ("dp", "tensor")),
            P("expert", None, ("dp", "tensor")),
            P("expert", "dp", "tensor"),
            P(None, ("expert", "dp"), "tensor"),
            P(),
        ),
        out_specs=P(("expert", "dp"), "tensor"),
        check_vma=False,
    )
```

profile of v0, /device:TPU:1, one launch (start us, length us, event | category | flops | bytes accessed | tf_op | source)
XLA Modules:
  0.0 233.8 jit_solution(14384665700464559694)
XLA Ops:
  6.5 0.9 copy.16
  7.4 0.1 eq.15
  7.5 0.1 fusion.9
  7.6 0.1 reduce_window_sum.12
  7.7 0.2 select_reduce_fusion
  7.8 0.1 reduce_sum.45
  8.0 0.1 copy.18
  8.0 0.1 convert_reduce_fusion
  8.1 1.2 convolution_convert_fusion
  9.3 0.1 reshape.70
  9.5 18.6 %all_to_all.15 = bf16[8,6,4096]{2,1,0:T(8,128)(2,1)S(1)} all-to-all(bf16[8,6,4096]{2,1,0:T(8,128)(2,1)S(1)} %reshape.70), channel_id=1, replica_groups=mesh['expert'=8,'dp'=16,'tensor'=4] {'expert'}, dimensions={0} | all-to-all | bytes 786432 | tf_op jit(solution)/shard_map/all_to_all | solution.py:54
  28.0 0.9 reshape.71
  29.0 82.5 %all-gather.2.cloned.1.call-done = bf16[768,4096]{1,0:T(8,128)(2,1)} async-done(((bf16[48,4096]{1,0:T(8,128)(2,1)}), bf16[768,4096]{1,0:T(8,128)(2,1)}) %all-gather.2.cloned.1.call-update) | async-done | bytes 6291472 | tf_op jit(solution)/shard_map/all_gather | solution.py:55
  111.5 5.0 %fusion.4 = f32[768,128]{1,0:T(8,128)S(1)} fusion(bf16[768,4096]{1,0:T(8,128)(2,1)} %all-gather.2.cloned.1.call-done, bf16[1,4096,128]{2,1,0:T(8,128)(2,1)} %param.11), kind=kOutput, calls=%fused_computation.7 | convolution fusion | flops 805306368 | bytes 7733248 | tf_op jit(solution)/shard_map/dot_general | solution.py:58
  116.5 1.8 fusion
  118.3 0.1 copy.19
  118.4 0.1 broadcast_in_dim.2
  118.5 12.1 %all_to_all.16 = bf16[4,768,128]{1,2,0:T(8,128)(2,1)S(1)} all-to-all(bf16[4,768,128]{1,2,0:T(8,128)(2,1)S(1)} %broadcast_in_dim.2), channel_id=1, replica_groups=mesh['expert'=8,'dp'=16,'tensor'=4] {'tensor'}, dimensions={0} | all-to-all | bytes 1572864 | tf_op jit(solution)/shard_map/all_to_all | solution.py:9
  130.7 2.7 %fusion.1 = f32[768,1024]{1,0:T(8,128)} fusion(bf16[768,512]{0,1:T(8,128)(2,1)S(1)} %bitcast.31, bf16[1,512,1024]{2,1,0:T(8,128)(2,1)S(1)} %copy-done), kind=kOutput, calls=%fused_computation.4 | convolution fusion | flops 805306368 | bytes 4980736 | tf_op jit(solution)/shard_map/dot_general | solution.py:63
  133.4 0.1 mul.52
  133.5 0.1 copy.20
  133.6 0.7 slice.6
  134.2 0.3 fusion.6
  134.5 68.1 %reduce-scatter.2.cloned.1.call-done = f32[48,1024]{1,0:T(8,128)} async-done(((f32[768,1024]{1,0:T(8,128)}), f32[48,1024]{1,0:T(8,128)}) %reduce-scatter.2.cloned.1.call-update) | async-done | bytes 196624 | tf_op jit(solution)/shard_map/reduce_scatter | solution.py:62
  202.6 0.9 convert_element_type.39
  203.5 0.7 reshape.73
  204.2 14.5 %all-to-all-start.2 = ((bf16[8,6,1024]{2,1,0:T(8,128)(2,1)}), bf16[8,6,1024]{2,1,0:T(8,128)(2,1)S(1)}, u32[]{:S(2)}, u32[]{:S(2)}) async-start(bf16[8,6,1024]{2,1,0:T(8,128)(2,1)} %reshape.73), calls=%async_computation.3 | async-start | bytes 262144 | tf_op jit(solution)/shard_map/all_to_all | solution.py:69
  218.7 5.2 %all-to-all-done.2 = bf16[8,6,1024]{2,1,0:T(8,128)(2,1)S(1)} async-done(((bf16[8,6,1024]{2,1,0:T(8,128)(2,1)}), bf16[8,6,1024]{2,1,0:T(8,128)(2,1)S(1)}, u32[]{:S(2)}, u32[]{:S(2)}) %all-to-all-start.2) | async-done | bytes 98336 | tf_op jit(solution)/shard_map/all_to_all | solution.py:69
  224.0 0.6 gather_fusion
  224.6 0.1 reshape.75
  224.7 0.2 multiply_reduce_fusion
  224.9 2.0 fusion.8
  (22 shorter events, 0.2 us)
Async XLA Ops:
  6.5 124.1 %copy-start = (bf16[1,512,1024]{2,1,0:T(8,128)(2,1)S(1)}, bf16[1,512,1024]{2,1,0:T(8,128)(2,1)}, u32[]{:S(2)}) copy-start(bf16[1,512,1024]{2,1,0:T(8,128)(2,1)} %param.13) | copy-start | bytes 3145732
  6.5 109.9 %copy-start.5 = (bf16[1,4096,128]{2,1,0:T(8,128)(2,1)S(1)}, bf16[1,4096,128]{2,1,0:T(8,128)(2,1)}, u32[]{:S(2)}) copy-start(bf16[1,4096,128]{2,1,0:T(8,128)(2,1)} %param.12) | copy-start | bytes 3145732
  6.5 104.9 %all-gather.2.cloned.1.call-start = ((), (), s32[]{:S(2)}) async-start(), calls=%async_computation.4 | async-start | bytes 6684672 | tf_op jit(solution)/shard_map/all_gather | solution.py:55
  28.9 173.6 %reduce-scatter.2.cloned.1.call-start = ((), (), s32[]{:S(2)}) async-start(), calls=%async_computation.5 | async-start | bytes 3342336 | tf_op jit(solution)/shard_map/reduce_scatter | solution.py:62
  111.5 5.0 %copy-start.4 = (bf16[768,4096]{1,0:T(8,128)(2,1)S(1)}, bf16[768,4096]{1,0:T(8,128)(2,1)}, u32[]{:S(2)}) copy-start(bf16[768,4096]{1,0:T(8,128)(2,1)} %all-gather.2.cloned.1.call-done) | copy-start | bytes 18874372
  118.3 15.2 %copy-start.2 = (f32[16,2]{0,1:T(2,128)S(1)}, f32[16,2]{0,1:T(2,128)}, u32[]{:S(2)}) copy-start(f32[16,2]{0,1:T(2,128)} %param.10) | copy-start | bytes 388
  118.3 15.3 %copy-start.3 = (f32[9]{0:T(128)S(1)}, f32[9]{0:T(128)}, u32[]{:S(2)}) copy-start(f32[9]{0:T(128)} %param.15) | copy-start | bytes 112
  118.3 16.0 %copy-start.1 = (bf16[8,16,1024]{2,1,0:T(8,128)(2,1)S(1)}, bf16[8,16,1024]{2,1,0:T(8,128)(2,1)}, u32[]{:S(2)}) copy-start(bf16[8,16,1024]{2,1,0:T(8,128)(2,1)} %param.14) | copy-start | bytes 786436
  204.2 19.7 %all-to-all-start.2 = ((bf16[8,6,1024]{2,1,0:T(8,128)(2,1)}), bf16[8,6,1024]{2,1,0:T(8,128)(2,1)S(1)}, u32[]{:S(2)}, u32[]{:S(2)}) async-start(bf16[8,6,1024]{2,1,0:T(8,128)(2,1)} %reshape.73), calls=%async_computation.3 | async-start | bytes 262144 | tf_op jit(solution)/shard_map/all_to_all | solution.py:69
Sparse Core Ops, SparseCore 0:
  29.1 82.3 all-gather.1
  133.5 69.0 reduce-scatter.1
where the time goes:
time: 234 us
  waiting for transfers between devices  156 us (67%)
  blocking collectives  30.7 us (13%)
  starting transfers between devices  14.5 us (6%)
  between operations  13.5 us (6%)
  matrix products  10.9 us (5%)
  local copies, waits for them, and re-layouts  4.67 us (2%)
  other arithmetic  3.63 us (2%)
    all_gather x1, waiting for transfers between devices, per_device(): lax.all_gather(arrived.reshape(experts * capacity, feature_width), 'dp',...  82.5 us
    reduce_scatter x1, waiting for transfers between devices, per_device(): lax.psum_scatter(jnp.dot(hidden_wide, w_down, preferred_element_type=jnp....  68.1 us
    all_to_all x1, blocking collectives, per_device(): lax.all_to_all(packed, 'expert', split_axis=0, concat_axis=0, tiled=True)  18.6 us
    all_to_all x1, starting transfers between devices, per_device(): lax.all_to_all(expert_out.reshape(experts, capacity, quarter), 'expert',...  14.5 us
    all_to_all x1, blocking collectives, from_everyone(): lax.all_to_all(jnp.broadcast_to(shard[None], (count, *shard.shape)), axis...  12.1 us
    all_to_all x1, waiting for transfers between devices, per_device(): lax.all_to_all(expert_out.reshape(experts, capacity, quarter), 'expert',...  5.23 us
    dot_general x1, matrix products, per_device(): gate = jnp.dot(block_rows, w_gate, preferred_element_type=jnp.float32)  4.98 us
  transfers between devices with their start and end apart: 3, of which 3 were waited for; matrix products, arithmetic and copies ran while one was open for 0% of the time, Pallas kernels for 0%

commit v1 on v0

--- a/solution.py
+++ b/solution.py
@@ -49,23 +49,29 @@
     w_down = down_weight[0]
     targets = assignment_slots(expert_ids, experts, capacity)
     selected = selector(expert_ids, experts, capacity)
-    packed = jnp.dot(selected, tokens, preferred_element_type=jnp.float32).astype(jnp.bfloat16)
-    packed = packed.reshape(experts, capacity, feature_width)
+    quarter = w_down.shape[1]
+    first_column = lax.axis_index("tensor") * quarter
+    own_columns = lax.dynamic_slice_in_dim(tokens, first_column, quarter, 1)
+    packed = jnp.dot(selected, own_columns, preferred_element_type=jnp.float32).astype(jnp.bfloat16)
+    packed = packed.reshape(experts, capacity, quarter)
     arrived = lax.all_to_all(packed, "expert", split_axis=0, concat_axis=0, tiled=True)
+    parts = lax.axis_size("tensor")
     block_rows = lax.all_gather(
-        arrived.reshape(experts * capacity, feature_width), "dp", axis=0, tiled=True
-    )
-    gate = jnp.dot(block_rows, w_gate, preferred_element_type=jnp.float32)
-    up = jnp.dot(block_rows, w_up, preferred_element_type=jnp.float32)
+        arrived.reshape(experts * capacity, quarter), ("tensor", "dp"), axis=0, tiled=True
+    ).reshape(parts, -1, quarter)
+    gate = up = 0.0
+    for part in range(parts):
+        rows = slice(part * quarter, (part + 1) * quarter)
+        gate += jnp.dot(block_rows[part], w_gate[rows], preferred_element_type=jnp.float32)
+        up += jnp.dot(block_rows[part], w_up[rows], preferred_element_type=jnp.float32)
     hidden = (jax.nn.silu(gate) * up).astype(jnp.bfloat16)
     hidden_wide = gathered_copies(hidden, "tensor", 1)
     expert_out = lax.psum_scatter(
-        jnp.dot(hidden_wide, w_down, preferred_element_type=jnp.float32),
+        jnp.dot(hidden_wide, w_down, preferred_element_type=jnp.float32).astype(jnp.bfloat16),
         "dp",
         scatter_dimension=0,
         tiled=True,
-    ).astype(jnp.bfloat16)
-    quarter = expert_out.shape[1]
+    )
     returned_rows = lax.all_to_all(
         expert_out.reshape(experts, capacity, quarter),
         "expert",
@@ -77,8 +83,7 @@
     fetched = returned_rows[targets].astype(jnp.float32).reshape(tok_rows, chosen_count, quarter)
     shares = route_weight / jnp.sum(route_weight, axis=1, keepdims=True)
     expert_mix = jnp.sum(fetched * shares[:, :, None], axis=1)
-    first_column = lax.axis_index("tensor") * quarter
-    residual = lax.dynamic_slice_in_dim(tokens, first_column, quarter, 1).astype(jnp.float32)
+    residual = own_columns.astype(jnp.float32)
     current = residual + expert_mix
     depth = past_layers.shape[0]
     history = jnp.einsum("j,jtd->td", dwa_weight[:depth], past_layers.astype(jnp.float32))

time: 234 us -> 288 us (1.23)
  waiting for transfers between devices: 156 us -> 213 us
  blocking collectives: 30.7 us -> 25.2 us
    all_gather x1, waiting for transfers between devices: 82.5 us -> 142 us  [per_device(): lax.all_gather(arrived.reshape(experts * capacity, quarter), ('tensor', '...]
    all_to_all x1, blocking collectives: 18.6 us -> 14.5 us  [per_device(): lax.all_to_all(packed, 'expert', split_axis=0, concat_axis=0, tiled=True)]
    dot_general x3 -> x9, matrix products: 7.95 us -> 10.1 us  [the longest x4 6.87 us: per_device(): jnp.dot(block_rows[part], w_gate[rows], preferred_element_type=jnp.float32)]
where the time goes in v1:
time: 288 us; the launch traced here: 287 us
  waiting for transfers between devices  213 us (74%)
  blocking collectives  25.2 us (9%)
  starting transfers between devices  15.3 us (5%)
  between operations  13.6 us (5%)
  matrix products  12.5 us (4%)
  local copies, waits for them, and re-layouts  5.18 us (2%)
    all_gather x1, waiting for transfers between devices, per_device(): lax.all_gather(arrived.reshape(experts * capacity, quarter), ('tensor', '...  142 us
    reduce_scatter x1, waiting for transfers between devices, per_device(): lax.psum_scatter(jnp.dot(hidden_wide, w_down, preferred_element_type=jnp....  65.6 us
    all_to_all x1, starting transfers between devices, per_device(): lax.all_to_all(expert_out.reshape(experts, capacity, quarter), 'expert',...  15.3 us
    all_to_all x1, blocking collectives, per_device(): lax.all_to_all(packed, 'expert', split_axis=0, concat_axis=0, tiled=True)  14.5 us
    all_to_all x1, blocking collectives, from_everyone(): lax.all_to_all(jnp.broadcast_to(shard[None], (count, *shard.shape)), axis...  10.7 us
    dot_general x4, matrix products, per_device(): jnp.dot(block_rows[part], w_gate[rows], preferred_element_type=jnp.float32)  6.87 us
  transfers between devices with their start and end apart: 3, of which 3 were waited for; matrix products, arithmetic and copies ran while one was open for 0% of the time, Pallas kernels for 0%

profile of v1, /device:TPU:1, one launch (start us, length us, event | category | flops | bytes accessed | tf_op | source)
XLA Modules:
  0.0 287.3 jit_solution(16490337823808237992)
XLA Ops:
  6.5 0.9 copy.16
  7.4 0.1 eq.15
  7.7 0.2 select_reduce_fusion
  7.8 0.1 reduce_sum.45
  8.0 0.1 copy.18
  8.1 1.0 convolution_convert_fusion.1
  9.1 14.5 %all_to_all.15 = bf16[8,6,1024]{2,1,0:T(8,128)(2,1)S(1)} all-to-all(bf16[8,6,1024]{2,1,0:T(8,128)(2,1)S(1)} %reshape.87), channel_id=1, replica_groups=mesh['expert'=8,'dp'=16,'tensor'=4] {'expert'}, dimensions={0} | all-to-all | bytes 196608 | tf_op jit(solution)/shard_map/all_to_all | solution.py:57
  23.6 0.7 reshape.88
  24.3 142.0 %all-gather.2.cloned.1.call-done = bf16[3072,1024]{1,0:T(8,128)(2,1)} async-done(((bf16[48,1024]{1,0:T(8,128)(2,1)}), bf16[3072,1024]{1,0:T(8,128)(2,1)}) %all-gather.2.cloned.1.call-update) | async-done | bytes 6291472 | tf_op jit(solution)/shard_map/all_gather | solution.py:59
  166.3 2.1 fusion.10
  168.5 2.2 fusion.2
  170.6 2.0 fusion.6
  172.6 0.6 fusion
  173.2 0.6 fusion.4
  173.8 0.6 fusion.8
  174.4 0.6 fusion.22
  174.9 0.6 fusion.37
  175.5 0.1 copy.19
  175.7 10.7 %all_to_all.16 = bf16[4,768,128]{1,2,0:T(8,128)(2,1)S(1)} all-to-all(bf16[4,768,128]{1,2,0:T(8,128)(2,1)S(1)} %broadcast_in_dim.2), channel_id=1, replica_groups=mesh['expert'=8,'dp'=16,'tensor'=4] {'tensor'}, dimensions={0} | all-to-all | bytes 1572864 | tf_op jit(solution)/shard_map/all_to_all | solution.py:9
  186.5 2.2 convolution_convert_fusion
  188.7 0.1 mul.52
  188.8 0.1 copy.20
  188.9 0.6 slice.74
  189.5 0.3 fusion.49
  189.8 65.6 %reduce-scatter.2.cloned.1.call-done = bf16[48,1024]{1,0:T(8,128)(2,1)} async-done(((bf16[768,1024]{1,0:T(8,128)(2,1)}), bf16[48,1024]{1,0:T(8,128)(2,1)}) %reduce-scatter.2.cloned.1.call-update) | async-done | bytes 98320 | tf_op jit(solution)/shard_map/reduce_scatter | solution.py:69
  255.3 1.6 reshape.90
  256.9 15.3 %all-to-all-start.2 = ((bf16[8,6,1024]{2,1,0:T(8,128)(2,1)}), bf16[8,6,1024]{2,1,0:T(8,128)(2,1)S(1)}, u32[]{:S(2)}, u32[]{:S(2)}) async-start(bf16[8,6,1024]{2,1,0:T(8,128)(2,1)} %reshape.90), calls=%async_computation.3 | async-start | bytes 262144 | tf_op jit(solution)/shard_map/all_to_all | solution.py:75
  272.2 5.2 %all-to-all-done.2 = bf16[8,6,1024]{2,1,0:T(8,128)(2,1)S(1)} async-done(((bf16[8,6,1024]{2,1,0:T(8,128)(2,1)}), bf16[8,6,1024]{2,1,0:T(8,128)(2,1)S(1)}, u32[]{:S(2)}, u32[]{:S(2)}) %all-to-all-start.2) | async-done | bytes 98336 | tf_op jit(solution)/shard_map/all_to_all | solution.py:75
  277.4 0.6 gather_fusion
  278.1 0.1 reshape.92
  278.2 0.2 multiply_reduce_fusion
  278.4 2.0 fusion.59
  (29 shorter events, 0.5 us)
Async XLA Ops:
  6.5 180.0 %copy-start = (bf16[1,512,1024]{2,1,0:T(8,128)(2,1)S(1)}, bf16[1,512,1024]{2,1,0:T(8,128)(2,1)}, u32[]{:S(2)}) copy-start(bf16[1,512,1024]{2,1,0:T(8,128)(2,1)} %param.13) | copy-start | bytes 3145732
  6.5 161.9 %copy-start.3 = (bf16[1,4096,128]{2,1,0:T(8,128)(2,1)S(1)}, bf16[1,4096,128]{2,1,0:T(8,128)(2,1)}, u32[]{:S(2)}) copy-start(bf16[1,4096,128]{2,1,0:T(8,128)(2,1)} %param.11) | copy-start | bytes 3145732
  6.5 159.8 %all-gather.2.cloned.1.call-start = ((), (), s32[]{:S(2)}) async-start(), calls=%async_computation.4 | async-start | bytes 6389760 | tf_op jit(solution)/shard_map/all_gather | solution.py:59
  24.3 231.1 %reduce-scatter.2.cloned.1.call-start = ((), (), s32[]{:S(2)}) async-start(), calls=%async_computation.5 | async-start | bytes 1671168 | tf_op jit(solution)/shard_map/reduce_scatter | solution.py:69
  166.3 6.3 %copy-start.1 = (bf16[3072,1024]{1,0:T(8,128)(2,1)S(1)}, bf16[3072,1024]{1,0:T(8,128)(2,1)}, u32[]{:S(2)}) copy-start(bf16[3072,1024]{1,0:T(8,128)(2,1)} %all-gather.2.cloned.1.call-done) | copy-start | bytes 18874372
  168.4 4.2 %copy-start.6 = (bf16[1,4096,128]{2,1,0:T(8,128)(2,1)S(1)}, bf16[1,4096,128]{2,1,0:T(8,128)(2,1)}, u32[]{:S(2)}) copy-start(bf16[1,4096,128]{2,1,0:T(8,128)(2,1)} %param.12) | copy-start | bytes 3145732
  186.5 2.3 copy-start.4
  186.5 2.4 copy-start.5
  186.5 3.0 %copy-start.2 = (bf16[8,16,1024]{2,1,0:T(8,128)(2,1)S(1)}, bf16[8,16,1024]{2,1,0:T(8,128)(2,1)}, u32[]{:S(2)}) copy-start(bf16[8,16,1024]{2,1,0:T(8,128)(2,1)} %param.14) | copy-start | bytes 786436
  256.9 20.5 %all-to-all-start.2 = ((bf16[8,6,1024]{2,1,0:T(8,128)(2,1)}), bf16[8,6,1024]{2,1,0:T(8,128)(2,1)S(1)}, u32[]{:S(2)}, u32[]{:S(2)}) async-start(bf16[8,6,1024]{2,1,0:T(8,128)(2,1)} %reshape.90), calls=%async_computation.3 | async-start | bytes 262144 | tf_op jit(solution)/shard_map/all_to_all | solution.py:75
Sparse Core Ops, SparseCore 0:
  24.4 141.8 all-gather.1
  188.8 66.4 reduce-scatter.1

commit v2 on v1

v2 whole, which is shorter than its diff:
```python
import jax
import jax.numpy as jnp
from jax import lax
from jax.experimental import pallas as pl
from jax.experimental.pallas import tpu as pltpu
from jax.sharding import PartitionSpec as P

RADIX = 4


VMEM = pl.BlockSpec(memory_space=pltpu.VMEM)


def far_groups(count):
    stride = count // RADIX
    return [[low + stride * high for high in range(RADIX)] for low in range(stride)]


def shifted(shard, even_shift, odd_shift):
    experts, count = lax.axis_size("expert"), lax.axis_size("dp")
    pairs = []
    for expert in range(experts):
        shift = odd_shift if expert % 2 else even_shift
        for place in range(count):
            pairs.append((expert * count + place, expert * count + (place + shift) % count))
    return lax.ppermute(shard, ("expert", "dp"), pairs)


def from_neighbours(shard):
    return [shifted(shard, 1, 1), shifted(shard, -1, -1), shifted(shard, 2, -2)]


def to_neighbours(shards):
    below, above, second = shards
    return [shifted(below, -1, -1), shifted(above, 1, 1), shifted(second, -2, 2)]


def assignment_slots(expert_ids, experts, capacity):
    flat_ids = expert_ids.reshape(-1)
    matches = (flat_ids[:, None] == jnp.arange(experts, dtype=jnp.int32)[None, :]).astype(jnp.int32)
    earlier = jnp.cumsum(matches, axis=0) - matches
    slot_ids = jnp.sum(earlier * matches, axis=1)
    return flat_ids * capacity + slot_ids


def selector(targets, shape, rows):
    matched = targets[None, :] == jnp.arange(rows, dtype=jnp.int32)[:, None]
    chosen = matched.reshape(rows, *shape)
    return jnp.sum(chosen.astype(jnp.float32), axis=2).astype(jnp.bfloat16)


def gate_up_parts(sets, weights):
    parts, _, width = weights.shape
    set_rows = sets[0].shape[0]
    rows = set_rows * len(sets)

    def kernel(*refs):
        set_refs, (w_ref, out_ref) = refs[: len(sets)], refs[len(sets) :]
        stacked = jnp.concatenate([ref[...] for ref in set_refs], axis=0)
        for part in range(parts):
            out_ref[part] = jnp.dot(stacked, w_ref[part], preferred_element_type=jnp.float32).astype(out_ref.dtype)

    return pl.pallas_call(
        kernel,
        out_shape=jax.ShapeDtypeStruct((parts, rows, width), jnp.bfloat16),
        in_specs=[VMEM] * (len(sets) + 1),
        out_specs=VMEM,
        name="gate_up_parts",
    )(*sets, weights)


def hidden_copies(parts):
    count, rows, both = parts.shape
    width = both // 2

    def kernel(in_ref, out_ref):
        total = in_ref[0].astype(jnp.float32)
        for part in range(1, count):
            total += in_ref[part].astype(jnp.float32)
        gate, up = total[:, :width], total[:, width:]
        hidden = (gate / (1.0 + jnp.exp(-gate)) * up).astype(out_ref.dtype)
        for part in range(count):
            out_ref[part] = hidden

    return pl.pallas_call(
        kernel,
        out_shape=jax.ShapeDtypeStruct((count, rows, width), jnp.bfloat16),
        in_specs=[VMEM],
        out_specs=VMEM,
        name="hidden_copies",
    )(parts)


def down_sets(hidden, w_down, count):
    parts, rows, _ = hidden.shape
    set_rows = rows // count
    features = w_down.shape[1]

    def kernel(hidden_ref, w_ref, *out_refs):
        wide = jnp.concatenate([hidden_ref[part] for part in range(parts)], axis=1)
        out = jnp.dot(wide, w_ref[...], preferred_element_type=jnp.float32)
        for place, ref in enumerate(out_refs):
            ref[...] = out[place * set_rows : (place + 1) * set_rows].astype(ref.dtype)

    return pl.pallas_call(
        kernel,
        out_shape=[
            jax.ShapeDtypeStruct((set_rows, features), jnp.bfloat16 if place else jnp.float32)
            for place in range(count)
        ],
        in_specs=[VMEM, VMEM],
        out_specs=[VMEM] * count,
        name="down_sets",
    )(hidden, w_down)


def per_device(
    tokens, expert_ids, route_weight, gate_weight, up_weight, down_weight, past_layers, dwa_weight
):
    experts = lax.axis_size("expert")
    parts = lax.axis_size("tensor")
    tok_rows, feature_width = tokens.shape
    chosen_count = expert_ids.shape[1]
    capacity = min(tok_rows, 3 * chosen_count * tok_rows // (2 * experts))
    quarter = feature_width // parts
    groups = far_groups(lax.axis_size("dp"))
    block = experts * capacity

    slabs = [w.reshape(parts, quarter, -1) for w in (gate_weight, up_weight)]
    w_both = lax.all_to_all(jnp.concatenate(slabs, axis=2), "tensor", 0, 0, tiled=True)

    targets = assignment_slots(expert_ids, experts, capacity)
    selected = selector(targets, expert_ids.shape, block)
    first_column = lax.axis_index("tensor") * quarter
    own_columns = lax.dynamic_slice_in_dim(tokens, first_column, quarter, 1)
    packed = jnp.dot(selected, own_columns, preferred_element_type=jnp.float32).astype(jnp.bfloat16)
    arrived = lax.all_to_all(packed.reshape(experts, capacity, quarter), "expert", 0, 0, tiled=True)
    far = lax.all_to_all(
        jnp.broadcast_to(arrived.reshape(1, block, quarter), (RADIX, block, quarter)),
        "dp",
        0,
        0,
        tiled=True,
        axis_index_groups=groups,
    ).reshape(RADIX * block, quarter)
    sets = [far, *from_neighbours(far)]

    partial = gate_up_parts(sets, w_both)
    partial = lax.all_to_all(partial, "tensor", 0, 0, tiled=True)
    hidden = lax.all_to_all(hidden_copies(partial), "tensor", 0, 0, tiled=True)
    own, *others = down_sets(hidden, down_weight[0], len(sets))
    for other in to_neighbours(others):
        own = own + other.astype(jnp.float32)
    own = own.astype(jnp.bfloat16).reshape(RADIX, block, quarter)
    own = lax.all_to_all(own, "dp", 0, 0, tiled=True, axis_index_groups=groups)
    expert_out = jnp.sum(own.astype(jnp.float32), axis=0).astype(jnp.bfloat16)
    returned_rows = lax.all_to_all(
        expert_out.reshape(experts, capacity, quarter), "expert", 0, 0, tiled=True
    ).reshape(block, quarter)

    fetched = returned_rows[targets].astype(jnp.float32).reshape(tok_rows, chosen_count, quarter)
    shares = route_weight / jnp.sum(route_weight, axis=1, keepdims=True)
    expert_mix = jnp.sum(fetched * shares[:, :, None], axis=1)
    current = own_columns.astype(jnp.float32) + expert_mix
    depth = past_layers.shape[0]
    history = jnp.einsum("j,jtd->td", dwa_weight[:depth], past_layers.astype(jnp.float32))
    return (dwa_weight[depth] * current + history).astype(jnp.bfloat16)


def solution(mesh):
    return jax.shard_map(
        per_device,
        mesh=mesh,
        in_specs=(
            P(("expert", "dp"), None),
            P(("expert", "dp"), None),
            P(("expert", "dp"), None),
            P("expert", None, ("dp", "tensor")),
            P("expert", None, ("dp", "tensor")),
            P("expert", "dp", "tensor"),
            P(None, ("expert", "dp"), "tensor"),
            P(),
        ),
        out_specs=P(("expert", "dp"), "tensor"),
        check_vma=False,
    )
```

time: 288 us -> 204 us (0.71)
  waiting for transfers between devices: 213 us -> 76.3 us
  starting transfers between devices: 15.3 us -> 49.3 us
  blocking collectives: 25.2 us -> 54.1 us
  between operations: 13.6 us -> 0.17 us
  matrix products: 12.5 us -> 1.22 us
  Pallas kernels: 0 us -> 11.2 us
  other arithmetic: 2.68 us -> 6.5 us
    all_gather x1 -> x0, waiting for transfers between devices: 142 us -> none  [per_device(): lax.all_gather(arrived.reshape(experts * capacity, quarter), ('tensor', '...]
    reduce_scatter x1 -> x0, waiting for transfers between devices: 65.6 us -> none  [per_device(): lax.psum_scatter(jnp.dot(hidden_wide, w_down, preferred_element_type=jnp....]
    all_to_all x0 -> x3, waiting for transfers between devices: none -> 52.2 us  [the longest x1 20.8 us: per_device(): own = lax.all_to_all(own, 'dp', 0, 0, tiled=True, axis_index_groups=groups)]
    all_to_all x2 -> x3, blocking collectives: 25.2 us -> 54.1 us  [the longest x1 24.7 us: per_device(): partial = lax.all_to_all(partial, 'tensor', 0, 0, tiled=True)]
    ppermute x0 -> x6, starting transfers between devices: none -> 21.6 us  [shifted(): return lax.ppermute(shard, ('expert', 'dp'), pairs)]
    all_to_all x0 -> x3, starting transfers between devices: none -> 20.7 us  [the longest x1 11.3 us: per_device(): lax.all_to_all(jnp.broadcast_to(arrived.reshape(1, block, quarter), (RADI...]
    ppermute x0 -> x6, waiting for transfers between devices: none -> 18.9 us  [shifted(): return lax.ppermute(shard, ('expert', 'dp'), pairs)]
    dot_general x9 -> x0, matrix products: 11.3 us -> none  [the longest x4 6.87 us: per_device(): jnp.dot(block_rows[part], w_gate[rows], preferred_element_type=jnp.float32)]
  transfers between devices with their start and end apart: 3 -> 10, of which waited for: 3 -> 8; matrix products, arithmetic and copies ran while one was open for 0% -> 1% of each run, Pallas kernels for 0% -> 0%
where the time goes in v2:
time: 204 us; the launch traced here: 203 us
  waiting for transfers between devices  76.3 us (37%)
  blocking collectives  54.1 us (27%)
  starting transfers between devices  49.3 us (24%)
  Pallas kernels  11.2 us (5%)
  other arithmetic  6.5 us (3%)
  local copies, waits for them, and re-layouts  4.34 us (2%)
    all_to_all x1, blocking collectives, per_device(): partial = lax.all_to_all(partial, 'tensor', 0, 0, tiled=True)  24.7 us
    ppermute x6, starting transfers between devices, shifted(): return lax.ppermute(shard, ('expert', 'dp'), pairs)  21.6 us
    all_to_all x1, waiting for transfers between devices, per_device(): own = lax.all_to_all(own, 'dp', 0, 0, tiled=True, axis_index_groups=groups)  20.8 us
    all_to_all x1, waiting for transfers between devices, per_device(): lax.all_to_all(jnp.broadcast_to(arrived.reshape(1, block, quarter), (RADI...  19.3 us
    ppermute x6, waiting for transfers between devices, shifted(): return lax.ppermute(shard, ('expert', 'dp'), pairs)  18.9 us
    all_to_all x1, blocking collectives, per_device(): hidden = lax.all_to_all(hidden_copies(partial), 'tensor', 0, 0, tiled=True)  14.9 us
    all_to_all x1, blocking collectives, per_device(): lax.all_to_all(packed.reshape(experts, capacity, quarter), 'expert', 0, 0...  14.5 us
    all_to_all x1, waiting for transfers between devices, per_device(): lax.all_to_all(jnp.concatenate(slabs, axis=2), 'tensor', 0, 0, tiled=True)  12.1 us
  transfers between devices with their start and end apart: 10, of which 8 were waited for; matrix products, arithmetic and copies ran while one was open for 1% of the time, Pallas kernels for 0%

profile of v2, /device:TPU:1, one launch (start us, length us, event | category | flops | bytes accessed | tf_op | source)
XLA Modules:
  0.0 203.1 jit_solution(3220911801186155157)
XLA Ops:
  0.0 0.9 copy.15
  1.6 1.0 convolution_convert_fusion
  2.6 14.5 %all_to_all.35 = bf16[8,6,1024]{2,1,0:T(8,128)(2,1)S(1)} all-to-all(bf16[8,6,1024]{2,1,0:T(8,128)(2,1)S(1)} %reshape.76), channel_id=1, replica_groups=mesh['expert'=8,'dp'=16,'tensor'=4] {'expert'}, dimensions={0} | all-to-all | bytes 196608 | tf_op jit(solution)/shard_map/all_to_all | solution.py:137
  17.1 0.8 broadcast_in_dim.5
  17.9 11.3 %all-to-all-start.1 = ((bf16[4,48,1024]{2,1,0:T(8,128)(2,1)}), bf16[4,48,1024]{2,1,0:T(8,128)(2,1)S(1)}, u32[]{:S(2)}, u32[]{:S(2)}) async-start(bf16[4,48,1024]{2,1,0:T(8,128)(2,1)} %broadcast_in_dim.5), calls=%async_computation.1 | async-start | bytes 786432 | tf_op jit(solution)/shard_map/all_to_all | solution.py:138
  29.2 1.6 pad_maximum_fusion
  30.8 19.3 %all-to-all-done.1 = bf16[4,48,1024]{2,1,0:T(8,128)(2,1)S(1)} async-done(((bf16[4,48,1024]{2,1,0:T(8,128)(2,1)}), bf16[4,48,1024]{2,1,0:T(8,128)(2,1)S(1)}, u32[]{:S(2)}, u32[]{:S(2)}) %all-to-all-start.1) | async-done | bytes 393248 | tf_op jit(solution)/shard_map/all_to_all | solution.py:138
  50.2 4.0 %all-to-all-start.2 = ((bf16[4,1024,256]{2,1,0:T(8,128)(2,1)}), bf16[4,1024,256]{2,1,0:T(8,128)(2,1)S(1)}, u32[]{:S(2)}, u32[]{:S(2)}) async-start(bf16[4,1024,256]{2,1,0:T(8,128)(2,1)} %pad_maximum_fusion), calls=%async_computation.2 | async-start | bytes 4194304 | tf_op jit(solution)/shard_map/all_to_all | solution.py:130
  54.2 6.6 %collective-permute-start = (bf16[192,1024]{1,0:T(8,128)(2,1)S(1)}, bf16[192,1024]{1,0:T(8,128)(2,1)S(1)}, u32[]{:S(2)}, u32[]{:S(2)}) collective-permute-start(bf16[192,1024]{1,0:T(8,128)(2,1)S(1)} %bitcast.20), channel_id=1, source_target_pairs={{0,4},{4,8},{8,12},{12,16},{16,20},{20,24},{24,28},{28,32},{32,36}... | collective-permute-start | bytes 1179656 | tf_op jit(solution)/shard_map/ppermute | solution.py:26
  60.8 1.9 collective-permute-start.1
  62.8 4.5 %collective-permute-start.2 = (bf16[192,1024]{1,0:T(8,128)(2,1)S(1)}, bf16[192,1024]{1,0:T(8,128)(2,1)}, u32[]{:S(2)}, u32[]{:S(2)}) collective-permute-start(bf16[192,1024]{1,0:T(8,128)(2,1)S(1)} %bitcast.22), channel_id=1, source_target_pairs={{0,8},{4,12},{8,16},{12,20},{16,24},{20,28},{24,32},{28,36},{32,40... | collective-permute-start | bytes 1179656 | tf_op jit(solution)/shard_map/ppermute | solution.py:26
  67.3 12.1 %all-to-all-done.2.refs_4_ = bf16[4,1024,256]{2,1,0:T(8,128)(2,1)S(1)} async-done(((bf16[4,1024,256]{2,1,0:T(8,128)(2,1)}), bf16[4,1024,256]{2,1,0:T(8,128)(2,1)S(1)}, u32[]{:S(2)}, u32[]{:S(2)}) %all-to-all-start.2) | async-done | bytes 2097184 | tf_op jit(solution)/shard_map/all_to_all | solution.py:130
  79.4 3.1 %collective-permute-done.2.refs_3_ = bf16[192,1024]{1,0:T(8,128)(2,1)} collective-permute-done((bf16[192,1024]{1,0:T(8,128)(2,1)S(1)}, bf16[192,1024]{1,0:T(8,128)(2,1)}, u32[]{:S(2)}, u32[]{:S(2)}) %collective-permute-start.2) | collective-permute-done | bytes 393248 | tf_op jit(solution)/shard_map/ppermute | solution.py:26
  82.5 5.0 %gate_up_parts.1 = bf16[4,768,256]{2,1,0:T(8,128)(2,1)} custom-call(bf16[192,1024]{1,0:T(8,128)(2,1)} %bitcast.23, bf16[192,1024]{1,0:T(8,128)(2,1)} %copy-done.5, bf16[192,1024]{1,0:T(8,128)(2,1)} %copy-done.6, bf16[192,1024]{1,0:T(8,128)(2,1)} %collective-permute-done.2.refs_3_, bf16[4,1024,256]{2,1,0:T(8,128)(2,1)} %copy-done.1), custom_call_target="tpu_custom_call" | custom-call | tf_op jit(solution)/shard_map/gate_up_parts/pallas_call | solution.py:63
  87.5 24.7 %all_to_all.36.in_ref = bf16[4,768,256]{2,1,0:T(8,128)(2,1)} all-to-all(bf16[4,768,256]{2,1,0:T(8,128)(2,1)} %gate_up_parts.1), channel_id=1, replica_groups=mesh['expert'=8,'dp'=16,'tensor'=4] {'tensor'}, dimensions={0} | all-to-all | bytes 3145728 | tf_op jit(solution)/shard_map/all_to_all | solution.py:149
  112.2 2.6 %hidden_copies.1 = bf16[4,768,128]{2,1,0:T(8,128)(2,1)} custom-call(bf16[4,768,256]{2,1,0:T(8,128)(2,1)} %all_to_all.36.in_ref), custom_call_target="tpu_custom_call" | custom-call | tf_op jit(solution)/shard_map/hidden_copies/pallas_call | solution.py:85
  114.8 14.9 %all_to_all.37.hidden_ref = bf16[4,768,128]{2,1,0:T(8,128)(2,1)} all-to-all(bf16[4,768,128]{2,1,0:T(8,128)(2,1)} %hidden_copies.1), channel_id=1, replica_groups=mesh['expert'=8,'dp'=16,'tensor'=4] {'tensor'}, dimensions={0} | all-to-all | bytes 1572864 | tf_op jit(solution)/shard_map/all_to_all | solution.py:150
  129.8 3.6 %down_sets.1 = (f32[192,1024]{1,0:T(8,128)}, bf16[192,1024]{1,0:T(8,128)(2,1)}, bf16[192,1024]{1,0:T(8,128)(2,1)}, bf16[192,1024]{1,0:T(8,128)(2,1)}) custom-call(bf16[4,768,128]{2,1,0:T(8,128)(2,1)} %all_to_all.37.hidden_ref, bf16[512,1024]{1,0:T(8,128)(2,1)} %bitcast.24), custom_call_target="tpu_custom_call" | custom-call | tf_op jit(solution)/shard_map/down_sets/pallas_call | solution.py:105
  133.4 1.9 collective-permute-start.3
  135.3 3.4 %collective-permute-start.4 = (bf16[192,1024]{1,0:T(8,128)(2,1)}, bf16[192,1024]{1,0:T(8,128)(2,1)S(1)}, u32[]{:S(2)}, u32[]{:S(2)}) collective-permute-start(bf16[192,1024]{1,0:T(8,128)(2,1)} %get-tuple-element.11), channel_id=1, source_target_pairs={{0,4},{4,8},{8,12},{12,16},{16,20},{20,24},{24,28},{28,32},{32,36}... | collective-permute-start | bytes 1179656 | tf_op jit(solution)/shard_map/ppermute | solution.py:26
  138.7 3.2 %collective-permute-start.5 = (bf16[192,1024]{1,0:T(8,128)(2,1)}, bf16[192,1024]{1,0:T(8,128)(2,1)S(1)}, u32[]{:S(2)}, u32[]{:S(2)}) collective-permute-start(bf16[192,1024]{1,0:T(8,128)(2,1)} %get-tuple-element.12), channel_id=1, source_target_pairs={{0,56},{4,60},{8,0},{12,4},{16,8},{20,12},{24,16},{28,20},{32,24},... | collective-permute-start | bytes 1179656 | tf_op jit(solution)/shard_map/ppermute | solution.py:26
  141.9 1.7 collective-permute-done.3
  143.6 3.4 %collective-permute-done.4 = bf16[192,1024]{1,0:T(8,128)(2,1)S(1)} collective-permute-done((bf16[192,1024]{1,0:T(8,128)(2,1)}, bf16[192,1024]{1,0:T(8,128)(2,1)S(1)}, u32[]{:S(2)}, u32[]{:S(2)}) %collective-permute-start.4) | collective-permute-done | bytes 393248 | tf_op jit(solution)/shard_map/ppermute | solution.py:26
  147.0 10.6 %collective-permute-done.5 = bf16[192,1024]{1,0:T(8,128)(2,1)S(1)} collective-permute-done((bf16[192,1024]{1,0:T(8,128)(2,1)}, bf16[192,1024]{1,0:T(8,128)(2,1)S(1)}, u32[]{:S(2)}, u32[]{:S(2)}) %collective-permute-start.5) | collective-permute-done | bytes 393248 | tf_op jit(solution)/shard_map/ppermute | solution.py:26
  157.6 2.1 %add_convert_fusion = bf16[192,1024]{1,0:T(8,128)(2,1)} fusion(bf16[192,1024]{1,0:T(8,128)(2,1)S(1)} %collective-permute-done.5, bf16[192,1024]{1,0:T(8,128)(2,1)S(1)} %collective-permute-done.4, f32[192,1024]{1,0:T(8,128)} %get-tuple-element.9, bf16[192,1024]{1,0:T(8,128)(2,1)S(1)} %collective-permute-done.3), kind=kLoop, calls=%fused_computation.3 | loop fusion | flops 1376256 | bytes 2359296 | tf_op jit(solution)/shard_map/convert_element_type | solution.py:154
  159.7 5.3 %all-to-all-start.5 = ((bf16[4,48,1024]{2,1,0:T(8,128)(2,1)}), bf16[4,48,1024]{2,1,0:T(8,128)(2,1)S(1)}, u32[]{:S(2)}, u32[]{:S(2)}) async-start(bf16[4,48,1024]{2,1,0:T(8,128)(2,1)} %bitcast.5), calls=%async_computation.5 | async-start | bytes 786432 | tf_op jit(solution)/shard_map/all_to_all | solution.py:155
  165.2 0.7 slice.6
  166.2 20.8 %all-to-all-done.5 = bf16[4,48,1024]{2,1,0:T(8,128)(2,1)S(1)} async-done(((bf16[4,48,1024]{2,1,0:T(8,128)(2,1)}), bf16[4,48,1024]{2,1,0:T(8,128)(2,1)S(1)}, u32[]{:S(2)}, u32[]{:S(2)}) %all-to-all-start.5) | async-done | bytes 393248 | tf_op jit(solution)/shard_map/all_to_all | solution.py:155
  187.0 0.7 reshape.81
  187.7 7.0 %all-to-all-start.6 = ((bf16[8,6,1024]{2,1,0:T(8,128)(2,1)}), bf16[8,6,1024]{2,1,0:T(8,128)(2,1)S(1)}, u32[]{:S(2)}, u32[]{:S(2)}) async-start(bf16[8,6,1024]{2,1,0:T(8,128)(2,1)} %reshape.81), calls=%async_computation.6 | async-start | bytes 262144 | tf_op jit(solution)/shard_map/all_to_all | solution.py:157
  194.7 5.3 %all-to-all-done.6 = bf16[8,6,1024]{2,1,0:T(8,128)(2,1)S(1)} async-done(((bf16[8,6,1024]{2,1,0:T(8,128)(2,1)}), bf16[8,6,1024]{2,1,0:T(8,128)(2,1)S(1)}, u32[]{:S(2)}, u32[]{:S(2)}) %all-to-all-start.6) | async-done | bytes 98336 | tf_op jit(solution)/shard_map/all_to_all | solution.py:157
  201.0 2.1 %fusion.2 = bf16[16,1024]{1,0:T(8,128)(2,1)} fusion(f32[1,16,1024]{2,0,1:T(1,128)S(1)} %fusion, f32[16,1024]{1,0:T(8,128)S(1)} %multiply_reduce_fusion, f32[]{:T(128)} %bitcast, bf16[16,4096]{1,0:T(8,128)(2,1)} %param.8, s32[]{:T(128)S(6)} %select_n.13), kind=kLoop, calls=%fused_computation.8 | loop fusion | flops 81920 | bytes 196616 | tf_op jit(solution)/shard_map/convert_element_type | solution.py:167
  (42 shorter events, 2.3 us)
Async XLA Ops:
  0.0 165.9 %copy-start = (bf16[8,16,1024]{2,1,0:T(8,128)(2,1)S(1)}, bf16[8,16,1024]{2,1,0:T(8,128)(2,1)}, u32[]{:S(2)}) copy-start(bf16[8,16,1024]{2,1,0:T(8,128)(2,1)} %param.14) | copy-start | bytes 786436
  0.0 29.2 %copy-start.4 = (bf16[1,4096,128]{2,1,0:T(8,128)(2,1)S(1)}, bf16[1,4096,128]{2,1,0:T(8,128)(2,1)}, u32[]{:S(2)}) copy-start(bf16[1,4096,128]{2,1,0:T(8,128)(2,1)} %param.11) | copy-start | bytes 3145732
  0.0 29.2 %copy-start.3 = (bf16[1,4096,128]{2,1,0:T(8,128)(2,1)S(1)}, bf16[1,4096,128]{2,1,0:T(8,128)(2,1)}, u32[]{:S(2)}) copy-start(bf16[1,4096,128]{2,1,0:T(8,128)(2,1)} %param.12) | copy-start | bytes 3145732
  17.9 32.3 %all-to-all-start.1 = ((bf16[4,48,1024]{2,1,0:T(8,128)(2,1)}), bf16[4,48,1024]{2,1,0:T(8,128)(2,1)S(1)}, u32[]{:S(2)}, u32[]{:S(2)}) async-start(bf16[4,48,1024]{2,1,0:T(8,128)(2,1)} %broadcast_in_dim.5), calls=%async_computation.1 | async-start | bytes 786432 | tf_op jit(solution)/shard_map/all_to_all | solution.py:138
  50.1 12.6 %copy-start.2 = (bf16[4,48,1024]{2,1,0:T(8,128)(2,1)}, bf16[4,48,1024]{2,1,0:T(8,128)(2,1)S(1)}, u32[]{:S(2)}) copy-start(bf16[4,48,1024]{2,1,0:T(8,128)(2,1)S(1)} %all-to-all-done.1) | copy-start | bytes 1179652
  50.2 29.2 %all-to-all-start.2 = ((bf16[4,1024,256]{2,1,0:T(8,128)(2,1)}), bf16[4,1024,256]{2,1,0:T(8,128)(2,1)S(1)}, u32[]{:S(2)}, u32[]{:S(2)}) async-start(bf16[4,1024,256]{2,1,0:T(8,128)(2,1)} %pad_maximum_fusion), calls=%async_computation.2 | async-start | bytes 4194304 | tf_op jit(solution)/shard_map/all_to_all | solution.py:130
  54.2 25.2 %collective-permute-start = (bf16[192,1024]{1,0:T(8,128)(2,1)S(1)}, bf16[192,1024]{1,0:T(8,128)(2,1)S(1)}, u32[]{:S(2)}, u32[]{:S(2)}) collective-permute-start(bf16[192,1024]{1,0:T(8,128)(2,1)S(1)} %bitcast.20), channel_id=1, source_target_pairs={{0,4},{4,8},{8,12},{12,16},{16,20},{20,24},{24,28},{28,32},{32,36}... | collective-permute-start | bytes 1179656 | tf_op jit(solution)/shard_map/ppermute | solution.py:26
  60.8 18.6 %collective-permute-start.1 = (bf16[192,1024]{1,0:T(8,128)(2,1)S(1)}, bf16[192,1024]{1,0:T(8,128)(2,1)S(1)}, u32[]{:S(2)}, u32[]{:S(2)}) collective-permute-start(bf16[192,1024]{1,0:T(8,128)(2,1)S(1)} %bitcast.21), channel_id=1, source_target_pairs={{0,60},{4,0},{8,4},{12,8},{16,12},{20,16},{24,20},{28,24},{32,28},... | collective-permute-start | bytes 1179656 | tf_op jit(solution)/shard_map/ppermute | solution.py:26
  62.8 19.8 %collective-permute-start.2 = (bf16[192,1024]{1,0:T(8,128)(2,1)S(1)}, bf16[192,1024]{1,0:T(8,128)(2,1)}, u32[]{:S(2)}, u32[]{:S(2)}) collective-permute-start(bf16[192,1024]{1,0:T(8,128)(2,1)S(1)} %bitcast.22), channel_id=1, source_target_pairs={{0,8},{4,12},{8,16},{12,20},{16,24},{20,28},{24,32},{28,36},{32,40... | collective-permute-start | bytes 1179656 | tf_op jit(solution)/shard_map/ppermute | solution.py:26
  79.4 3.1 %copy-start.1 = (bf16[4,1024,256]{2,1,0:T(8,128)(2,1)}, bf16[4,1024,256]{2,1,0:T(8,128)(2,1)S(1)}, u32[]{:S(2)}) copy-start(bf16[4,1024,256]{2,1,0:T(8,128)(2,1)S(1)} %all-to-all-done.2.refs_4_) | copy-start | bytes 6291460
  79.4 3.1 %copy-start.5 = (bf16[192,1024]{1,0:T(8,128)(2,1)}, bf16[192,1024]{1,0:T(8,128)(2,1)S(1)}, u32[]{:S(2)}) copy-start(bf16[192,1024]{1,0:T(8,128)(2,1)S(1)} %collective-permute-done.refs_1_) | copy-start | bytes 1179652
  79.4 3.1 %copy-start.6 = (bf16[192,1024]{1,0:T(8,128)(2,1)}, bf16[192,1024]{1,0:T(8,128)(2,1)S(1)}, u32[]{:S(2)}) copy-start(bf16[192,1024]{1,0:T(8,128)(2,1)S(1)} %collective-permute-done.1.refs_2_) | copy-start | bytes 1179652
  129.8 35.4 %copy-start.7 = (f32[16,2]{0,1:T(2,128)S(1)}, f32[16,2]{0,1:T(2,128)}, u32[]{:S(2)}) copy-start(f32[16,2]{0,1:T(2,128)} %param.10) | copy-start | bytes 388
  129.8 35.5 %copy-start.8 = (f32[9]{0:T(128)S(1)}, f32[9]{0:T(128)}, u32[]{:S(2)}) copy-start(f32[9]{0:T(128)} %param.15) | copy-start | bytes 112
  133.4 10.2 %collective-permute-start.3 = (bf16[192,1024]{1,0:T(8,128)(2,1)}, bf16[192,1024]{1,0:T(8,128)(2,1)S(1)}, u32[]{:S(2)}, u32[]{:S(2)}) collective-permute-start(bf16[192,1024]{1,0:T(8,128)(2,1)} %get-tuple-element.10), channel_id=1, source_target_pairs={{0,60},{4,0},{8,4},{12,8},{16,12},{20,16},{24,20},{28,24},{32,28},... | collective-permute-start | bytes 1179656 | tf_op jit(solution)/shard_map/ppermute | solution.py:26
  135.3 11.7 %collective-permute-start.4 = (bf16[192,1024]{1,0:T(8,128)(2,1)}, bf16[192,1024]{1,0:T(8,128)(2,1)S(1)}, u32[]{:S(2)}, u32[]{:S(2)}) collective-permute-start(bf16[192,1024]{1,0:T(8,128)(2,1)} %get-tuple-element.11), channel_id=1, source_target_pairs={{0,4},{4,8},{8,12},{12,16},{16,20},{20,24},{24,28},{28,32},{32,36}... | collective-permute-start | bytes 1179656 | tf_op jit(solution)/shard_map/ppermute | solution.py:26
  138.7 18.9 %collective-permute-start.5 = (bf16[192,1024]{1,0:T(8,128)(2,1)}, bf16[192,1024]{1,0:T(8,128)(2,1)S(1)}, u32[]{:S(2)}, u32[]{:S(2)}) collective-permute-start(bf16[192,1024]{1,0:T(8,128)(2,1)} %get-tuple-element.12), channel_id=1, source_target_pairs={{0,56},{4,60},{8,0},{12,4},{16,8},{20,12},{24,16},{28,20},{32,24},... | collective-permute-start | bytes 1179656 | tf_op jit(solution)/shard_map/ppermute | solution.py:26
  159.7 27.2 %all-to-all-start.5 = ((bf16[4,48,1024]{2,1,0:T(8,128)(2,1)}), bf16[4,48,1024]{2,1,0:T(8,128)(2,1)S(1)}, u32[]{:S(2)}, u32[]{:S(2)}) async-start(bf16[4,48,1024]{2,1,0:T(8,128)(2,1)} %bitcast.5), calls=%async_computation.5 | async-start | bytes 786432 | tf_op jit(solution)/shard_map/all_to_all | solution.py:155
  187.7 12.3 %all-to-all-start.6 = ((bf16[8,6,1024]{2,1,0:T(8,128)(2,1)}), bf16[8,6,1024]{2,1,0:T(8,128)(2,1)S(1)}, u32[]{:S(2)}, u32[]{:S(2)}) async-start(bf16[8,6,1024]{2,1,0:T(8,128)(2,1)} %reshape.81), calls=%async_computation.6 | async-start | bytes 262144 | tf_op jit(solution)/shard_map/all_to_all | solution.py:157

commit v3 on v2

--- a/solution.py
+++ b/solution.py
@@ -8,6 +8,7 @@
 RADIX = 4
 
 
+LIMIT = pltpu.CompilerParams(vmem_limit_bytes=16 * 2**20)
 VMEM = pl.BlockSpec(memory_space=pltpu.VMEM)
 
 
@@ -65,6 +66,7 @@
         out_shape=jax.ShapeDtypeStruct((parts, rows, width), jnp.bfloat16),
         in_specs=[VMEM] * (len(sets) + 1),
         out_specs=VMEM,
+        compiler_params=LIMIT,
         name="gate_up_parts",
     )(*sets, weights)
 
@@ -87,6 +89,7 @@
         out_shape=jax.ShapeDtypeStruct((count, rows, width), jnp.bfloat16),
         in_specs=[VMEM],
         out_specs=VMEM,
+        compiler_params=LIMIT,
         name="hidden_copies",
     )(parts)
 
@@ -110,6 +113,7 @@
         ],
         in_specs=[VMEM, VMEM],
         out_specs=[VMEM] * count,
+        compiler_params=LIMIT,
         name="down_sets",
     )(hidden, w_down)
 

time: 204 us -> 191 us (0.936)
  waiting for transfers between devices: 76.3 us -> 65.4 us
  Pallas kernels: 11.2 us -> 4.03 us
  starting transfers between devices: 49.3 us -> 53.5 us
    all_to_all x1, waiting for transfers between devices: 20.8 us -> 12.7 us  [per_device(): own = lax.all_to_all(own, 'dp', 0, 0, tiled=True, axis_index_groups=groups)]
    all_to_all x1, starting transfers between devices: 7.03 us -> 11.8 us  [per_device(): lax.all_to_all(expert_out.reshape(experts, capacity, quarter), 'expert',...]
    ppermute x6, waiting for transfers between devices: 18.9 us -> 16 us  [shifted(): return lax.ppermute(shard, ('expert', 'dp'), pairs)]
    pallas_call x1, Pallas kernels: 3.62 us -> 0.97 us  [down_sets(): pl.pallas_call(kernel, out_shape=[jax.ShapeDtypeStruct((set_rows, feature...]
    pallas_call x1, Pallas kernels: 2.58 us -> 0.28 us  [hidden_copies(): pl.pallas_call(kernel, out_shape=jax.ShapeDtypeStruct((count, rows, width...]
    pallas_call x1, Pallas kernels: 5.02 us -> 2.78 us  [gate_up_parts(): pl.pallas_call(kernel, out_shape=jax.ShapeDtypeStruct((parts, rows, width...]
where the time goes in v3:
time: 191 us; the launch traced here: 188 us
  waiting for transfers between devices  65.4 us (34%)
  blocking collectives  54.3 us (28%)
  starting transfers between devices  53.5 us (28%)
  other arithmetic  5.35 us (3%)
  local copies, waits for them, and re-layouts  4.32 us (2%)
  Pallas kernels  4.03 us (2%)
    all_to_all x1, blocking collectives, per_device(): partial = lax.all_to_all(partial, 'tensor', 0, 0, tiled=True)  25.3 us
    ppermute x6, starting transfers between devices, shifted(): return lax.ppermute(shard, ('expert', 'dp'), pairs)  20.6 us
    all_to_all x1, waiting for transfers between devices, per_device(): lax.all_to_all(jnp.broadcast_to(arrived.reshape(1, block, quarter), (RADI...  19.4 us
    ppermute x6, waiting for transfers between devices, shifted(): return lax.ppermute(shard, ('expert', 'dp'), pairs)  16 us
    all_to_all x1, blocking collectives, per_device(): hidden = lax.all_to_all(hidden_copies(partial), 'tensor', 0, 0, tiled=True)  14.5 us
    all_to_all x1, blocking collectives, per_device(): lax.all_to_all(packed.reshape(experts, capacity, quarter), 'expert', 0, 0...  14.5 us
    all_to_all x1, waiting for transfers between devices, per_device(): own = lax.all_to_all(own, 'dp', 0, 0, tiled=True, axis_index_groups=groups)  12.7 us
    all_to_all x1, waiting for transfers between devices, per_device(): lax.all_to_all(jnp.concatenate(slabs, axis=2), 'tensor', 0, 0, tiled=True)  12.1 us
  transfers between devices with their start and end apart: 10, of which 8 were waited for; matrix products, arithmetic and copies ran while one was open for 1% of the time, Pallas kernels for 0%

profile of v3, /device:TPU:1, one launch (start us, length us, event | category | flops | bytes accessed | tf_op | source)
XLA Modules:
  0.0 188.2 jit_solution(4234967524156522564)
XLA Ops:
  0.0 0.9 copy.15
  1.6 1.0 convolution_convert_fusion
  2.6 14.5 %all_to_all.35 = bf16[8,6,1024]{2,1,0:T(8,128)(2,1)S(1)} all-to-all(bf16[8,6,1024]{2,1,0:T(8,128)(2,1)S(1)} %reshape.76), channel_id=1, replica_groups=mesh['expert'=8,'dp'=16,'tensor'=4] {'expert'}, dimensions={0} | all-to-all | bytes 196608 | tf_op jit(solution)/shard_map/all_to_all | solution.py:141
  17.1 0.8 broadcast_in_dim.5
  17.9 11.3 %all-to-all-start.1 = ((bf16[4,48,1024]{2,1,0:T(8,128)(2,1)}), bf16[4,48,1024]{2,1,0:T(8,128)(2,1)S(1)}, u32[]{:S(2)}, u32[]{:S(2)}) async-start(bf16[4,48,1024]{2,1,0:T(8,128)(2,1)} %broadcast_in_dim.5), calls=%async_computation.1 | async-start | bytes 786432 | tf_op jit(solution)/shard_map/all_to_all | solution.py:142
  29.2 1.6 pad_maximum_fusion
  30.8 19.4 %all-to-all-done.1 = bf16[4,48,1024]{2,1,0:T(8,128)(2,1)S(1)} async-done(((bf16[4,48,1024]{2,1,0:T(8,128)(2,1)}), bf16[4,48,1024]{2,1,0:T(8,128)(2,1)S(1)}, u32[]{:S(2)}, u32[]{:S(2)}) %all-to-all-start.1) | async-done | bytes 393248 | tf_op jit(solution)/shard_map/all_to_all | solution.py:142
  50.1 4.0 %all-to-all-start.2 = ((bf16[4,1024,256]{2,1,0:T(8,128)(2,1)}), bf16[4,1024,256]{2,1,0:T(8,128)(2,1)S(1)}, u32[]{:S(2)}, u32[]{:S(2)}) async-start(bf16[4,1024,256]{2,1,0:T(8,128)(2,1)} %pad_maximum_fusion), calls=%async_computation.2 | async-start | bytes 4194304 | tf_op jit(solution)/shard_map/all_to_all | solution.py:134
  54.2 6.6 %collective-permute-start = (bf16[192,1024]{1,0:T(8,128)(2,1)S(1)}, bf16[192,1024]{1,0:T(8,128)(2,1)S(1)}, u32[]{:S(2)}, u32[]{:S(2)}) collective-permute-start(bf16[192,1024]{1,0:T(8,128)(2,1)S(1)} %bitcast.20), channel_id=1, source_target_pairs={{0,4},{4,8},{8,12},{12,16},{16,20},{20,24},{24,28},{28,32},{32,36}... | collective-permute-start | bytes 1179656 | tf_op jit(solution)/shard_map/ppermute | solution.py:27
  60.8 1.9 %collective-permute-start.1 = (bf16[192,1024]{1,0:T(8,128)(2,1)S(1)}, bf16[192,1024]{1,0:T(8,128)(2,1)S(1)}, u32[]{:S(2)}, u32[]{:S(2)}) collective-permute-start(bf16[192,1024]{1,0:T(8,128)(2,1)S(1)} %bitcast.21), channel_id=1, source_target_pairs={{0,60},{4,0},{8,4},{12,8},{16,12},{20,16},{24,20},{28,24},{32,28},... | collective-permute-start | bytes 1179656 | tf_op jit(solution)/shard_map/ppermute | solution.py:27
  62.7 4.5 %collective-permute-start.2 = (bf16[192,1024]{1,0:T(8,128)(2,1)S(1)}, bf16[192,1024]{1,0:T(8,128)(2,1)}, u32[]{:S(2)}, u32[]{:S(2)}) collective-permute-start(bf16[192,1024]{1,0:T(8,128)(2,1)S(1)} %bitcast.22), channel_id=1, source_target_pairs={{0,8},{4,12},{8,16},{12,20},{16,24},{20,28},{24,32},{28,36},{32,40... | collective-permute-start | bytes 1179656 | tf_op jit(solution)/shard_map/ppermute | solution.py:27
  67.3 12.1 %all-to-all-done.2.refs_4_ = bf16[4,1024,256]{2,1,0:T(8,128)(2,1)S(1)} async-done(((bf16[4,1024,256]{2,1,0:T(8,128)(2,1)}), bf16[4,1024,256]{2,1,0:T(8,128)(2,1)S(1)}, u32[]{:S(2)}, u32[]{:S(2)}) %all-to-all-start.2) | async-done | bytes 2097184 | tf_op jit(solution)/shard_map/all_to_all | solution.py:134
  79.4 3.1 %collective-permute-done.2.refs_3_ = bf16[192,1024]{1,0:T(8,128)(2,1)} collective-permute-done((bf16[192,1024]{1,0:T(8,128)(2,1)S(1)}, bf16[192,1024]{1,0:T(8,128)(2,1)}, u32[]{:S(2)}, u32[]{:S(2)}) %collective-permute-start.2) | collective-permute-done | bytes 393248 | tf_op jit(solution)/shard_map/ppermute | solution.py:27
  82.5 2.8 %gate_up_parts.1 = bf16[4,768,256]{2,1,0:T(8,128)(2,1)S(1)} custom-call(bf16[192,1024]{1,0:T(8,128)(2,1)S(1)} %bitcast.23, bf16[192,1024]{1,0:T(8,128)(2,1)S(1)} %collective-permute-done.refs_1_, bf16[192,1024]{1,0:T(8,128)(2,1)S(1)} %collective-permute-done.1.refs_2_, bf16[192,1024]{1,0:T(8,128)(2,1)} %collective-permute-done.2.refs_3_, ...), custom_call_target="tpu_custom_call" | custom-call | tf_op jit(solution)/shard_map/gate_up_parts/pallas_call | solution.py:64
  85.3 25.3 %all_to_all.36.in_ref = bf16[4,768,256]{2,1,0:T(8,128)(2,1)S(1)} all-to-all(bf16[4,768,256]{2,1,0:T(8,128)(2,1)S(1)} %gate_up_parts.1), channel_id=1, replica_groups=mesh['expert'=8,'dp'=16,'tensor'=4] {'tensor'}, dimensions={0} | all-to-all | bytes 3145728 | tf_op jit(solution)/shard_map/all_to_all | solution.py:153
  110.9 14.5 %all_to_all.37.hidden_ref = bf16[4,768,128]{2,1,0:T(8,128)(2,1)S(1)} all-to-all(bf16[4,768,128]{2,1,0:T(8,128)(2,1)S(1)} %hidden_copies.1), channel_id=1, replica_groups=mesh['expert'=8,'dp'=16,'tensor'=4] {'tensor'}, dimensions={0} | all-to-all | bytes 1572864 | tf_op jit(solution)/shard_map/all_to_all | solution.py:154
  125.4 1.0 down_sets.1
  126.4 1.9 %collective-permute-start.3 = (bf16[192,1024]{1,0:T(8,128)(2,1)S(1)}, bf16[192,1024]{1,0:T(8,128)(2,1)S(1)}, u32[]{:S(2)}, u32[]{:S(2)}) collective-permute-start(bf16[192,1024]{1,0:T(8,128)(2,1)S(1)} %get-tuple-element.10), channel_id=1, source_target_pairs={{0,60},{4,0},{8,4},{12,8},{16,12},{20,16},{24,20},{28,24},{32,28},... | collective-permute-start | bytes 1179656 | tf_op jit(solution)/shard_map/ppermute | solution.py:27
  128.3 3.4 %collective-permute-start.4 = (bf16[192,1024]{1,0:T(8,128)(2,1)S(1)}, bf16[192,1024]{1,0:T(8,128)(2,1)S(1)}, u32[]{:S(2)}, u32[]{:S(2)}) collective-permute-start(bf16[192,1024]{1,0:T(8,128)(2,1)S(1)} %get-tuple-element.11), channel_id=1, source_target_pairs={{0,4},{4,8},{8,12},{12,16},{16,20},{20,24},{24,28},{28,32},{32,36}... | collective-permute-start | bytes 1179656 | tf_op jit(solution)/shard_map/ppermute | solution.py:27
  131.7 2.2 %collective-permute-start.5 = (bf16[192,1024]{1,0:T(8,128)(2,1)S(1)}, bf16[192,1024]{1,0:T(8,128)(2,1)S(1)}, u32[]{:S(2)}, u32[]{:S(2)}) collective-permute-start(bf16[192,1024]{1,0:T(8,128)(2,1)S(1)} %get-tuple-element.12), channel_id=1, source_target_pairs={{0,56},{4,60},{8,0},{12,4},{16,8},{20,12},{24,16},{28,20},{32,24},... | collective-permute-start | bytes 1179656 | tf_op jit(solution)/shard_map/ppermute | solution.py:27
  133.9 3.8 %collective-permute-done.3 = bf16[192,1024]{1,0:T(8,128)(2,1)S(1)} collective-permute-done((bf16[192,1024]{1,0:T(8,128)(2,1)S(1)}, bf16[192,1024]{1,0:T(8,128)(2,1)S(1)}, u32[]{:S(2)}, u32[]{:S(2)}) %collective-permute-start.3) | collective-permute-done | bytes 393248 | tf_op jit(solution)/shard_map/ppermute | solution.py:27
  137.7 3.5 %collective-permute-done.4 = bf16[192,1024]{1,0:T(8,128)(2,1)S(1)} collective-permute-done((bf16[192,1024]{1,0:T(8,128)(2,1)S(1)}, bf16[192,1024]{1,0:T(8,128)(2,1)S(1)}, u32[]{:S(2)}, u32[]{:S(2)}) %collective-permute-start.4) | collective-permute-done | bytes 393248 | tf_op jit(solution)/shard_map/ppermute | solution.py:27
  141.2 5.6 %collective-permute-done.5 = bf16[192,1024]{1,0:T(8,128)(2,1)S(1)} collective-permute-done((bf16[192,1024]{1,0:T(8,128)(2,1)S(1)}, bf16[192,1024]{1,0:T(8,128)(2,1)S(1)}, u32[]{:S(2)}, u32[]{:S(2)}) %collective-permute-start.5) | collective-permute-done | bytes 393248 | tf_op jit(solution)/shard_map/ppermute | solution.py:27
  146.8 1.0 add_convert_fusion
  147.8 5.7 %all-to-all-start.5 = ((bf16[4,48,1024]{2,1,0:T(8,128)(2,1)}), bf16[4,48,1024]{2,1,0:T(8,128)(2,1)S(1)}, u32[]{:S(2)}, u32[]{:S(2)}) async-start(bf16[4,48,1024]{2,1,0:T(8,128)(2,1)} %bitcast.5), calls=%async_computation.5 | async-start | bytes 786432 | tf_op jit(solution)/shard_map/all_to_all | solution.py:159
  153.7 0.7 slice.6
  154.6 12.7 %all-to-all-done.5 = bf16[4,48,1024]{2,1,0:T(8,128)(2,1)S(1)} async-done(((bf16[4,48,1024]{2,1,0:T(8,128)(2,1)}), bf16[4,48,1024]{2,1,0:T(8,128)(2,1)S(1)}, u32[]{:S(2)}, u32[]{:S(2)}) %all-to-all-start.5) | async-done | bytes 393248 | tf_op jit(solution)/shard_map/all_to_all | solution.py:159
  167.4 0.7 reshape.81
  168.1 11.8 %all-to-all-start.6 = ((bf16[8,6,1024]{2,1,0:T(8,128)(2,1)}), bf16[8,6,1024]{2,1,0:T(8,128)(2,1)S(1)}, u32[]{:S(2)}, u32[]{:S(2)}) async-start(bf16[8,6,1024]{2,1,0:T(8,128)(2,1)} %reshape.81), calls=%async_computation.6 | async-start | bytes 262144 | tf_op jit(solution)/shard_map/all_to_all | solution.py:161
  179.9 5.3 %all-to-all-done.6 = bf16[8,6,1024]{2,1,0:T(8,128)(2,1)S(1)} async-done(((bf16[8,6,1024]{2,1,0:T(8,128)(2,1)}), bf16[8,6,1024]{2,1,0:T(8,128)(2,1)S(1)}, u32[]{:S(2)}, u32[]{:S(2)}) %all-to-all-start.6) | async-done | bytes 98336 | tf_op jit(solution)/shard_map/all_to_all | solution.py:161
  185.2 0.6 gather_fusion
  186.2 2.1 %fusion.2 = bf16[16,1024]{1,0:T(8,128)(2,1)} fusion(f32[1,16,1024]{2,0,1:T(1,128)S(1)} %fusion, f32[16,1024]{1,0:T(8,128)S(1)} %multiply_reduce_fusion, f32[]{:T(128)} %bitcast, bf16[16,4096]{1,0:T(8,128)(2,1)} %param.8, s32[]{:T(128)S(6)} %select_n.13), kind=kLoop, calls=%fused_computation.8 | loop fusion | flops 81920 | bytes 196616 | tf_op jit(solution)/shard_map/convert_element_type | solution.py:171
  (36 shorter events, 1.9 us)
Async XLA Ops:
  0.0 154.3 %copy-start = (bf16[8,16,1024]{2,1,0:T(8,128)(2,1)S(1)}, bf16[8,16,1024]{2,1,0:T(8,128)(2,1)}, u32[]{:S(2)}) copy-start(bf16[8,16,1024]{2,1,0:T(8,128)(2,1)} %param.14) | copy-start | bytes 786436
  0.0 29.2 %copy-start.3 = (bf16[1,4096,128]{2,1,0:T(8,128)(2,1)S(1)}, bf16[1,4096,128]{2,1,0:T(8,128)(2,1)}, u32[]{:S(2)}) copy-start(bf16[1,4096,128]{2,1,0:T(8,128)(2,1)} %param.11) | copy-start | bytes 3145732
  0.0 29.2 %copy-start.2 = (bf16[1,4096,128]{2,1,0:T(8,128)(2,1)S(1)}, bf16[1,4096,128]{2,1,0:T(8,128)(2,1)}, u32[]{:S(2)}) copy-start(bf16[1,4096,128]{2,1,0:T(8,128)(2,1)} %param.12) | copy-start | bytes 3145732
  17.9 32.3 %all-to-all-start.1 = ((bf16[4,48,1024]{2,1,0:T(8,128)(2,1)}), bf16[4,48,1024]{2,1,0:T(8,128)(2,1)S(1)}, u32[]{:S(2)}, u32[]{:S(2)}) async-start(bf16[4,48,1024]{2,1,0:T(8,128)(2,1)} %broadcast_in_dim.5), calls=%async_computation.1 | async-start | bytes 786432 | tf_op jit(solution)/shard_map/all_to_all | solution.py:142
  50.1 29.2 %all-to-all-start.2 = ((bf16[4,1024,256]{2,1,0:T(8,128)(2,1)}), bf16[4,1024,256]{2,1,0:T(8,128)(2,1)S(1)}, u32[]{:S(2)}, u32[]{:S(2)}) async-start(bf16[4,1024,256]{2,1,0:T(8,128)(2,1)} %pad_maximum_fusion), calls=%async_computation.2 | async-start | bytes 4194304 | tf_op jit(solution)/shard_map/all_to_all | solution.py:134
  54.2 25.2 %collective-permute-start = (bf16[192,1024]{1,0:T(8,128)(2,1)S(1)}, bf16[192,1024]{1,0:T(8,128)(2,1)S(1)}, u32[]{:S(2)}, u32[]{:S(2)}) collective-permute-start(bf16[192,1024]{1,0:T(8,128)(2,1)S(1)} %bitcast.20), channel_id=1, source_target_pairs={{0,4},{4,8},{8,12},{12,16},{16,20},{20,24},{24,28},{28,32},{32,36}... | collective-permute-start | bytes 1179656 | tf_op jit(solution)/shard_map/ppermute | solution.py:27
  60.8 18.6 %collective-permute-start.1 = (bf16[192,1024]{1,0:T(8,128)(2,1)S(1)}, bf16[192,1024]{1,0:T(8,128)(2,1)S(1)}, u32[]{:S(2)}, u32[]{:S(2)}) collective-permute-start(bf16[192,1024]{1,0:T(8,128)(2,1)S(1)} %bitcast.21), channel_id=1, source_target_pairs={{0,60},{4,0},{8,4},{12,8},{16,12},{20,16},{24,20},{28,24},{32,28},... | collective-permute-start | bytes 1179656 | tf_op jit(solution)/shard_map/ppermute | solution.py:27
  62.7 19.8 %collective-permute-start.2 = (bf16[192,1024]{1,0:T(8,128)(2,1)S(1)}, bf16[192,1024]{1,0:T(8,128)(2,1)}, u32[]{:S(2)}, u32[]{:S(2)}) collective-permute-start(bf16[192,1024]{1,0:T(8,128)(2,1)S(1)} %bitcast.22), channel_id=1, source_target_pairs={{0,8},{4,12},{8,16},{12,20},{16,24},{20,28},{24,32},{28,36},{32,40... | collective-permute-start | bytes 1179656 | tf_op jit(solution)/shard_map/ppermute | solution.py:27
  110.6 14.8 %copy-start.1 = (bf16[1,512,1024]{2,1,0:T(8,128)(2,1)S(1)}, bf16[1,512,1024]{2,1,0:T(8,128)(2,1)}, u32[]{:S(2)}) copy-start(bf16[1,512,1024]{2,1,0:T(8,128)(2,1)} %param.13) | copy-start | bytes 3145732
  125.4 28.1 %copy-start.4 = (f32[16,2]{0,1:T(2,128)S(1)}, f32[16,2]{0,1:T(2,128)}, u32[]{:S(2)}) copy-start(f32[16,2]{0,1:T(2,128)} %param.10) | copy-start | bytes 388
  125.4 28.3 %copy-start.5 = (f32[9]{0:T(128)S(1)}, f32[9]{0:T(128)}, u32[]{:S(2)}) copy-start(f32[9]{0:T(128)} %param.15) | copy-start | bytes 112
  126.4 11.3 %collective-permute-start.3 = (bf16[192,1024]{1,0:T(8,128)(2,1)S(1)}, bf16[192,1024]{1,0:T(8,128)(2,1)S(1)}, u32[]{:S(2)}, u32[]{:S(2)}) collective-permute-start(bf16[192,1024]{1,0:T(8,128)(2,1)S(1)} %get-tuple-element.10), channel_id=1, source_target_pairs={{0,60},{4,0},{8,4},{12,8},{16,12},{20,16},{24,20},{28,24},{32,28},... | collective-permute-start | bytes 1179656 | tf_op jit(solution)/shard_map/ppermute | solution.py:27
  128.3 12.8 %collective-permute-start.4 = (bf16[192,1024]{1,0:T(8,128)(2,1)S(1)}, bf16[192,1024]{1,0:T(8,128)(2,1)S(1)}, u32[]{:S(2)}, u32[]{:S(2)}) collective-permute-start(bf16[192,1024]{1,0:T(8,128)(2,1)S(1)} %get-tuple-element.11), channel_id=1, source_target_pairs={{0,4},{4,8},{8,12},{12,16},{16,20},{20,24},{24,28},{28,32},{32,36}... | collective-permute-start | bytes 1179656 | tf_op jit(solution)/shard_map/ppermute | solution.py:27
  131.7 15.1 %collective-permute-start.5 = (bf16[192,1024]{1,0:T(8,128)(2,1)S(1)}, bf16[192,1024]{1,0:T(8,128)(2,1)S(1)}, u32[]{:S(2)}, u32[]{:S(2)}) collective-permute-start(bf16[192,1024]{1,0:T(8,128)(2,1)S(1)} %get-tuple-element.12), channel_id=1, source_target_pairs={{0,56},{4,60},{8,0},{12,4},{16,8},{20,12},{24,16},{28,20},{32,24},... | collective-permute-start | bytes 1179656 | tf_op jit(solution)/shard_map/ppermute | solution.py:27
  147.8 19.5 %all-to-all-start.5 = ((bf16[4,48,1024]{2,1,0:T(8,128)(2,1)}), bf16[4,48,1024]{2,1,0:T(8,128)(2,1)S(1)}, u32[]{:S(2)}, u32[]{:S(2)}) async-start(bf16[4,48,1024]{2,1,0:T(8,128)(2,1)} %bitcast.5), calls=%async_computation.5 | async-start | bytes 786432 | tf_op jit(solution)/shard_map/all_to_all | solution.py:159
  168.1 17.1 %all-to-all-start.6 = ((bf16[8,6,1024]{2,1,0:T(8,128)(2,1)}), bf16[8,6,1024]{2,1,0:T(8,128)(2,1)S(1)}, u32[]{:S(2)}, u32[]{:S(2)}) async-start(bf16[8,6,1024]{2,1,0:T(8,128)(2,1)} %reshape.81), calls=%async_computation.6 | async-start | bytes 262144 | tf_op jit(solution)/shard_map/all_to_all | solution.py:161

commit v4 on v3

v4 whole, which is shorter than its diff:
```python
import jax
import jax.numpy as jnp
import numpy as np
from jax import lax
from jax.experimental import pallas as pl
from jax.experimental.pallas import tpu as pltpu
from jax.sharding import PartitionSpec as P

RADIX = 4
LANES = 128
SHIFTS = (0, 1, 3, 2)


LIMIT = pltpu.CompilerParams(vmem_limit_bytes=16 * 2**20)
SMEM = pl.BlockSpec(memory_space=pltpu.SMEM)
VMEM = pl.BlockSpec(memory_space=pltpu.VMEM)


def far_groups(count):
    stride = count // RADIX
    return [[low + stride * high for high in range(RADIX)] for low in range(stride)]


def shifted(shard, even_shift, odd_shift):
    experts, count = lax.axis_size("expert"), lax.axis_size("dp")
    pairs = []
    for expert in range(experts):
        shift = odd_shift if expert % 2 else even_shift
        for place in range(count):
            pairs.append((expert * count + place, expert * count + (place + shift) % count))
    return lax.ppermute(shard, ("expert", "dp"), pairs)


def to_neighbours(shards):
    above, second, below = shards
    return [shifted(above, 1, 1), shifted(below, -1, -1), shifted(second, 2, -2)]


def assignment_slots(expert_ids, experts, capacity):
    flat_ids = expert_ids.reshape(-1)
    matches = (flat_ids[:, None] == jnp.arange(experts, dtype=jnp.int32)[None, :]).astype(jnp.int32)
    earlier = jnp.cumsum(matches, axis=0) - matches
    slot_ids = jnp.sum(earlier * matches, axis=1)
    return flat_ids * capacity + slot_ids


def packed_rows(gathered, offset, feature_width, experts, capacity, chosen_count, block):
    rows = gathered.shape[0]
    groups = rows // block // RADIX
    set_rows = groups * capacity
    per_expert = RADIX * set_rows

    def kernel(offset_ref, in_ref, out_ref):
        labels = in_ref[:, feature_width:].astype(jnp.float32)
        lanes = labels.shape[1]
        lane = lax.broadcasted_iota(jnp.int32, (rows, lanes), 1).astype(jnp.float32)
        named = jnp.zeros((rows, lanes), jnp.float32)
        for place in range(chosen_count):
            named += (labels[:, place : place + 1] == lane).astype(jnp.float32)
        row = lax.broadcasted_iota(jnp.int32, (rows, rows), 0)
        column = lax.broadcasted_iota(jnp.int32, (rows, rows), 1)
        before = ((row // block == column // block) & (column < row)).astype(jnp.float32)
        earlier = jnp.dot(
            before.astype(jnp.bfloat16), named.astype(jnp.bfloat16), preferred_element_type=jnp.float32
        )
        source = lax.broadcasted_iota(jnp.int32, (rows, lanes), 0) // block
        residue = (source % RADIX - offset_ref[0] + RADIX) % RADIX
        first = (residue * set_rows + source // RADIX * capacity).astype(jnp.float32)
        target = jnp.where(named > 0.0, first + earlier, -1.0).T
        wanted = lax.broadcasted_iota(jnp.int32, (per_expert, rows), 0).astype(jnp.float32)
        chosen = [(wanted == target[expert : expert + 1, :]).astype(jnp.float32) for expert in range(experts)]
        chosen = jnp.concatenate(chosen, axis=0).astype(jnp.bfloat16)
        out = jnp.dot(chosen, in_ref[:, :feature_width], preferred_element_type=jnp.float32)
        out_ref[...] = out.astype(out_ref.dtype).reshape(out_ref.shape)

    return pl.pallas_call(
        kernel,
        out_shape=jax.ShapeDtypeStruct((experts, per_expert, feature_width), gathered.dtype),
        in_specs=[SMEM, VMEM],
        out_specs=VMEM,
        compiler_params=LIMIT,
        name="packed_rows",
    )(offset, gathered)


def weights_by_features(gate_weight, up_weight, quarter):
    parts = lax.axis_size("tensor")
    here = lax.axis_index("tensor")
    slabs = [w.reshape(parts, quarter, -1) for w in (gate_weight, up_weight)]

    def slab(shift):
        place = (here + shift) % parts
        both = [lax.dynamic_index_in_dim(w, place, 0, keepdims=False) for w in slabs]
        both = jnp.concatenate(both, axis=1)
        if shift == 0:
            return both
        return lax.ppermute(both, "tensor", [(i, (i + shift) % parts) for i in range(parts)])

    return [slab(shift) for shift in SHIFTS]


def gate_up_parts(rows, weights, place):
    parts = len(weights)
    width = weights[0].shape[1]
    count = rows.shape[0] * rows.shape[1]

    def kernel(place_ref, in_ref, *refs):
        w_refs, out_ref = refs[:-1], refs[-1]
        stacked = in_ref[...].reshape(count, in_ref.shape[2])
        for shift, w_ref in zip(SHIFTS, w_refs):
            part = (place_ref[0] + (parts - shift)) % parts
            out = jnp.dot(stacked, w_ref[...], preferred_element_type=jnp.float32)
            out_ref[part] = out.astype(out_ref.dtype)

    return pl.pallas_call(
        kernel,
        out_shape=jax.ShapeDtypeStruct((parts, count, width), jnp.bfloat16),
        in_specs=[SMEM] + [VMEM] * (1 + parts),
        out_specs=VMEM,
        compiler_params=LIMIT,
        name="gate_up_parts",
    )(place, rows, *weights)


def hidden_copies(parts):
    count, rows, both = parts.shape
    width = both // 2

    def kernel(in_ref, out_ref):
        total = in_ref[0].astype(jnp.float32)
        for part in range(1, count):
            total += in_ref[part].astype(jnp.float32)
        gate, up = total[:, :width], total[:, width:]
        hidden = (gate / (1.0 + jnp.exp(-gate)) * up).astype(out_ref.dtype)
        for part in range(count):
            out_ref[part] = hidden

    return pl.pallas_call(
        kernel,
        out_shape=jax.ShapeDtypeStruct((count, rows, width), jnp.bfloat16),
        in_specs=[VMEM],
        out_specs=VMEM,
        compiler_params=LIMIT,
        name="hidden_copies",
    )(parts)


def down_sets(hidden, w_down, experts):
    parts, rows, _ = hidden.shape
    set_rows = rows // RADIX
    piece = set_rows // experts
    features = w_down.shape[1]

    def kernel(hidden_ref, w_ref, *out_refs):
        wide = jnp.concatenate([hidden_ref[part] for part in range(parts)], axis=1)
        out = jnp.dot(wide, w_ref[...], preferred_element_type=jnp.float32)
        for place, ref in enumerate(out_refs):
            starts = [(expert * RADIX + place) * piece for expert in range(experts)]
            ref[...] = jnp.concatenate([out[at : at + piece] for at in starts], axis=0).astype(ref.dtype)

    return pl.pallas_call(
        kernel,
        out_shape=[
            jax.ShapeDtypeStruct((set_rows, features), jnp.bfloat16 if place else jnp.float32)
            for place in range(RADIX)
        ],
        in_specs=[VMEM, VMEM],
        out_specs=[VMEM] * RADIX,
        compiler_params=LIMIT,
        name="down_sets",
    )(hidden, w_down)


def summed_by_block(own, others, experts, capacity):
    rows, features = own.shape
    order = np.arange(rows).reshape(experts, RADIX, capacity).transpose(1, 0, 2).reshape(-1)
    moved = jnp.asarray(np.eye(rows)[order], jnp.bfloat16)

    def kernel(moved_ref, own_ref, *refs):
        other_refs, out_ref = refs[:-1], refs[-1]
        total = own_ref[...]
        for ref in other_refs:
            total += ref[...].astype(jnp.float32)
        out = jnp.dot(moved_ref[...], total.astype(jnp.bfloat16), preferred_element_type=jnp.float32)
        out_ref[...] = out.astype(out_ref.dtype).reshape(out_ref.shape)

    return pl.pallas_call(
        kernel,
        out_shape=jax.ShapeDtypeStruct((RADIX, rows // RADIX, features), jnp.bfloat16),
        in_specs=[VMEM] * (2 + len(others)),
        out_specs=VMEM,
        compiler_params=LIMIT,
        name="summed_by_block",
    )(moved, own, *others)


def per_device(
    tokens, expert_ids, route_weight, gate_weight, up_weight, down_weight, past_layers, dwa_weight
):
    experts = lax.axis_size("expert")
    parts = lax.axis_size("tensor")
    tok_rows, feature_width = tokens.shape
    chosen_count = expert_ids.shape[1]
    capacity = min(tok_rows, 3 * chosen_count * tok_rows // (2 * experts))
    quarter = feature_width // parts
    groups = far_groups(lax.axis_size("dp"))
    block = experts * capacity

    weights = weights_by_features(gate_weight, up_weight, quarter)
    first_column = lax.axis_index("tensor") * quarter
    own_columns = lax.dynamic_slice_in_dim(tokens, first_column, quarter, 1)
    labels = jnp.pad(expert_ids.astype(tokens.dtype), ((0, 0), (0, LANES - chosen_count)))
    gathered = lax.all_gather(jnp.concatenate([own_columns, labels], axis=1), "dp", axis=0, tiled=True)
    offset = (lax.axis_index("dp") % RADIX).reshape(1)
    packed = packed_rows(gathered, offset, quarter, experts, capacity, chosen_count, tok_rows)
    rows = lax.all_to_all(packed, "expert", 0, 0, tiled=True)

    partial = gate_up_parts(rows, weights, lax.axis_index("tensor").reshape(1))
    partial = lax.all_to_all(partial, "tensor", 0, 0, tiled=True)
    hidden = lax.all_to_all(hidden_copies(partial), "tensor", 0, 0, tiled=True)
    own, *others = down_sets(hidden, down_weight[0], experts)
    own = summed_by_block(own, to_neighbours(others), experts, capacity)
    own = lax.all_to_all(own, "dp", 0, 0, tiled=True, axis_index_groups=groups)
    expert_out = jnp.sum(own.astype(jnp.float32), axis=0).astype(jnp.bfloat16)
    returned_rows = lax.all_to_all(
        expert_out.reshape(experts, capacity, quarter), "expert", 0, 0, tiled=True
    ).reshape(block, quarter)

    targets = assignment_slots(expert_ids, experts, capacity)
    fetched = returned_rows[targets].astype(jnp.float32).reshape(tok_rows, chosen_count, quarter)
    shares = route_weight / jnp.sum(route_weight, axis=1, keepdims=True)
    expert_mix = jnp.sum(fetched * shares[:, :, None], axis=1)
    current = own_columns.astype(jnp.float32) + expert_mix
    depth = past_layers.shape[0]
    history = jnp.einsum("j,jtd->td", dwa_weight[:depth], past_layers.astype(jnp.float32))
    return (dwa_weight[depth] * current + history).astype(jnp.bfloat16)


def solution(mesh):
    return jax.shard_map(
        per_device,
        mesh=mesh,
        in_specs=(
            P(("expert", "dp"), None),
            P(("expert", "dp"), None),
            P(("expert", "dp"), None),
            P("expert", None, ("dp", "tensor")),
            P("expert", None, ("dp", "tensor")),
            P("expert", "dp", "tensor"),
            P(None, ("expert", "dp"), "tensor"),
            P(),
        ),
        out_specs=P(("expert", "dp"), "tensor"),
        check_vma=False,
    )
```

time: 191 us -> 188 us (0.984)
  blocking collectives: 54.3 us -> 68.7 us
  starting transfers between devices: 53.5 us -> 42.7 us
  waiting for transfers between devices: 65.4 us -> 58.8 us
  local copies, waits for them, and re-layouts: 4.32 us -> 6.57 us
  Pallas kernels: 4.03 us -> 6.22 us
    all_gather x0 -> x1, blocking collectives: none -> 32.1 us  [per_device(): lax.all_gather(jnp.concatenate([own_columns, labels], axis=1), 'dp', axis...]
    all_to_all x2 -> x1, waiting for transfers between devices: 31.4 us -> 0.01 us  [per_device(): rows = lax.all_to_all(packed, 'expert', 0, 0, tiled=True)]
    ppermute x0 -> x3, waiting for transfers between devices: none -> 18.3 us  [slab(): lax.ppermute(both, 'tensor', [(i, (i + shift) % parts) for i in range(par...]
    all_to_all x1 -> x0, blocking collectives: 14.5 us -> none  [per_device(): lax.all_to_all(packed.reshape(experts, capacity, quarter), 'expert', 0, 0...]
    ppermute x6 -> x3, starting transfers between devices: 20.6 us -> 8.41 us  [shifted(): return lax.ppermute(shard, ('expert', 'dp'), pairs)]
    ppermute x0 -> x3, starting transfers between devices: none -> 9.94 us  [slab(): lax.ppermute(both, 'tensor', [(i, (i + shift) % parts) for i in range(par...]
    all_to_all x1, waiting for transfers between devices: 12.7 us -> 19.9 us  [per_device(): own = lax.all_to_all(own, 'dp', 0, 0, tiled=True, axis_index_groups=groups)]
    all_to_all x1, starting transfers between devices: 11.8 us -> 5.21 us  [per_device(): lax.all_to_all(expert_out.reshape(experts, capacity, quarter), 'expert',...]
  transfers between devices with their start and end apart: 10 -> 9, of which waited for: 8 -> 8; matrix products, arithmetic and copies ran while one was open for 1% -> 2% of each run, Pallas kernels for 0% -> 0%
where the time goes in v4:
time: 188 us; the launch traced here: 187 us
  blocking collectives  68.7 us (37%)
  waiting for transfers between devices  58.8 us (31%)
  starting transfers between devices  42.7 us (23%)
  local copies, waits for them, and re-layouts  6.57 us (3%)
  Pallas kernels  6.22 us (3%)
  other arithmetic  3.67 us (2%)
    all_gather x1, blocking collectives, per_device(): lax.all_gather(jnp.concatenate([own_columns, labels], axis=1), 'dp', axis...  32.1 us
    all_to_all x1, blocking collectives, per_device(): partial = lax.all_to_all(partial, 'tensor', 0, 0, tiled=True)  23.6 us
    all_to_all x1, waiting for transfers between devices, per_device(): own = lax.all_to_all(own, 'dp', 0, 0, tiled=True, axis_index_groups=groups)  19.9 us
    ppermute x3, waiting for transfers between devices, slab(): lax.ppermute(both, 'tensor', [(i, (i + shift) % parts) for i in range(par...  18.3 us
    ppermute x3, waiting for transfers between devices, shifted(): return lax.ppermute(shard, ('expert', 'dp'), pairs)  15.4 us
    all_to_all x1, blocking collectives, per_device(): hidden = lax.all_to_all(hidden_copies(partial), 'tensor', 0, 0, tiled=True)  13 us
    all_to_all x1, starting transfers between devices, per_device(): rows = lax.all_to_all(packed, 'expert', 0, 0, tiled=True)  12.8 us
    ppermute x3, starting transfers between devices, slab(): lax.ppermute(both, 'tensor', [(i, (i + shift) % parts) for i in range(par...  9.94 us
  transfers between devices with their start and end apart: 9, of which 8 were waited for; matrix products, arithmetic and copies ran while one was open for 2% of the time, Pallas kernels for 0%

profile of v4, /device:TPU:1, one launch (start us, length us, event | category | flops | bytes accessed | tf_op | source)
XLA Modules:
  0.0 187.1 jit_solution(14067633902848699755)
XLA Ops:
  0.0 0.8 broadcast_multiply_fusion
  0.9 0.8 constant_dynamic-slice_fusion
  1.6 32.1 %all_gather.3.in_ref = bf16[256,1152]{1,0:T(8,128)(2,1)S(1)} all-gather(bf16[16,1152]{1,0:T(8,128)(2,1)S(1)} %fusion.4), channel_id=1, replica_groups=mesh['expert'=8,'dp'=16,'tensor'=4] {'dp'}, dimensions={0}, use_global_device_ids=true | all-gather | bytes 626688 | tf_op jit(solution)/shard_map/all_gather | solution.py:213
  33.8 2.0 %packed_rows.1 = bf16[8,96,1024]{2,1,0:T(8,128)(2,1)} custom-call(s32[1]{0:T(128)} %bitcast.2.offset_ref, bf16[256,1152]{1,0:T(8,128)(2,1)S(1)} %all_gather.3.in_ref), custom_call_target="tpu_custom_call" | custom-call | tf_op jit(solution)/shard_map/packed_rows/pallas_call | solution.py:76
  35.8 12.8 %all-to-all-start = ((bf16[8,96,1024]{2,1,0:T(8,128)(2,1)}), bf16[8,96,1024]{2,1,0:T(8,128)(2,1)S(1)}, u32[]{:S(2)}, u32[]{:S(2)}) async-start(bf16[8,96,1024]{2,1,0:T(8,128)(2,1)} %packed_rows.1), calls=%async_computation | async-start | bytes 3145728 | tf_op jit(solution)/shard_map/all_to_all | solution.py:216
  48.6 1.3 dynamic-slice_bitcast_fusion
  50.0 4.7 %collective-permute-start.2 = (bf16[1024,256]{1,0:T(8,128)(2,1)S(1)}, bf16[1024,256]{1,0:T(8,128)(2,1)S(1)}, u32[]{:S(2)}, u32[]{:S(2)}) collective-permute-start(bf16[1024,256]{1,0:T(8,128)(2,1)S(1)} %pad_maximum_fusion.3), channel_id=1, source_target_pairs={{0,2},{1,3},{2,0},{3,1},{4,6},{5,7},{6,4},{7,5},{8,10},{9,11},{10,... | collective-permute-start | bytes 1572872 | tf_op jit(solution)/shard_map/ppermute | solution.py:97
  54.7 2.8 %collective-permute-start.1 = (bf16[1024,256]{1,0:T(8,128)(2,1)S(1)}, bf16[1024,256]{1,0:T(8,128)(2,1)S(1)}, u32[]{:S(2)}, u32[]{:S(2)}) collective-permute-start(bf16[1024,256]{1,0:T(8,128)(2,1)S(1)} %pad_maximum_fusion.2), channel_id=1, source_target_pairs={{0,3},{1,0},{2,1},{3,2},{4,7},{5,4},{6,5},{7,6},{8,11},{9,8},{10,9... | collective-permute-start | bytes 1572872 | tf_op jit(solution)/shard_map/ppermute | solution.py:97
  57.6 2.5 %collective-permute-start = (bf16[1024,256]{1,0:T(8,128)(2,1)S(1)}, bf16[1024,256]{1,0:T(8,128)(2,1)S(1)}, u32[]{:S(2)}, u32[]{:S(2)}) collective-permute-start(bf16[1024,256]{1,0:T(8,128)(2,1)S(1)} %pad_maximum_fusion.1), channel_id=1, source_target_pairs={{0,1},{1,2},{2,3},{3,0},{4,5},{5,6},{6,7},{7,4},{8,9},{9,10},{10,1... | collective-permute-start | bytes 1572872 | tf_op jit(solution)/shard_map/ppermute | solution.py:97
  60.2 6.7 %collective-permute-done.2.refs_3_ = bf16[1024,256]{1,0:T(8,128)(2,1)S(1)} collective-permute-done((bf16[1024,256]{1,0:T(8,128)(2,1)S(1)}, bf16[1024,256]{1,0:T(8,128)(2,1)S(1)}, u32[]{:S(2)}, u32[]{:S(2)}) %collective-permute-start.2) | collective-permute-done | bytes 524320 | tf_op jit(solution)/shard_map/ppermute | solution.py:97
  66.9 11.3 %collective-permute-done.1.refs_2_ = bf16[1024,256]{1,0:T(8,128)(2,1)S(1)} collective-permute-done((bf16[1024,256]{1,0:T(8,128)(2,1)S(1)}, bf16[1024,256]{1,0:T(8,128)(2,1)S(1)}, u32[]{:S(2)}, u32[]{:S(2)}) %collective-permute-start.1) | collective-permute-done | bytes 524320 | tf_op jit(solution)/shard_map/ppermute | solution.py:97
  78.5 0.8 copy-done.2
  79.3 1.0 copy-done.3
  80.3 1.9 gate_up_parts.1
  82.2 23.6 %all_to_all.25.in_ref = bf16[4,768,256]{2,1,0:T(8,128)(2,1)S(1)} all-to-all(bf16[4,768,256]{2,1,0:T(8,128)(2,1)S(1)} %gate_up_parts.1), channel_id=1, replica_groups=mesh['expert'=8,'dp'=16,'tensor'=4] {'tensor'}, dimensions={0} | all-to-all | bytes 3145728 | tf_op jit(solution)/shard_map/all_to_all | solution.py:219
  106.0 13.0 %all_to_all.26.hidden_ref = bf16[4,768,128]{2,1,0:T(8,128)(2,1)S(1)} all-to-all(bf16[4,768,128]{2,1,0:T(8,128)(2,1)S(1)} %hidden_copies.1), channel_id=1, replica_groups=mesh['expert'=8,'dp'=16,'tensor'=4] {'tensor'}, dimensions={0} | all-to-all | bytes 1572864 | tf_op jit(solution)/shard_map/all_to_all | solution.py:220
  119.0 1.0 down_sets.1
  120.0 1.9 %collective-permute-start.3 = (bf16[192,1024]{1,0:T(8,128)(2,1)S(1)}, bf16[192,1024]{1,0:T(8,128)(2,1)S(1)}, u32[]{:S(2)}, u32[]{:S(2)}) collective-permute-start(bf16[192,1024]{1,0:T(8,128)(2,1)S(1)} %get-tuple-element.10), channel_id=1, source_target_pairs={{0,4},{4,8},{8,12},{12,16},{16,20},{20,24},{24,28},{28,32},{32,36}... | collective-permute-start | bytes 1179656 | tf_op jit(solution)/shard_map/ppermute | solution.py:31
  121.9 4.6 %collective-permute-start.4 = (bf16[192,1024]{1,0:T(8,128)(2,1)S(1)}, bf16[192,1024]{1,0:T(8,128)(2,1)S(1)}, u32[]{:S(2)}, u32[]{:S(2)}) collective-permute-start(bf16[192,1024]{1,0:T(8,128)(2,1)S(1)} %get-tuple-element.11), channel_id=1, source_target_pairs={{0,60},{4,0},{8,4},{12,8},{16,12},{20,16},{24,20},{28,24},{32,28},... | collective-permute-start | bytes 1179656 | tf_op jit(solution)/shard_map/ppermute | solution.py:31
  126.5 1.9 %collective-permute-start.5 = (bf16[192,1024]{1,0:T(8,128)(2,1)S(1)}, bf16[192,1024]{1,0:T(8,128)(2,1)S(1)}, u32[]{:S(2)}, u32[]{:S(2)}) collective-permute-start(bf16[192,1024]{1,0:T(8,128)(2,1)S(1)} %get-tuple-element.12), channel_id=1, source_target_pairs={{0,8},{4,12},{8,16},{12,20},{16,24},{20,28},{24,32},{28,36},{32,40... | collective-permute-start | bytes 1179656 | tf_op jit(solution)/shard_map/ppermute | solution.py:31
  128.5 2.6 %collective-permute-done.3.refs_0_ = bf16[192,1024]{1,0:T(8,128)(2,1)S(1)} collective-permute-done((bf16[192,1024]{1,0:T(8,128)(2,1)S(1)}, bf16[192,1024]{1,0:T(8,128)(2,1)S(1)}, u32[]{:S(2)}, u32[]{:S(2)}) %collective-permute-start.3) | collective-permute-done | bytes 393248 | tf_op jit(solution)/shard_map/ppermute | solution.py:31
  131.0 1.3 collective-permute-done.4.refs_1_
  132.3 11.5 %collective-permute-done.5.refs_2_ = bf16[192,1024]{1,0:T(8,128)(2,1)S(1)} collective-permute-done((bf16[192,1024]{1,0:T(8,128)(2,1)S(1)}, bf16[192,1024]{1,0:T(8,128)(2,1)S(1)}, u32[]{:S(2)}, u32[]{:S(2)}) %collective-permute-start.5) | collective-permute-done | bytes 393248 | tf_op jit(solution)/shard_map/ppermute | solution.py:31
  143.9 1.1 summed_by_block.1
  145.0 6.3 %all-to-all-start.3 = ((bf16[4,48,1024]{2,1,0:T(8,128)(2,1)}), bf16[4,48,1024]{2,1,0:T(8,128)(2,1)S(1)}, u32[]{:S(2)}, u32[]{:S(2)}) async-start(bf16[4,48,1024]{2,1,0:T(8,128)(2,1)} %summed_by_block.1), calls=%async_computation.3 | async-start | bytes 786432 | tf_op jit(solution)/shard_map/all_to_all | solution.py:223
  151.9 0.7 slice.6
  153.0 19.9 %all-to-all-done.3 = bf16[4,48,1024]{2,1,0:T(8,128)(2,1)S(1)} async-done(((bf16[4,48,1024]{2,1,0:T(8,128)(2,1)}), bf16[4,48,1024]{2,1,0:T(8,128)(2,1)S(1)}, u32[]{:S(2)}, u32[]{:S(2)}) %all-to-all-start.3) | async-done | bytes 393248 | tf_op jit(solution)/shard_map/all_to_all | solution.py:223
  172.9 0.7 reshape.58
  173.6 5.2 %all-to-all-start.4 = ((bf16[8,6,1024]{2,1,0:T(8,128)(2,1)}), bf16[8,6,1024]{2,1,0:T(8,128)(2,1)S(1)}, u32[]{:S(2)}, u32[]{:S(2)}) async-start(bf16[8,6,1024]{2,1,0:T(8,128)(2,1)} %reshape.58), calls=%async_computation.4 | async-start | bytes 262144 | tf_op jit(solution)/shard_map/all_to_all | solution.py:225
  178.8 5.2 %all-to-all-done.4 = bf16[8,6,1024]{2,1,0:T(8,128)(2,1)S(1)} async-done(((bf16[8,6,1024]{2,1,0:T(8,128)(2,1)}), bf16[8,6,1024]{2,1,0:T(8,128)(2,1)S(1)}, u32[]{:S(2)}, u32[]{:S(2)}) %all-to-all-start.4) | async-done | bytes 98336 | tf_op jit(solution)/shard_map/all_to_all | solution.py:225
  184.1 0.6 gather_fusion
  185.1 2.0 %fusion.3 = bf16[16,1024]{1,0:T(8,128)(2,1)} fusion(f32[1,16,1024]{2,0,1:T(1,128)S(1)} %fusion, f32[16,1024]{1,0:T(8,128)S(1)} %multiply_reduce_fusion, f32[]{:T(128)} %bitcast, bf16[16,4096]{1,0:T(8,128)(2,1)} %param.9, s32[]{:T(128)S(6)} %select_n.53), kind=kLoop, calls=%fused_computation.19 | loop fusion | flops 81920 | bytes 196616 | tf_op jit(solution)/shard_map/convert_element_type | solution.py:236
  (42 shorter events, 2.4 us)
Async XLA Ops:
  0.0 152.7 %copy-start = (bf16[8,16,1024]{2,1,0:T(8,128)(2,1)S(1)}, bf16[8,16,1024]{2,1,0:T(8,128)(2,1)}, u32[]{:S(2)}) copy-start(bf16[8,16,1024]{2,1,0:T(8,128)(2,1)} %param.15) | copy-start | bytes 786436
  35.8 12.8 %copy-start.5 = (bf16[1,4096,128]{2,1,0:T(8,128)(2,1)S(1)}, bf16[1,4096,128]{2,1,0:T(8,128)(2,1)}, u32[]{:S(2)}) copy-start(bf16[1,4096,128]{2,1,0:T(8,128)(2,1)} %param.13) | copy-start | bytes 3145732
  35.8 43.5 %all-to-all-start = ((bf16[8,96,1024]{2,1,0:T(8,128)(2,1)}), bf16[8,96,1024]{2,1,0:T(8,128)(2,1)S(1)}, u32[]{:S(2)}, u32[]{:S(2)}) async-start(bf16[8,96,1024]{2,1,0:T(8,128)(2,1)} %packed_rows.1), calls=%async_computation | async-start | bytes 3145728 | tf_op jit(solution)/shard_map/all_to_all | solution.py:216
  50.0 16.9 %collective-permute-start.2 = (bf16[1024,256]{1,0:T(8,128)(2,1)S(1)}, bf16[1024,256]{1,0:T(8,128)(2,1)S(1)}, u32[]{:S(2)}, u32[]{:S(2)}) collective-permute-start(bf16[1024,256]{1,0:T(8,128)(2,1)S(1)} %pad_maximum_fusion.3), channel_id=1, source_target_pairs={{0,2},{1,3},{2,0},{3,1},{4,6},{5,7},{6,4},{7,5},{8,10},{9,11},{10,... | collective-permute-start | bytes 1572872 | tf_op jit(solution)/shard_map/ppermute | solution.py:97
  54.7 23.5 %collective-permute-start.1 = (bf16[1024,256]{1,0:T(8,128)(2,1)S(1)}, bf16[1024,256]{1,0:T(8,128)(2,1)S(1)}, u32[]{:S(2)}, u32[]{:S(2)}) collective-permute-start(bf16[1024,256]{1,0:T(8,128)(2,1)S(1)} %pad_maximum_fusion.2), channel_id=1, source_target_pairs={{0,3},{1,0},{2,1},{3,2},{4,7},{5,4},{6,5},{7,6},{8,11},{9,8},{10,9... | collective-permute-start | bytes 1572872 | tf_op jit(solution)/shard_map/ppermute | solution.py:97
  57.6 20.9 %collective-permute-start = (bf16[1024,256]{1,0:T(8,128)(2,1)S(1)}, bf16[1024,256]{1,0:T(8,128)(2,1)S(1)}, u32[]{:S(2)}, u32[]{:S(2)}) collective-permute-start(bf16[1024,256]{1,0:T(8,128)(2,1)S(1)} %pad_maximum_fusion.1), channel_id=1, source_target_pairs={{0,1},{1,2},{2,3},{3,0},{4,5},{5,6},{6,7},{7,4},{8,9},{9,10},{10,1... | collective-permute-start | bytes 1572872 | tf_op jit(solution)/shard_map/ppermute | solution.py:97
  78.5 0.8 copy-start.2
  79.3 1.0 copy-start.3
  105.7 13.3 %copy-start.1 = (bf16[1,512,1024]{2,1,0:T(8,128)(2,1)S(1)}, bf16[1,512,1024]{2,1,0:T(8,128)(2,1)}, u32[]{:S(2)}) copy-start(bf16[1,512,1024]{2,1,0:T(8,128)(2,1)} %param.14) | copy-start | bytes 3145732
  106.0 37.8 %copy-start.4 = (bf16[192,192]{1,0:T(8,128)(2,1)S(1)}, bf16[192,192]{1,0:T(8,128)(2,1)}, u32[]{:S(2)}) copy-start(bf16[192,192]{1,0:T(8,128)(2,1)} %constant.82.clone.moved_ref) | copy-start | bytes 221188
  120.0 11.0 %collective-permute-start.3 = (bf16[192,1024]{1,0:T(8,128)(2,1)S(1)}, bf16[192,1024]{1,0:T(8,128)(2,1)S(1)}, u32[]{:S(2)}, u32[]{:S(2)}) collective-permute-start(bf16[192,1024]{1,0:T(8,128)(2,1)S(1)} %get-tuple-element.10), channel_id=1, source_target_pairs={{0,4},{4,8},{8,12},{12,16},{16,20},{20,24},{24,28},{28,32},{32,36}... | collective-permute-start | bytes 1179656 | tf_op jit(solution)/shard_map/ppermute | solution.py:31
  121.9 10.4 %collective-permute-start.4 = (bf16[192,1024]{1,0:T(8,128)(2,1)S(1)}, bf16[192,1024]{1,0:T(8,128)(2,1)S(1)}, u32[]{:S(2)}, u32[]{:S(2)}) collective-permute-start(bf16[192,1024]{1,0:T(8,128)(2,1)S(1)} %get-tuple-element.11), channel_id=1, source_target_pairs={{0,60},{4,0},{8,4},{12,8},{16,12},{20,16},{24,20},{28,24},{32,28},... | collective-permute-start | bytes 1179656 | tf_op jit(solution)/shard_map/ppermute | solution.py:31
  126.5 17.3 %collective-permute-start.5 = (bf16[192,1024]{1,0:T(8,128)(2,1)S(1)}, bf16[192,1024]{1,0:T(8,128)(2,1)S(1)}, u32[]{:S(2)}, u32[]{:S(2)}) collective-permute-start(bf16[192,1024]{1,0:T(8,128)(2,1)S(1)} %get-tuple-element.12), channel_id=1, source_target_pairs={{0,8},{4,12},{8,16},{12,20},{16,24},{20,28},{24,32},{28,36},{32,40... | collective-permute-start | bytes 1179656 | tf_op jit(solution)/shard_map/ppermute | solution.py:31
  143.9 7.4 %copy-start.6 = (s32[16,2]{0,1:T(2,128)S(1)}, s32[16,2]{0,1:T(2,128)}, u32[]{:S(2)}) copy-start(s32[16,2]{0,1:T(2,128)} %param.10) | copy-start | bytes 388
  143.9 7.9 %copy-start.7 = (f32[16,2]{0,1:T(2,128)S(1)}, f32[16,2]{0,1:T(2,128)}, u32[]{:S(2)}) copy-start(f32[16,2]{0,1:T(2,128)} %param.11) | copy-start | bytes 388
  143.9 8.0 %copy-start.8 = (f32[9]{0:T(128)S(1)}, f32[9]{0:T(128)}, u32[]{:S(2)}) copy-start(f32[9]{0:T(128)} %param.16) | copy-start | bytes 112
  145.0 27.9 %all-to-all-start.3 = ((bf16[4,48,1024]{2,1,0:T(8,128)(2,1)}), bf16[4,48,1024]{2,1,0:T(8,128)(2,1)S(1)}, u32[]{:S(2)}, u32[]{:S(2)}) async-start(bf16[4,48,1024]{2,1,0:T(8,128)(2,1)} %summed_by_block.1), calls=%async_computation.3 | async-start | bytes 786432 | tf_op jit(solution)/shard_map/all_to_all | solution.py:223
  173.6 10.5 %all-to-all-start.4 = ((bf16[8,6,1024]{2,1,0:T(8,128)(2,1)}), bf16[8,6,1024]{2,1,0:T(8,128)(2,1)S(1)}, u32[]{:S(2)}, u32[]{:S(2)}) async-start(bf16[8,6,1024]{2,1,0:T(8,128)(2,1)} %reshape.58), calls=%async_computation.4 | async-start | bytes 262144 | tf_op jit(solution)/shard_map/all_to_all | solution.py:225

commit v5 on v2

v5 whole, which is shorter than its diff:
```python
import jax
import jax.numpy as jnp
import numpy as np
from jax import lax
from jax.experimental import pallas as pl
from jax.experimental.pallas import tpu as pltpu
from jax.sharding import PartitionSpec as P

RADIX = 4
LANES = 128
LIMIT = pltpu.CompilerParams(vmem_limit_bytes=16 * 2**20)
SMEM = pl.BlockSpec(memory_space=pltpu.SMEM)
VMEM = pl.BlockSpec(memory_space=pltpu.VMEM)


def far_groups():
    experts, count = lax.axis_size("expert"), lax.axis_size("dp")
    stride = count // RADIX
    return [
        [expert * count + low + stride * high for expert in range(experts) for high in range(RADIX)]
        for low in range(stride)
    ]


def far_exchange(chunks):
    return lax.all_to_all(chunks, ("expert", "dp"), 0, 0, tiled=True, axis_index_groups=far_groups())


def shifted(shard, even_shift, odd_shift):
    experts, count = lax.axis_size("expert"), lax.axis_size("dp")
    pairs = []
    for expert in range(experts):
        shift = odd_shift if expert % 2 else even_shift
        for place in range(count):
            pairs.append((expert * count + place, expert * count + (place + shift) % count))
    return lax.ppermute(shard, ("expert", "dp"), pairs)


def from_neighbours(shard):
    return [shifted(shard, 1, 1), shifted(shard, -1, -1), shifted(shard, 2, -2)]


def to_neighbours(shards):
    below, above, second = shards
    return [shifted(below, -1, -1), shifted(above, 1, 1), shifted(second, -2, 2)]


def call(kernel, name, out_shape, *operands, in_specs=None):
    many = isinstance(out_shape, list)
    return pl.pallas_call(
        kernel,
        out_shape=out_shape,
        in_specs=in_specs or [VMEM] * len(operands),
        out_specs=[VMEM] * len(out_shape) if many else VMEM,
        compiler_params=LIMIT,
        name=name,
    )(*operands)


def assigned_slots(ids, experts, tok_rows):
    choices, lanes = ids.shape
    expert = lax.broadcasted_iota(jnp.int32, (experts, lanes), 0)
    chosen = [ids[place : place + 1, :] == expert for place in range(choices)]
    named = sum(mask.astype(jnp.float32) for mask in chosen)
    source = lax.broadcasted_iota(jnp.int32, (lanes, lanes), 0)
    token = lax.broadcasted_iota(jnp.int32, (lanes, lanes), 1) % tok_rows
    before = (source < token).astype(jnp.float32)
    earlier = jnp.dot(named, before, preferred_element_type=jnp.float32)
    return [jnp.where(mask, earlier, -1.0) for mask in chosen]


def placed(slots, values, capacity, tok_rows):
    experts, lanes = slots[0].shape
    blocks = lanes // tok_rows
    shape = (capacity * blocks, lanes)
    row = lax.broadcasted_iota(jnp.int32, shape, 0)
    column = lax.broadcasted_iota(jnp.int32, shape, 1)
    same_block = row % blocks == column // tok_rows
    slot = (row // blocks).astype(jnp.float32)
    pieces = []
    for expert in range(experts):
        piece = jnp.zeros(shape, jnp.float32)
        for found, value in zip(slots, values):
            piece += jnp.where(same_block & (found[expert : expert + 1, :] == slot), value, 0.0)
        pieces.append(piece)
    return jnp.concatenate(pieces, axis=0)


def packed_rows(ids, own_columns, experts, capacity):
    tok_rows, features = own_columns.shape
    blocks = features // LANES

    def kernel(ids_ref, in_ref, out_ref):
        slots = assigned_slots(ids_ref[...], experts, tok_rows)
        chosen = placed(slots, [1.0] * len(slots), capacity, tok_rows).astype(jnp.bfloat16)
        tall = [in_ref[:, block * LANES : (block + 1) * LANES] for block in range(blocks)]
        out = jnp.dot(chosen, jnp.concatenate(tall, axis=0), preferred_element_type=jnp.float32)
        out = out.astype(out_ref.dtype)
        height = capacity * blocks
        for expert in range(experts):
            for far in range(RADIX):
                out_ref[expert * RADIX + far] = out[expert * height : (expert + 1) * height]

    shape = jax.ShapeDtypeStruct((experts * RADIX, capacity * blocks, LANES), own_columns.dtype)
    return call(kernel, "packed_rows", shape, ids, own_columns)


def chunk_order(chunks, capacity, blocks):
    count = chunks * capacity * blocks
    order = np.arange(count).reshape(chunks, capacity, blocks).transpose(2, 0, 1).reshape(-1)
    return np.eye(count, dtype=np.float32)[order]


def wide_rows(chunks, order, capacity):
    count, height, _ = chunks.shape
    blocks = height // capacity
    together = order.shape[0] // height
    rows = together * capacity

    def kernel(order_ref, in_ref, out_ref):
        for group in range(count // together):
            tall = in_ref[group * together : (group + 1) * together].reshape(together * height, LANES)
            out = jnp.dot(order_ref[...], tall, preferred_element_type=jnp.float32).astype(out_ref.dtype)
            for block in range(blocks):
                piece = out[block * rows : (block + 1) * rows]
                out_ref[group * rows : (group + 1) * rows, block * LANES : (block + 1) * LANES] = piece

    shape = jax.ShapeDtypeStruct((count * capacity, blocks * LANES), chunks.dtype)
    return call(kernel, "wide_rows", shape, order, chunks)


def summed_chunks(own, others, order, capacity):
    total_rows, features = own.shape
    blocks = features // LANES
    height = capacity * blocks
    together = order.shape[0] // height
    rows = together * capacity

    def kernel(order_ref, own_ref, *refs):
        other_refs, out_ref = refs[:-1], refs[-1]
        total = own_ref[...]
        for ref in other_refs:
            total += ref[...].astype(jnp.float32)
        total = total.astype(out_ref.dtype)
        for group in range(total_rows // rows):
            part = total[group * rows : (group + 1) * rows]
            tall = [part[:, block * LANES : (block + 1) * LANES] for block in range(blocks)]
            out = jnp.dot(order_ref[...], jnp.concatenate(tall, axis=0), preferred_element_type=jnp.float32)
            out = out.astype(out_ref.dtype).reshape(together, height, LANES)
            out_ref[group * together : (group + 1) * together] = out

    shape = jax.ShapeDtypeStruct((total_rows // capacity, height, LANES), jnp.bfloat16)
    return call(kernel, "summed_chunks", shape, order, own, *others)


def gate_up_parts(sets, weights):
    parts, _, width = weights.shape
    set_rows = sets[0].shape[0]
    rows = set_rows * len(sets)

    def kernel(*refs):
        set_refs, (w_ref, out_ref) = refs[: len(sets)], refs[len(sets) :]
        stacked = jnp.concatenate([ref[...] for ref in set_refs], axis=0)
        for part in range(parts):
            out = jnp.dot(stacked, w_ref[part], preferred_element_type=jnp.float32)
            out_ref[part] = out.astype(out_ref.dtype)

    shape = jax.ShapeDtypeStruct((parts, rows, width), jnp.bfloat16)
    return call(kernel, "gate_up_parts", shape, *sets, weights)


def hidden_copies(parts):
    count, rows, both = parts.shape
    width = both // 2

    def kernel(in_ref, out_ref):
        total = in_ref[0].astype(jnp.float32)
        for part in range(1, count):
            total += in_ref[part].astype(jnp.float32)
        gate, up = total[:, :width], total[:, width:]
        hidden = (gate / (1.0 + jnp.exp(-gate)) * up).astype(out_ref.dtype)
        for part in range(count):
            out_ref[part] = hidden

    return call(kernel, "hidden_copies", jax.ShapeDtypeStruct((count, rows, width), jnp.bfloat16), parts)


def down_sets(hidden, w_down, count):
    parts, rows, _ = hidden.shape
    set_rows = rows // count
    features = w_down.shape[1]

    def kernel(hidden_ref, w_ref, *out_refs):
        wide = jnp.concatenate([hidden_ref[part] for part in range(parts)], axis=1)
        out = jnp.dot(wide, w_ref[...], preferred_element_type=jnp.float32)
        for place, ref in enumerate(out_refs):
            ref[...] = out[place * set_rows : (place + 1) * set_rows].astype(ref.dtype)

    shapes = [
        jax.ShapeDtypeStruct((set_rows, features), jnp.bfloat16 if place else jnp.float32)
        for place in range(count)
    ]
    return call(kernel, "down_sets", shapes, hidden, w_down)


def mixed_layers(returned, ids, route, own_columns, past_layers, dwa_weight, experts, capacity):
    tok_rows, features = own_columns.shape
    blocks = features // LANES
    height = capacity * blocks
    depth = past_layers.shape[0]

    def kernel(dwa_ref, ids_ref, route_ref, own_ref, past_ref, in_ref, out_ref):
        outs = []
        for expert in range(experts):
            total = in_ref[expert * RADIX].astype(jnp.float32)
            for far in range(1, RADIX):
                total += in_ref[expert * RADIX + far].astype(jnp.float32)
            outs.append(total.astype(jnp.bfloat16))
        outs = jnp.concatenate(outs, axis=0)
        slots = assigned_slots(ids_ref[...], experts, tok_rows)
        route = route_ref[...]
        total = sum(route[place : place + 1, :] for place in range(len(slots)))
        shares = [route[place : place + 1, :] / total for place in range(len(slots))]
        rest = placed(slots, shares, capacity, tok_rows)
        mix = jnp.zeros((blocks * tok_rows, LANES), jnp.float32)
        for _ in range(3):
            term = rest.astype(jnp.bfloat16)
            rest = rest - term.astype(jnp.float32)
            mix += lax.dot_general(term, outs, (((0,), (0,)), ((), ())), preferred_element_type=jnp.float32)
        for block in range(blocks):
            lanes = slice(block * LANES, (block + 1) * LANES)
            current = own_ref[:, lanes].astype(jnp.float32) + mix[block * tok_rows : (block + 1) * tok_rows]
            value = dwa_ref[depth] * current
            for layer in range(depth):
                value += dwa_ref[layer] * past_ref[layer, :, lanes].astype(jnp.float32)
            out_ref[:, lanes] = value.astype(out_ref.dtype)

    return call(
        kernel,
        "mixed_layers",
        jax.ShapeDtypeStruct((tok_rows, features), own_columns.dtype),
        dwa_weight,
        ids,
        route,
        own_columns,
        past_layers,
        returned,
        in_specs=[SMEM] + [VMEM] * 5,
    )


def per_device(
    tokens, expert_ids, route_weight, gate_weight, up_weight, down_weight, past_layers, dwa_weight
):
    experts = lax.axis_size("expert")
    parts = lax.axis_size("tensor")
    tok_rows, feature_width = tokens.shape
    chosen_count = expert_ids.shape[1]
    capacity = min(tok_rows, 3 * chosen_count * tok_rows // (2 * experts))
    quarter = feature_width // parts
    blocks = quarter // LANES
    together = 2 * RADIX
    order = chunk_order(together, capacity, blocks)
    ids = jnp.tile(expert_ids.T, (1, blocks))
    route = jnp.tile(route_weight.T, (1, blocks))
    first_column = lax.axis_index("tensor") * quarter
    own_columns = lax.dynamic_slice_in_dim(tokens, first_column, quarter, 1)

    slabs = [w.reshape(parts, quarter, -1) for w in (gate_weight, up_weight)]
    weights = lax.all_to_all(jnp.concatenate(slabs, axis=2), "tensor", 0, 0, tiled=True)

    arrived = far_exchange(packed_rows(ids, own_columns, experts, capacity))
    own_set = wide_rows(arrived, jnp.asarray(order, jnp.bfloat16), capacity)
    sets = [own_set, *from_neighbours(own_set)]
    partial = lax.all_to_all(gate_up_parts(sets, weights), "tensor", 0, 0, tiled=True)
    hidden = lax.all_to_all(hidden_copies(partial), "tensor", 0, 0, tiled=True)
    own, *others = down_sets(hidden, down_weight[0], len(sets))
    summed = summed_chunks(own, to_neighbours(others), jnp.asarray(order.T, jnp.bfloat16), capacity)
    returned = far_exchange(summed)
    return mixed_layers(
        returned, ids, route, own_columns, past_layers, dwa_weight, experts, capacity
    )


def solution(mesh):
    return jax.shard_map(
        per_device,
        mesh=mesh,
        in_specs=(
            P(("expert", "dp"), None),
            P(("expert", "dp"), None),
            P(("expert", "dp"), None),
            P("expert", None, ("dp", "tensor")),
            P("expert", None, ("dp", "tensor")),
            P("expert", "dp", "tensor"),
            P(None, ("expert", "dp"), "tensor"),
            P(),
        ),
        out_specs=P(("expert", "dp"), "tensor"),
        check_vma=False,
    )
```

time: 204 us -> 182 us (0.89)
  blocking collectives: 54.1 us -> 35.3 us
  starting transfers between devices: 49.3 us -> 56.9 us
  other arithmetic: 6.5 us -> 3.11 us
  local copies, waits for them, and re-layouts: 4.34 us -> 1.04 us
  Pallas kernels: 11.2 us -> 8.43 us
    all_to_all x2 -> x1, blocking collectives: 39.1 us -> 22.2 us  [per_device(): lax.all_to_all(gate_up_parts(sets, weights), 'tensor', 0, 0, tiled=True)]
    ppermute x6, starting transfers between devices: 21.6 us -> 26.8 us  [shifted(): return lax.ppermute(shard, ('expert', 'dp'), pairs)]
    convert_element_type x3 -> x0, other arithmetic: 4.27 us -> none  [the longest x1 2.12 us: per_device(): own = own.astype(jnp.bfloat16).reshape(RADIX, block, quarter)]
    pallas_call x3 -> x7, Pallas kernels: 11.2 us -> 8.43 us  [call(): pl.pallas_call(kernel, out_shape=out_shape, in_specs=in_specs or [VMEM] *...]
    all_to_all x3 -> x2, starting transfers between devices: 23.7 us -> 26.1 us  [far_exchange(): lax.all_to_all(chunks, ('expert', 'dp'), 0, 0, tiled=True, axis_index_gro...]
    ppermute x6, waiting for transfers between devices: 18.9 us -> 20.9 us  [shifted(): return lax.ppermute(shard, ('expert', 'dp'), pairs)]
    all_to_all x3 -> x2, waiting for transfers between devices: 45.4 us -> 43.3 us  [far_exchange(): lax.all_to_all(chunks, ('expert', 'dp'), 0, 0, tiled=True, axis_index_gro...]
  transfers between devices with their start and end apart: 10 -> 9, of which waited for: 8 -> 7; matrix products, arithmetic and copies ran while one was open for 1% -> 2% of each run, Pallas kernels for 0% -> 0%
where the time goes in v5:
time: 182 us; the launch traced here: 180 us
  waiting for transfers between devices  74.7 us (41%)
  starting transfers between devices  56.9 us (31%)
  blocking collectives  35.3 us (19%)
  Pallas kernels  8.43 us (5%)
  other arithmetic  3.11 us (2%)
    all_to_all x2, waiting for transfers between devices, far_exchange(): lax.all_to_all(chunks, ('expert', 'dp'), 0, 0, tiled=True, axis_index_gro...  43.3 us
    ppermute x6, starting transfers between devices, shifted(): return lax.ppermute(shard, ('expert', 'dp'), pairs)  26.8 us
    all_to_all x2, starting transfers between devices, far_exchange(): lax.all_to_all(chunks, ('expert', 'dp'), 0, 0, tiled=True, axis_index_gro...  26.1 us
    all_to_all x1, blocking collectives, per_device(): lax.all_to_all(gate_up_parts(sets, weights), 'tensor', 0, 0, tiled=True)  22.2 us
    ppermute x6, waiting for transfers between devices, shifted(): return lax.ppermute(shard, ('expert', 'dp'), pairs)  20.9 us
    all_to_all x1, blocking collectives, per_device(): hidden = lax.all_to_all(hidden_copies(partial), 'tensor', 0, 0, tiled=True)  13.1 us
    all_to_all x1, waiting for transfers between devices, per_device(): lax.all_to_all(jnp.concatenate(slabs, axis=2), 'tensor', 0, 0, tiled=True)  10.4 us
    pallas_call x7, Pallas kernels, call(): pl.pallas_call(kernel, out_shape=out_shape, in_specs=in_specs or [VMEM] *...  8.43 us
  transfers between devices with their start and end apart: 9, of which 7 were waited for; matrix products, arithmetic and copies ran while one was open for 2% of the time, Pallas kernels for 0%

profile of v5, /device:TPU:1, one launch (start us, length us, event | category | flops | bytes accessed | tf_op | source)
XLA Modules:
  0.0 179.6 jit_solution(4873518581092457324)
XLA Ops:
  0.0 0.7 tile.8
  0.7 0.1 tile.9.ids_ref
  0.8 0.1 copy-done
  0.9 1.0 packed_rows.1
  2.0 19.4 %all-to-all-start = ((bf16[32,48,128]{2,1,0:T(8,128)(2,1)}), bf16[32,48,128]{2,1,0:T(8,128)(2,1)S(1)}, u32[]{:S(2)}, u32[]{:S(2)}) async-start(bf16[32,48,128]{2,1,0:T(8,128)(2,1)} %packed_rows.1), calls=%async_computation | async-start | bytes 786432 | tf_op jit(solution)/shard_map/all_to_all | solution.py:26
  21.3 3.1 %pad_maximum_fusion = bf16[4,1024,256]{2,1,0:T(8,128)(2,1)} fusion(bf16[4,1024,128]{2,1,0:T(8,128)(2,1)} %bitcast.6, bf16[4,1024,128]{2,1,0:T(8,128)(2,1)} %bitcast.7), kind=kLoop, calls=%fused_computation | loop fusion | flops 4194304 | bytes 4194304 | tf_op jit(solution)/shard_map/concatenate | solution.py:270
  24.5 19.5 %all-to-all-done.in_ref = bf16[32,48,128]{2,1,0:T(8,128)(2,1)S(1)} async-done(((bf16[32,48,128]{2,1,0:T(8,128)(2,1)}), bf16[32,48,128]{2,1,0:T(8,128)(2,1)S(1)}, u32[]{:S(2)}, u32[]{:S(2)}) %all-to-all-start) | async-done | bytes 393248 | tf_op jit(solution)/shard_map/all_to_all | solution.py:26
  44.0 4.0 %all-to-all-start.1 = ((bf16[4,1024,256]{2,1,0:T(8,128)(2,1)}), bf16[4,1024,256]{2,1,0:T(8,128)(2,1)S(1)}, u32[]{:S(2)}, u32[]{:S(2)}) async-start(bf16[4,1024,256]{2,1,0:T(8,128)(2,1)} %pad_maximum_fusion), calls=%async_computation.1 | async-start | bytes 4194304 | tf_op jit(solution)/shard_map/all_to_all | solution.py:270
  48.0 0.5 wide_rows.1.refs_0_
  48.5 9.0 %collective-permute-start = (bf16[192,1024]{1,0:T(8,128)(2,1)S(1)}, bf16[192,1024]{1,0:T(8,128)(2,1)S(1)}, u32[]{:S(2)}, u32[]{:S(2)}) collective-permute-start(bf16[192,1024]{1,0:T(8,128)(2,1)S(1)} %wide_rows.1.refs_0_), channel_id=1, source_target_pairs={{0,4},{4,8},{8,12},{12,16},{16,20},{20,24},{24,28},{28,32},{32,36}... | collective-permute-start | bytes 1179656 | tf_op jit(solution)/shard_map/ppermute | solution.py:36
  57.5 1.9 %collective-permute-start.1 = (bf16[192,1024]{1,0:T(8,128)(2,1)S(1)}, bf16[192,1024]{1,0:T(8,128)(2,1)S(1)}, u32[]{:S(2)}, u32[]{:S(2)}) collective-permute-start(bf16[192,1024]{1,0:T(8,128)(2,1)S(1)} %wide_rows.1.refs_0_), channel_id=1, source_target_pairs={{0,60},{4,0},{8,4},{12,8},{16,12},{20,16},{24,20},{28,24},{32,28},... | collective-permute-start | bytes 1179656 | tf_op jit(solution)/shard_map/ppermute | solution.py:36
  59.4 2.9 %collective-permute-start.2 = (bf16[192,1024]{1,0:T(8,128)(2,1)S(1)}, bf16[192,1024]{1,0:T(8,128)(2,1)}, u32[]{:S(2)}, u32[]{:S(2)}) collective-permute-start(bf16[192,1024]{1,0:T(8,128)(2,1)S(1)} %wide_rows.1.refs_0_), channel_id=1, source_target_pairs={{0,8},{4,12},{8,16},{12,20},{16,24},{20,28},{24,32},{28,36},{32,40... | collective-permute-start | bytes 1179656 | tf_op jit(solution)/shard_map/ppermute | solution.py:36
  62.4 10.4 %all-to-all-done.1.refs_4_ = bf16[4,1024,256]{2,1,0:T(8,128)(2,1)S(1)} async-done(((bf16[4,1024,256]{2,1,0:T(8,128)(2,1)}), bf16[4,1024,256]{2,1,0:T(8,128)(2,1)S(1)}, u32[]{:S(2)}, u32[]{:S(2)}) %all-to-all-start.1) | async-done | bytes 2097184 | tf_op jit(solution)/shard_map/all_to_all | solution.py:270
  72.8 5.6 %collective-permute-done.2.refs_3_ = bf16[192,1024]{1,0:T(8,128)(2,1)} collective-permute-done((bf16[192,1024]{1,0:T(8,128)(2,1)S(1)}, bf16[192,1024]{1,0:T(8,128)(2,1)}, u32[]{:S(2)}, u32[]{:S(2)}) %collective-permute-start.2) | collective-permute-done | bytes 393248 | tf_op jit(solution)/shard_map/ppermute | solution.py:36
  78.4 2.8 %gate_up_parts.1 = bf16[4,768,256]{2,1,0:T(8,128)(2,1)S(1)} custom-call(bf16[192,1024]{1,0:T(8,128)(2,1)S(1)} %wide_rows.1.refs_0_, bf16[192,1024]{1,0:T(8,128)(2,1)S(1)} %collective-permute-done.refs_1_, bf16[192,1024]{1,0:T(8,128)(2,1)S(1)} %collective-permute-done.1.refs_2_, bf16[192,1024]{1,0:T(8,128)(2,1)} %collective-permute-done.2.refs_3_, ...), custom_call_target="tpu_custom_call" | custom-call | tf_op jit(solution)/shard_map/gate_up_parts/pallas_call | solution.py:50
  81.2 22.2 %all_to_all.25.in_ref = bf16[4,768,256]{2,1,0:T(8,128)(2,1)S(1)} all-to-all(bf16[4,768,256]{2,1,0:T(8,128)(2,1)S(1)} %gate_up_parts.1), channel_id=1, replica_groups=mesh['expert'=8,'dp'=16,'tensor'=4] {'tensor'}, dimensions={0} | all-to-all | bytes 3145728 | tf_op jit(solution)/shard_map/all_to_all | solution.py:275
  103.4 0.3 hidden_copies.1
  103.7 0.0 copy-start.2
  103.7 13.1 %all_to_all.26.hidden_ref = bf16[4,768,128]{2,1,0:T(8,128)(2,1)S(1)} all-to-all(bf16[4,768,128]{2,1,0:T(8,128)(2,1)S(1)} %hidden_copies.1), channel_id=1, replica_groups=mesh['expert'=8,'dp'=16,'tensor'=4] {'tensor'}, dimensions={0} | all-to-all | bytes 1572864 | tf_op jit(solution)/shard_map/all_to_all | solution.py:276
  116.8 1.0 down_sets.1
  117.8 0.0 copy-start.6
  117.8 3.5 %collective-permute-start.3 = (bf16[192,1024]{1,0:T(8,128)(2,1)S(1)}, bf16[192,1024]{1,0:T(8,128)(2,1)S(1)}, u32[]{:S(2)}, u32[]{:S(2)}) collective-permute-start(bf16[192,1024]{1,0:T(8,128)(2,1)S(1)} %get-tuple-element.10), channel_id=1, source_target_pairs={{0,60},{4,0},{8,4},{12,8},{16,12},{20,16},{24,20},{28,24},{32,28},... | collective-permute-start | bytes 1179656 | tf_op jit(solution)/shard_map/ppermute | solution.py:36
  121.3 4.6 %collective-permute-start.4 = (bf16[192,1024]{1,0:T(8,128)(2,1)S(1)}, bf16[192,1024]{1,0:T(8,128)(2,1)S(1)}, u32[]{:S(2)}, u32[]{:S(2)}) collective-permute-start(bf16[192,1024]{1,0:T(8,128)(2,1)S(1)} %get-tuple-element.11), channel_id=1, source_target_pairs={{0,4},{4,8},{8,12},{12,16},{16,20},{20,24},{24,28},{28,32},{32,36}... | collective-permute-start | bytes 1179656 | tf_op jit(solution)/shard_map/ppermute | solution.py:36
  125.9 4.8 %collective-permute-start.5 = (bf16[192,1024]{1,0:T(8,128)(2,1)S(1)}, bf16[192,1024]{1,0:T(8,128)(2,1)S(1)}, u32[]{:S(2)}, u32[]{:S(2)}) collective-permute-start(bf16[192,1024]{1,0:T(8,128)(2,1)S(1)} %get-tuple-element.12), channel_id=1, source_target_pairs={{0,56},{4,60},{8,0},{12,4},{16,8},{20,12},{24,16},{28,20},{32,24},... | collective-permute-start | bytes 1179656 | tf_op jit(solution)/shard_map/ppermute | solution.py:36
  130.8 0.8 collective-permute-done.3.refs_0_
  131.6 2.8 %collective-permute-done.4.refs_1_ = bf16[192,1024]{1,0:T(8,128)(2,1)S(1)} collective-permute-done((bf16[192,1024]{1,0:T(8,128)(2,1)S(1)}, bf16[192,1024]{1,0:T(8,128)(2,1)S(1)}, u32[]{:S(2)}, u32[]{:S(2)}) %collective-permute-start.4) | collective-permute-done | bytes 393248 | tf_op jit(solution)/shard_map/ppermute | solution.py:36
  134.3 11.8 %collective-permute-done.5.refs_2_ = bf16[192,1024]{1,0:T(8,128)(2,1)S(1)} collective-permute-done((bf16[192,1024]{1,0:T(8,128)(2,1)S(1)}, bf16[192,1024]{1,0:T(8,128)(2,1)S(1)}, u32[]{:S(2)}, u32[]{:S(2)}) %collective-permute-start.5) | collective-permute-done | bytes 393248 | tf_op jit(solution)/shard_map/ppermute | solution.py:36
  146.1 1.2 summed_chunks.1
  147.3 6.7 %all-to-all-start.4 = ((bf16[32,48,128]{2,1,0:T(8,128)(2,1)}), bf16[32,48,128]{2,1,0:T(8,128)(2,1)S(1)}, u32[]{:S(2)}, u32[]{:S(2)}) async-start(bf16[32,48,128]{2,1,0:T(8,128)(2,1)} %summed_chunks.1), calls=%async_computation.4 | async-start | bytes 786432 | tf_op jit(solution)/shard_map/all_to_all | solution.py:26
  154.1 0.1 tile.21.route_ref
  154.1 23.8 %all-to-all-done.4.in_ref = bf16[32,48,128]{2,1,0:T(8,128)(2,1)S(1)} async-done(((bf16[32,48,128]{2,1,0:T(8,128)(2,1)}), bf16[32,48,128]{2,1,0:T(8,128)(2,1)S(1)}, u32[]{:S(2)}, u32[]{:S(2)}) %all-to-all-start.4) | async-done | bytes 393248 | tf_op jit(solution)/shard_map/all_to_all | solution.py:26
  177.9 1.6 mixed_layers.1
  (15 shorter events, 0.0 us)
Async XLA Ops:
  0.0 0.9 copy-start
  2.0 42.0 %all-to-all-start = ((bf16[32,48,128]{2,1,0:T(8,128)(2,1)}), bf16[32,48,128]{2,1,0:T(8,128)(2,1)S(1)}, u32[]{:S(2)}, u32[]{:S(2)}) async-start(bf16[32,48,128]{2,1,0:T(8,128)(2,1)} %packed_rows.1), calls=%async_computation | async-start | bytes 786432 | tf_op jit(solution)/shard_map/all_to_all | solution.py:26
  24.5 23.5 %copy-start.3 = (bf16[384,384]{1,0:T(8,128)(2,1)S(1)}, bf16[384,384]{1,0:T(8,128)(2,1)}, u32[]{:S(2)}) copy-start(bf16[384,384]{1,0:T(8,128)(2,1)} %constant.14.clone.order_ref) | copy-start | bytes 884740
  44.0 28.9 %all-to-all-start.1 = ((bf16[4,1024,256]{2,1,0:T(8,128)(2,1)}), bf16[4,1024,256]{2,1,0:T(8,128)(2,1)S(1)}, u32[]{:S(2)}, u32[]{:S(2)}) async-start(bf16[4,1024,256]{2,1,0:T(8,128)(2,1)} %pad_maximum_fusion), calls=%async_computation.1 | async-start | bytes 4194304 | tf_op jit(solution)/shard_map/all_to_all | solution.py:270
  48.5 24.4 %collective-permute-start = (bf16[192,1024]{1,0:T(8,128)(2,1)S(1)}, bf16[192,1024]{1,0:T(8,128)(2,1)S(1)}, u32[]{:S(2)}, u32[]{:S(2)}) collective-permute-start(bf16[192,1024]{1,0:T(8,128)(2,1)S(1)} %wide_rows.1.refs_0_), channel_id=1, source_target_pairs={{0,4},{4,8},{8,12},{12,16},{16,20},{20,24},{24,28},{28,32},{32,36}... | collective-permute-start | bytes 1179656 | tf_op jit(solution)/shard_map/ppermute | solution.py:36
  57.5 15.3 %collective-permute-start.1 = (bf16[192,1024]{1,0:T(8,128)(2,1)S(1)}, bf16[192,1024]{1,0:T(8,128)(2,1)S(1)}, u32[]{:S(2)}, u32[]{:S(2)}) collective-permute-start(bf16[192,1024]{1,0:T(8,128)(2,1)S(1)} %wide_rows.1.refs_0_), channel_id=1, source_target_pairs={{0,60},{4,0},{8,4},{12,8},{16,12},{20,16},{24,20},{28,24},{32,28},... | collective-permute-start | bytes 1179656 | tf_op jit(solution)/shard_map/ppermute | solution.py:36
  59.4 19.0 %collective-permute-start.2 = (bf16[192,1024]{1,0:T(8,128)(2,1)S(1)}, bf16[192,1024]{1,0:T(8,128)(2,1)}, u32[]{:S(2)}, u32[]{:S(2)}) collective-permute-start(bf16[192,1024]{1,0:T(8,128)(2,1)S(1)} %wide_rows.1.refs_0_), channel_id=1, source_target_pairs={{0,8},{4,12},{8,16},{12,20},{16,24},{20,28},{24,32},{28,36},{32,40... | collective-permute-start | bytes 1179656 | tf_op jit(solution)/shard_map/ppermute | solution.py:36
  103.4 13.4 %copy-start.1 = (bf16[1,512,1024]{2,1,0:T(8,128)(2,1)S(1)}, bf16[1,512,1024]{2,1,0:T(8,128)(2,1)}, u32[]{:S(2)}) copy-start(bf16[1,512,1024]{2,1,0:T(8,128)(2,1)} %param.15) | copy-start | bytes 3145732
  103.7 42.4 %copy-start.2 = (bf16[384,384]{1,0:T(8,128)(2,1)S(1)}, bf16[384,384]{1,0:T(8,128)(2,1)}, u32[]{:S(2)}) copy-start(bf16[384,384]{1,0:T(8,128)(2,1)} %constant.15.clone.order_ref) | copy-start | bytes 884740
  117.8 36.2 %copy-start.6 = (f32[16,2]{0,1:T(2,128)S(1)}, f32[16,2]{0,1:T(2,128)}, u32[]{:S(2)}) copy-start(f32[16,2]{0,1:T(2,128)} %param.12) | copy-start | bytes 388
  117.8 60.1 %copy-start.4 = (bf16[8,16,1024]{2,1,0:T(8,128)(2,1)S(1)}, bf16[8,16,1024]{2,1,0:T(8,128)(2,1)}, u32[]{:S(2)}) copy-start(bf16[8,16,1024]{2,1,0:T(8,128)(2,1)} %past_ref.1) | copy-start | bytes 786436
  117.8 60.1 %copy-start.5 = (f32[9]{0:T(128)S(1)}, f32[9]{0:T(128)}, u32[]{:S(2)}) copy-start(f32[9]{0:T(128)} %dwa_ref.1) | copy-start | bytes 112
  117.8 13.7 %collective-permute-start.3 = (bf16[192,1024]{1,0:T(8,128)(2,1)S(1)}, bf16[192,1024]{1,0:T(8,128)(2,1)S(1)}, u32[]{:S(2)}, u32[]{:S(2)}) collective-permute-start(bf16[192,1024]{1,0:T(8,128)(2,1)S(1)} %get-tuple-element.10), channel_id=1, source_target_pairs={{0,60},{4,0},{8,4},{12,8},{16,12},{20,16},{24,20},{28,24},{32,28},... | collective-permute-start | bytes 1179656 | tf_op jit(solution)/shard_map/ppermute | solution.py:36
  121.3 13.0 %collective-permute-start.4 = (bf16[192,1024]{1,0:T(8,128)(2,1)S(1)}, bf16[192,1024]{1,0:T(8,128)(2,1)S(1)}, u32[]{:S(2)}, u32[]{:S(2)}) collective-permute-start(bf16[192,1024]{1,0:T(8,128)(2,1)S(1)} %get-tuple-element.11), channel_id=1, source_target_pairs={{0,4},{4,8},{8,12},{12,16},{16,20},{20,24},{24,28},{28,32},{32,36}... | collective-permute-start | bytes 1179656 | tf_op jit(solution)/shard_map/ppermute | solution.py:36
  125.9 20.2 %collective-permute-start.5 = (bf16[192,1024]{1,0:T(8,128)(2,1)S(1)}, bf16[192,1024]{1,0:T(8,128)(2,1)S(1)}, u32[]{:S(2)}, u32[]{:S(2)}) collective-permute-start(bf16[192,1024]{1,0:T(8,128)(2,1)S(1)} %get-tuple-element.12), channel_id=1, source_target_pairs={{0,56},{4,60},{8,0},{12,4},{16,8},{20,12},{24,16},{28,20},{32,24},... | collective-permute-start | bytes 1179656 | tf_op jit(solution)/shard_map/ppermute | solution.py:36
  147.3 30.6 %all-to-all-start.4 = ((bf16[32,48,128]{2,1,0:T(8,128)(2,1)}), bf16[32,48,128]{2,1,0:T(8,128)(2,1)S(1)}, u32[]{:S(2)}, u32[]{:S(2)}) async-start(bf16[32,48,128]{2,1,0:T(8,128)(2,1)} %summed_chunks.1), calls=%async_computation.4 | async-start | bytes 786432 | tf_op jit(solution)/shard_map/all_to_all | solution.py:26

commit v6 on v5

--- a/solution.py
+++ b/solution.py
@@ -8,6 +8,7 @@
 
 RADIX = 4
 LANES = 128
+SHIFTS = (0, 1, 3, 2)
 LIMIT = pltpu.CompilerParams(vmem_limit_bytes=16 * 2**20)
 SMEM = pl.BlockSpec(memory_space=pltpu.SMEM)
 VMEM = pl.BlockSpec(memory_space=pltpu.VMEM)
@@ -57,9 +58,18 @@
     )(*operands)
 
 
+def repeated_ids(ids):
+    tok_rows = ids.shape[1]
+    token = lax.broadcasted_iota(jnp.int32, (tok_rows, LANES), 0)
+    lane = lax.broadcasted_iota(jnp.int32, (tok_rows, LANES), 1)
+    spread = (lane % tok_rows == token).astype(jnp.float32)
+    return jnp.dot(ids.astype(jnp.float32), spread, preferred_element_type=jnp.float32)
+
+
 def assigned_slots(ids, experts, tok_rows):
+    ids = repeated_ids(ids)
     choices, lanes = ids.shape
-    expert = lax.broadcasted_iota(jnp.int32, (experts, lanes), 0)
+    expert = lax.broadcasted_iota(jnp.int32, (experts, lanes), 0).astype(jnp.float32)
     chosen = [ids[place : place + 1, :] == expert for place in range(choices)]
     named = sum(mask.astype(jnp.float32) for mask in chosen)
     source = lax.broadcasted_iota(jnp.int32, (lanes, lanes), 0)
@@ -153,23 +163,42 @@
     return call(kernel, "summed_chunks", shape, order, own, *others)
 
 
-def gate_up_parts(sets, weights):
-    parts, _, width = weights.shape
+def weights_by_features(gate_weight, up_weight, quarter):
+    parts = lax.axis_size("tensor")
+    here = lax.axis_index("tensor")
+    slabs = [w.reshape(parts, quarter, -1) for w in (gate_weight, up_weight)]
+
+    def slab(shift):
+        place = (here + shift) % parts
+        both = [lax.dynamic_index_in_dim(w, place, 0, keepdims=False) for w in slabs]
+        both = jnp.concatenate(both, axis=1)
+        if shift == 0:
+            return both
+        return lax.ppermute(both, "tensor", [(i, (i + shift) % parts) for i in range(parts)])
+
+    return [slab(shift) for shift in SHIFTS]
+
+
+def gate_up_parts(sets, weights, place):
+    parts = len(weights)
+    width = weights[0].shape[1]
     set_rows = sets[0].shape[0]
     rows = set_rows * len(sets)
 
-    def kernel(*refs):
-        set_refs, (w_ref, out_ref) = refs[: len(sets)], refs[len(sets) :]
+    def kernel(place_ref, *refs):
+        set_refs, w_refs, out_ref = refs[: len(sets)], refs[len(sets) : -1], refs[-1]
         stacked = jnp.concatenate([ref[...] for ref in set_refs], axis=0)
-        for part in range(parts):
-            out = jnp.dot(stacked, w_ref[part], preferred_element_type=jnp.float32)
+        for shift, w_ref in zip(SHIFTS, w_refs):
+            part = (place_ref[0] + (parts - shift)) % parts
+            out = jnp.dot(stacked, w_ref[...], preferred_element_type=jnp.float32)
             out_ref[part] = out.astype(out_ref.dtype)
 
     shape = jax.ShapeDtypeStruct((parts, rows, width), jnp.bfloat16)
-    return call(kernel, "gate_up_parts", shape, *sets, weights)
-
-
-def hidden_copies(parts):
+    specs = [SMEM] + [VMEM] * (len(sets) + parts)
+    return call(kernel, "gate_up_parts", shape, place, *sets, *weights, in_specs=specs)
+
+
+def hidden_units(parts):
     count, rows, both = parts.shape
     width = both // 2
 
@@ -178,11 +207,9 @@
         for part in range(1, count):
             total += in_ref[part].astype(jnp.float32)
         gate, up = total[:, :width], total[:, width:]
-        hidden = (gate / (1.0 + jnp.exp(-gate)) * up).astype(out_ref.dtype)
-        for part in range(count):
-            out_ref[part] = hidden
-
-    return call(kernel, "hidden_copies", jax.ShapeDtypeStruct((count, rows, width), jnp.bfloat16), parts)
+        out_ref[...] = (gate / (1.0 + jnp.exp(-gate)) * up).astype(out_ref.dtype)
+
+    return call(kernel, "hidden_units", jax.ShapeDtypeStruct((rows, width), jnp.bfloat16), parts)
 
 
 def down_sets(hidden, w_down, count):
@@ -261,19 +288,18 @@
     blocks = quarter // LANES
     together = 2 * RADIX
     order = chunk_order(together, capacity, blocks)
-    ids = jnp.tile(expert_ids.T, (1, blocks))
+    ids = expert_ids.T
     route = jnp.tile(route_weight.T, (1, blocks))
     first_column = lax.axis_index("tensor") * quarter
     own_columns = lax.dynamic_slice_in_dim(tokens, first_column, quarter, 1)
 
-    slabs = [w.reshape(parts, quarter, -1) for w in (gate_weight, up_weight)]
-    weights = lax.all_to_all(jnp.concatenate(slabs, axis=2), "tensor", 0, 0, tiled=True)
-
+    weights = weights_by_features(gate_weight, up_weight, quarter)
+    place = lax.axis_index("tensor").reshape(1)
     arrived = far_exchange(packed_rows(ids, own_columns, experts, capacity))
     own_set = wide_rows(arrived, jnp.asarray(order, jnp.bfloat16), capacity)
     sets = [own_set, *from_neighbours(own_set)]
-    partial = lax.all_to_all(gate_up_parts(sets, weights), "tensor", 0, 0, tiled=True)
-    hidden = lax.all_to_all(hidden_copies(partial), "tensor", 0, 0, tiled=True)
+    partial = lax.all_to_all(gate_up_parts(sets, weights, place), "tensor", 0, 0, tiled=True)
+    hidden = lax.all_gather(hidden_units(partial), "tensor", axis=0, tiled=False)
     own, *others = down_sets(hidden, down_weight[0], len(sets))
     summed = summed_chunks(own, to_neighbours(others), jnp.asarray(order.T, jnp.bfloat16), capacity)
     returned = far_exchange(summed)

time: 182 us -> 175 us (0.962)
  waiting for transfers between devices: 74.7 us -> 65.5 us
  starting transfers between devices: 56.9 us -> 62.6 us
  local copies, waits for them, and re-layouts: 1.04 us -> 3.04 us
  blocking collectives: 35.3 us -> 33.3 us
    all_to_all x2 -> x1, blocking collectives: 35.3 us -> 21.8 us  [per_device(): lax.all_to_all(gate_up_parts(sets, weights, place), 'tensor', 0, 0, tiled...]
    all_gather x0 -> x1, blocking collectives: none -> 11.5 us  [per_device(): lax.all_gather(hidden_units(partial), 'tensor', axis=0, tiled=False)]
    all_to_all x1 -> x0, waiting for transfers between devices: 10.4 us -> none  [per_device(): lax.all_to_all(jnp.concatenate(slabs, axis=2), 'tensor', 0, 0, tiled=True)]
    ppermute x0 -> x3, starting transfers between devices: none -> 9.91 us  [slab(): lax.ppermute(both, 'tensor', [(i, (i + shift) % parts) for i in range(par...]
    ppermute x6, waiting for transfers between devices: 20.9 us -> 29.9 us  [shifted(): return lax.ppermute(shard, ('expert', 'dp'), pairs)]
    all_to_all x2, waiting for transfers between devices: 43.3 us -> 35.6 us  [far_exchange(): lax.all_to_all(chunks, ('expert', 'dp'), 0, 0, tiled=True, axis_index_gro...]
    all_to_all x1 -> x0, starting transfers between devices: 4.01 us -> none  [per_device(): lax.all_to_all(jnp.concatenate(slabs, axis=2), 'tensor', 0, 0, tiled=True)]
    ppermute x6, starting transfers between devices: 26.8 us -> 24.5 us  [shifted(): return lax.ppermute(shard, ('expert', 'dp'), pairs)]
  transfers between devices with their start and end apart: 9 -> 11, of which waited for: 7 -> 8; matrix products, arithmetic and copies ran while one was open for 2% -> 2% of each run, Pallas kernels for 0% -> 0%
where the time goes in v6:
time: 175 us; the launch traced here: 174 us
  waiting for transfers between devices  65.5 us (37%)
  starting transfers between devices  62.6 us (36%)
  blocking collectives  33.3 us (19%)
  Pallas kernels  7.75 us (4%)
  local copies, waits for them, and re-layouts  3.04 us (2%)
  other arithmetic  1.85 us (1%)
    all_to_all x2, waiting for transfers between devices, far_exchange(): lax.all_to_all(chunks, ('expert', 'dp'), 0, 0, tiled=True, axis_index_gro...  35.6 us
    ppermute x6, waiting for transfers between devices, shifted(): return lax.ppermute(shard, ('expert', 'dp'), pairs)  29.9 us
    all_to_all x2, starting transfers between devices, far_exchange(): lax.all_to_all(chunks, ('expert', 'dp'), 0, 0, tiled=True, axis_index_gro...  28.2 us
    ppermute x6, starting transfers between devices, shifted(): return lax.ppermute(shard, ('expert', 'dp'), pairs)  24.5 us
    all_to_all x1, blocking collectives, per_device(): lax.all_to_all(gate_up_parts(sets, weights, place), 'tensor', 0, 0, tiled...  21.8 us
    all_gather x1, blocking collectives, per_device(): lax.all_gather(hidden_units(partial), 'tensor', axis=0, tiled=False)  11.5 us
    ppermute x3, starting transfers between devices, slab(): lax.ppermute(both, 'tensor', [(i, (i + shift) % parts) for i in range(par...  9.91 us
    pallas_call x7, Pallas kernels, call(): pl.pallas_call(kernel, out_shape=out_shape, in_specs=in_specs or [VMEM] *...  7.75 us
  transfers between devices with their start and end apart: 11, of which 8 were waited for; matrix products, arithmetic and copies ran while one was open for 2% of the time, Pallas kernels for 0%

profile of v6, /device:TPU:1, one launch (start us, length us, event | category | flops | bytes accessed | tf_op | source)
XLA Modules:
  0.0 174.2 jit_solution(1130420061431553338)
XLA Ops:
  0.0 0.9 copy-done
  0.9 0.7 copy-done.5
  1.6 1.2 packed_rows.1
  2.8 19.4 %all-to-all-start = ((bf16[32,48,128]{2,1,0:T(8,128)(2,1)}), bf16[32,48,128]{2,1,0:T(8,128)(2,1)S(1)}, u32[]{:S(2)}, u32[]{:S(2)}) async-start(bf16[32,48,128]{2,1,0:T(8,128)(2,1)} %packed_rows.1), calls=%async_computation | async-start | bytes 786432 | tf_op jit(solution)/shard_map/all_to_all | solution.py:27
  22.2 1.3 dynamic-slice_bitcast_fusion
  23.6 0.9 pad_maximum_fusion.3
  24.4 4.6 %collective-permute-start.5 = (bf16[1024,256]{1,0:T(8,128)(2,1)}, bf16[1024,256]{1,0:T(8,128)(2,1)S(1)}, u32[]{:S(2)}, u32[]{:S(2)}) collective-permute-start(bf16[1024,256]{1,0:T(8,128)(2,1)} %pad_maximum_fusion.3), channel_id=1, source_target_pairs={{0,2},{1,3},{2,0},{3,1},{4,6},{5,7},{6,4},{7,5},{8,10},{9,11},{10,... | collective-permute-start | bytes 1572872 | tf_op jit(solution)/shard_map/ppermute | solution.py:177
  29.1 2.8 %collective-permute-start.4 = (bf16[1024,256]{1,0:T(8,128)(2,1)S(1)}, bf16[1024,256]{1,0:T(8,128)(2,1)S(1)}, u32[]{:S(2)}, u32[]{:S(2)}) collective-permute-start(bf16[1024,256]{1,0:T(8,128)(2,1)S(1)} %pad_maximum_fusion.2), channel_id=1, source_target_pairs={{0,3},{1,0},{2,1},{3,2},{4,7},{5,4},{6,5},{7,6},{8,11},{9,8},{10,9... | collective-permute-start | bytes 1572872 | tf_op jit(solution)/shard_map/ppermute | solution.py:177
  31.9 0.9 pad_maximum_fusion.1
  32.8 2.5 %collective-permute-start.3 = (bf16[1024,256]{1,0:T(8,128)(2,1)}, bf16[1024,256]{1,0:T(8,128)(2,1)S(1)}, u32[]{:S(2)}, u32[]{:S(2)}) collective-permute-start(bf16[1024,256]{1,0:T(8,128)(2,1)} %pad_maximum_fusion.1), channel_id=1, source_target_pairs={{0,1},{1,2},{2,3},{3,0},{4,5},{5,6},{6,7},{7,4},{8,9},{9,10},{10,1... | collective-permute-start | bytes 1572872 | tf_op jit(solution)/shard_map/ppermute | solution.py:177
  35.3 9.5 %all-to-all-done.in_ref = bf16[32,48,128]{2,1,0:T(8,128)(2,1)S(1)} async-done(((bf16[32,48,128]{2,1,0:T(8,128)(2,1)}), bf16[32,48,128]{2,1,0:T(8,128)(2,1)S(1)}, u32[]{:S(2)}, u32[]{:S(2)}) %all-to-all-start) | async-done | bytes 393248 | tf_op jit(solution)/shard_map/all_to_all | solution.py:27
  44.8 0.5 wide_rows.1.refs_0_
  45.3 9.0 %collective-permute-start = (bf16[192,1024]{1,0:T(8,128)(2,1)S(1)}, bf16[192,1024]{1,0:T(8,128)(2,1)S(1)}, u32[]{:S(2)}, u32[]{:S(2)}) collective-permute-start(bf16[192,1024]{1,0:T(8,128)(2,1)S(1)} %wide_rows.1.refs_0_), channel_id=1, source_target_pairs={{0,4},{4,8},{8,12},{12,16},{16,20},{20,24},{24,28},{28,32},{32,36}... | collective-permute-start | bytes 1179656 | tf_op jit(solution)/shard_map/ppermute | solution.py:37
  54.3 1.9 %collective-permute-start.1 = (bf16[192,1024]{1,0:T(8,128)(2,1)S(1)}, bf16[192,1024]{1,0:T(8,128)(2,1)S(1)}, u32[]{:S(2)}, u32[]{:S(2)}) collective-permute-start(bf16[192,1024]{1,0:T(8,128)(2,1)S(1)} %wide_rows.1.refs_0_), channel_id=1, source_target_pairs={{0,60},{4,0},{8,4},{12,8},{16,12},{20,16},{24,20},{28,24},{32,28},... | collective-permute-start | bytes 1179656 | tf_op jit(solution)/shard_map/ppermute | solution.py:37
  56.2 2.9 %collective-permute-start.2 = (bf16[192,1024]{1,0:T(8,128)(2,1)S(1)}, bf16[192,1024]{1,0:T(8,128)(2,1)S(1)}, u32[]{:S(2)}, u32[]{:S(2)}) collective-permute-start(bf16[192,1024]{1,0:T(8,128)(2,1)S(1)} %wide_rows.1.refs_0_), channel_id=1, source_target_pairs={{0,8},{4,12},{8,16},{12,20},{16,24},{20,28},{24,32},{28,36},{32,40... | collective-permute-start | bytes 1179656 | tf_op jit(solution)/shard_map/ppermute | solution.py:37
  59.3 4.8 %collective-permute-done.refs_1_ = bf16[192,1024]{1,0:T(8,128)(2,1)S(1)} collective-permute-done((bf16[192,1024]{1,0:T(8,128)(2,1)S(1)}, bf16[192,1024]{1,0:T(8,128)(2,1)S(1)}, u32[]{:S(2)}, u32[]{:S(2)}) %collective-permute-start) | collective-permute-done | bytes 393248 | tf_op jit(solution)/shard_map/ppermute | solution.py:37
  64.1 2.5 %collective-permute-done.1.refs_2_ = bf16[192,1024]{1,0:T(8,128)(2,1)S(1)} collective-permute-done((bf16[192,1024]{1,0:T(8,128)(2,1)S(1)}, bf16[192,1024]{1,0:T(8,128)(2,1)S(1)}, u32[]{:S(2)}, u32[]{:S(2)}) %collective-permute-start.1) | collective-permute-done | bytes 393248 | tf_op jit(solution)/shard_map/ppermute | solution.py:37
  66.6 8.3 %collective-permute-done.2.refs_3_ = bf16[192,1024]{1,0:T(8,128)(2,1)S(1)} collective-permute-done((bf16[192,1024]{1,0:T(8,128)(2,1)S(1)}, bf16[192,1024]{1,0:T(8,128)(2,1)S(1)}, u32[]{:S(2)}, u32[]{:S(2)}) %collective-permute-start.2) | collective-permute-done | bytes 393248 | tf_op jit(solution)/shard_map/ppermute | solution.py:37
  74.8 1.9 %gate_up_parts.1 = bf16[4,768,256]{2,1,0:T(8,128)(2,1)S(1)} custom-call(s32[1]{0:T(128)} %bitcast.2.place_ref, bf16[192,1024]{1,0:T(8,128)(2,1)S(1)} %wide_rows.1.refs_0_, bf16[192,1024]{1,0:T(8,128)(2,1)S(1)} %collective-permute-done.refs_1_, bf16[192,1024]{1,0:T(8,128)(2,1)S(1)} %collective-permute-done.1.refs_2_, ...), custom_call_target="tpu_custom_call" | custom-call | tf_op jit(solution)/shard_map/gate_up_parts/pallas_call | solution.py:51
  76.7 21.8 %all_to_all.15.in_ref = bf16[4,768,256]{2,1,0:T(8,128)(2,1)S(1)} all-to-all(bf16[4,768,256]{2,1,0:T(8,128)(2,1)S(1)} %gate_up_parts.1), channel_id=1, replica_groups=mesh['expert'=8,'dp'=16,'tensor'=4] {'tensor'}, dimensions={0} | all-to-all | bytes 3145728 | tf_op jit(solution)/shard_map/all_to_all | solution.py:301
  98.8 11.5 %all-gather = bf16[3072,128]{1,0:T(8,128)(2,1)S(1)} all-gather(bf16[768,128]{1,0:T(8,128)(2,1)S(1)} %hidden_units.1), channel_id=2, replica_groups=mesh['expert'=8,'dp'=16,'tensor'=4] {'tensor'}, dimensions={0}, use_global_device_ids=true | all-gather | bytes 983040 | tf_op jit(solution)/shard_map/all_gather | solution.py:302
  110.3 1.0 down_sets.1
  111.3 2.8 %collective-permute-start.6 = (bf16[192,1024]{1,0:T(8,128)(2,1)S(1)}, bf16[192,1024]{1,0:T(8,128)(2,1)S(1)}, u32[]{:S(2)}, u32[]{:S(2)}) collective-permute-start(bf16[192,1024]{1,0:T(8,128)(2,1)S(1)} %get-tuple-element.10), channel_id=1, source_target_pairs={{0,60},{4,0},{8,4},{12,8},{16,12},{20,16},{24,20},{28,24},{32,28},... | collective-permute-start | bytes 1179656 | tf_op jit(solution)/shard_map/ppermute | solution.py:37
  114.1 2.5 %collective-permute-start.7 = (bf16[192,1024]{1,0:T(8,128)(2,1)S(1)}, bf16[192,1024]{1,0:T(8,128)(2,1)S(1)}, u32[]{:S(2)}, u32[]{:S(2)}) collective-permute-start(bf16[192,1024]{1,0:T(8,128)(2,1)S(1)} %get-tuple-element.11), channel_id=1, source_target_pairs={{0,4},{4,8},{8,12},{12,16},{16,20},{20,24},{24,28},{28,32},{32,36}... | collective-permute-start | bytes 1179656 | tf_op jit(solution)/shard_map/ppermute | solution.py:37
  116.6 5.3 %collective-permute-start.8 = (bf16[192,1024]{1,0:T(8,128)(2,1)S(1)}, bf16[192,1024]{1,0:T(8,128)(2,1)S(1)}, u32[]{:S(2)}, u32[]{:S(2)}) collective-permute-start(bf16[192,1024]{1,0:T(8,128)(2,1)S(1)} %get-tuple-element.12), channel_id=1, source_target_pairs={{0,56},{4,60},{8,0},{12,4},{16,8},{20,12},{24,16},{28,20},{32,24},... | collective-permute-start | bytes 1179656 | tf_op jit(solution)/shard_map/ppermute | solution.py:37
  121.9 0.4 collective-permute-done.6.refs_0_
  122.3 1.5 collective-permute-done.7.refs_1_
  123.8 12.4 %collective-permute-done.8.refs_2_ = bf16[192,1024]{1,0:T(8,128)(2,1)S(1)} collective-permute-done((bf16[192,1024]{1,0:T(8,128)(2,1)S(1)}, bf16[192,1024]{1,0:T(8,128)(2,1)S(1)}, u32[]{:S(2)}, u32[]{:S(2)}) %collective-permute-start.8) | collective-permute-done | bytes 393248 | tf_op jit(solution)/shard_map/ppermute | solution.py:37
  136.2 1.2 summed_chunks.1
  137.5 8.8 %all-to-all-start.2 = ((bf16[32,48,128]{2,1,0:T(8,128)(2,1)}), bf16[32,48,128]{2,1,0:T(8,128)(2,1)S(1)}, u32[]{:S(2)}, u32[]{:S(2)}) async-start(bf16[32,48,128]{2,1,0:T(8,128)(2,1)} %summed_chunks.1), calls=%async_computation.2 | async-start | bytes 786432 | tf_op jit(solution)/shard_map/all_to_all | solution.py:27
  146.4 26.1 %all-to-all-done.2.in_ref = bf16[32,48,128]{2,1,0:T(8,128)(2,1)S(1)} async-done(((bf16[32,48,128]{2,1,0:T(8,128)(2,1)}), bf16[32,48,128]{2,1,0:T(8,128)(2,1)S(1)}, u32[]{:S(2)}, u32[]{:S(2)}) %all-to-all-start.2) | async-done | bytes 393248 | tf_op jit(solution)/shard_map/all_to_all | solution.py:27
  172.5 1.8 %mixed_layers.1 = bf16[16,1024]{1,0:T(8,128)(2,1)} custom-call(f32[9]{0:T(128)S(1)} %copy-done.7, s32[2,16]{1,0:T(2,128)S(1)} %bitcast.26, f32[2,128]{1,0:T(2,128)S(1)} %tile.10.route_ref, bf16[16,1024]{1,0:T(8,128)(2,1)S(1)} %constant_dynamic-slice_fusion.in_ref.own_ref, bf16[8,16,1024]{2,1,0:T(8,128)(2,1)S(1)} %copy-done.4, ...), custom_call_target="tpu_custom_call" | custom-call | tf_op jit(solution)/shard_map/mixed_layers/pallas_call | solution.py:51
  (27 shorter events, 0.5 us)
Async XLA Ops:
  0.0 0.9 copy-start
  0.9 0.7 copy-start.5
  1.6 20.6 %copy-start.8 = (bf16[1,4096,128]{2,1,0:T(8,128)(2,1)S(1)}, bf16[1,4096,128]{2,1,0:T(8,128)(2,1)}, u32[]{:S(2)}) copy-start(bf16[1,4096,128]{2,1,0:T(8,128)(2,1)} %param.14) | copy-start | bytes 3145732
  2.8 42.0 %all-to-all-start = ((bf16[32,48,128]{2,1,0:T(8,128)(2,1)}), bf16[32,48,128]{2,1,0:T(8,128)(2,1)S(1)}, u32[]{:S(2)}, u32[]{:S(2)}) async-start(bf16[32,48,128]{2,1,0:T(8,128)(2,1)} %packed_rows.1), calls=%async_computation | async-start | bytes 786432 | tf_op jit(solution)/shard_map/all_to_all | solution.py:27
  23.5 21.2 %copy-start.3 = (bf16[384,384]{1,0:T(8,128)(2,1)S(1)}, bf16[384,384]{1,0:T(8,128)(2,1)}, u32[]{:S(2)}) copy-start(bf16[384,384]{1,0:T(8,128)(2,1)} %constant.61.clone.order_ref) | copy-start | bytes 884740
  24.4 31.8 %collective-permute-start.5 = (bf16[1024,256]{1,0:T(8,128)(2,1)}, bf16[1024,256]{1,0:T(8,128)(2,1)S(1)}, u32[]{:S(2)}, u32[]{:S(2)}) collective-permute-start(bf16[1024,256]{1,0:T(8,128)(2,1)} %pad_maximum_fusion.3), channel_id=1, source_target_pairs={{0,2},{1,3},{2,0},{3,1},{4,6},{5,7},{6,4},{7,5},{8,10},{9,11},{10,... | collective-permute-start | bytes 1572872 | tf_op jit(solution)/shard_map/ppermute | solution.py:177
  29.1 30.1 %collective-permute-start.4 = (bf16[1024,256]{1,0:T(8,128)(2,1)S(1)}, bf16[1024,256]{1,0:T(8,128)(2,1)S(1)}, u32[]{:S(2)}, u32[]{:S(2)}) collective-permute-start(bf16[1024,256]{1,0:T(8,128)(2,1)S(1)} %pad_maximum_fusion.2), channel_id=1, source_target_pairs={{0,3},{1,0},{2,1},{3,2},{4,7},{5,4},{6,5},{7,6},{8,11},{9,8},{10,9... | collective-permute-start | bytes 1572872 | tf_op jit(solution)/shard_map/ppermute | solution.py:177
  32.8 26.5 %collective-permute-start.3 = (bf16[1024,256]{1,0:T(8,128)(2,1)}, bf16[1024,256]{1,0:T(8,128)(2,1)S(1)}, u32[]{:S(2)}, u32[]{:S(2)}) collective-permute-start(bf16[1024,256]{1,0:T(8,128)(2,1)} %pad_maximum_fusion.1), channel_id=1, source_target_pairs={{0,1},{1,2},{2,3},{3,0},{4,5},{5,6},{6,7},{7,4},{8,9},{9,10},{10,1... | collective-permute-start | bytes 1572872 | tf_op jit(solution)/shard_map/ppermute | solution.py:177
  45.3 18.8 %collective-permute-start = (bf16[192,1024]{1,0:T(8,128)(2,1)S(1)}, bf16[192,1024]{1,0:T(8,128)(2,1)S(1)}, u32[]{:S(2)}, u32[]{:S(2)}) collective-permute-start(bf16[192,1024]{1,0:T(8,128)(2,1)S(1)} %wide_rows.1.refs_0_), channel_id=1, source_target_pairs={{0,4},{4,8},{8,12},{12,16},{16,20},{20,24},{24,28},{28,32},{32,36}... | collective-permute-start | bytes 1179656 | tf_op jit(solution)/shard_map/ppermute | solution.py:37
  54.3 12.3 %collective-permute-start.1 = (bf16[192,1024]{1,0:T(8,128)(2,1)S(1)}, bf16[192,1024]{1,0:T(8,128)(2,1)S(1)}, u32[]{:S(2)}, u32[]{:S(2)}) collective-permute-start(bf16[192,1024]{1,0:T(8,128)(2,1)S(1)} %wide_rows.1.refs_0_), channel_id=1, source_target_pairs={{0,60},{4,0},{8,4},{12,8},{16,12},{20,16},{24,20},{28,24},{32,28},... | collective-permute-start | bytes 1179656 | tf_op jit(solution)/shard_map/ppermute | solution.py:37
  56.2 18.6 %collective-permute-start.2 = (bf16[192,1024]{1,0:T(8,128)(2,1)S(1)}, bf16[192,1024]{1,0:T(8,128)(2,1)S(1)}, u32[]{:S(2)}, u32[]{:S(2)}) collective-permute-start(bf16[192,1024]{1,0:T(8,128)(2,1)S(1)} %wide_rows.1.refs_0_), channel_id=1, source_target_pairs={{0,8},{4,12},{8,16},{12,20},{16,24},{20,28},{24,32},{28,36},{32,40... | collective-permute-start | bytes 1179656 | tf_op jit(solution)/shard_map/ppermute | solution.py:37
  98.5 11.8 %copy-start.1 = (bf16[1,512,1024]{2,1,0:T(8,128)(2,1)S(1)}, bf16[1,512,1024]{2,1,0:T(8,128)(2,1)}, u32[]{:S(2)}) copy-start(bf16[1,512,1024]{2,1,0:T(8,128)(2,1)} %param.15) | copy-start | bytes 3145732
  98.8 37.4 %copy-start.2 = (bf16[384,384]{1,0:T(8,128)(2,1)S(1)}, bf16[384,384]{1,0:T(8,128)(2,1)}, u32[]{:S(2)}) copy-start(bf16[384,384]{1,0:T(8,128)(2,1)} %constant.62.clone.order_ref) | copy-start | bytes 884740
  111.3 11.0 %collective-permute-start.6 = (bf16[192,1024]{1,0:T(8,128)(2,1)S(1)}, bf16[192,1024]{1,0:T(8,128)(2,1)S(1)}, u32[]{:S(2)}, u32[]{:S(2)}) collective-permute-start(bf16[192,1024]{1,0:T(8,128)(2,1)S(1)} %get-tuple-element.10), channel_id=1, source_target_pairs={{0,60},{4,0},{8,4},{12,8},{16,12},{20,16},{24,20},{28,24},{32,28},... | collective-permute-start | bytes 1179656 | tf_op jit(solution)/shard_map/ppermute | solution.py:37
  114.1 9.7 %collective-permute-start.7 = (bf16[192,1024]{1,0:T(8,128)(2,1)S(1)}, bf16[192,1024]{1,0:T(8,128)(2,1)S(1)}, u32[]{:S(2)}, u32[]{:S(2)}) collective-permute-start(bf16[192,1024]{1,0:T(8,128)(2,1)S(1)} %get-tuple-element.11), channel_id=1, source_target_pairs={{0,4},{4,8},{8,12},{12,16},{16,20},{20,24},{24,28},{28,32},{32,36}... | collective-permute-start | bytes 1179656 | tf_op jit(solution)/shard_map/ppermute | solution.py:37
  116.6 19.6 %collective-permute-start.8 = (bf16[192,1024]{1,0:T(8,128)(2,1)S(1)}, bf16[192,1024]{1,0:T(8,128)(2,1)S(1)}, u32[]{:S(2)}, u32[]{:S(2)}) collective-permute-start(bf16[192,1024]{1,0:T(8,128)(2,1)S(1)} %get-tuple-element.12), channel_id=1, source_target_pairs={{0,56},{4,60},{8,0},{12,4},{16,8},{20,12},{24,16},{28,20},{32,24},... | collective-permute-start | bytes 1179656 | tf_op jit(solution)/shard_map/ppermute | solution.py:37
  136.2 10.1 %copy-start.9 = (f32[16,2]{0,1:T(2,128)S(1)}, f32[16,2]{0,1:T(2,128)}, u32[]{:S(2)}) copy-start(f32[16,2]{0,1:T(2,128)} %param.12) | copy-start | bytes 388
  136.2 36.3 %copy-start.4 = (bf16[8,16,1024]{2,1,0:T(8,128)(2,1)S(1)}, bf16[8,16,1024]{2,1,0:T(8,128)(2,1)}, u32[]{:S(2)}) copy-start(bf16[8,16,1024]{2,1,0:T(8,128)(2,1)} %past_ref.1) | copy-start | bytes 786436
  136.2 36.3 %copy-start.6 = (s32[16,2]{0,1:T(2,128)S(1)}, s32[16,2]{0,1:T(2,128)}, u32[]{:S(2)}) copy-start(s32[16,2]{0,1:T(2,128)} %param.11) | copy-start | bytes 388
  136.2 36.3 %copy-start.7 = (f32[9]{0:T(128)S(1)}, f32[9]{0:T(128)}, u32[]{:S(2)}) copy-start(f32[9]{0:T(128)} %dwa_ref.1) | copy-start | bytes 112
  137.5 35.0 %all-to-all-start.2 = ((bf16[32,48,128]{2,1,0:T(8,128)(2,1)}), bf16[32,48,128]{2,1,0:T(8,128)(2,1)S(1)}, u32[]{:S(2)}, u32[]{:S(2)}) async-start(bf16[32,48,128]{2,1,0:T(8,128)(2,1)} %summed_chunks.1), calls=%async_computation.2 | async-start | bytes 786432 | tf_op jit(solution)/shard_map/all_to_all | solution.py:27

commit v7 on v6

--- a/solution.py
+++ b/solution.py
@@ -41,12 +41,11 @@
     return [shifted(shard, 1, 1), shifted(shard, -1, -1), shifted(shard, 2, -2)]
 
 
-def to_neighbours(shards):
-    below, above, second = shards
+def to_neighbours(below, above, second):
     return [shifted(below, -1, -1), shifted(above, 1, 1), shifted(second, -2, 2)]
 
 
-def call(kernel, name, out_shape, *operands, in_specs=None):
+def call(kernel, out_shape, *operands, in_specs=None):
     many = isinstance(out_shape, list)
     return pl.pallas_call(
         kernel,
@@ -54,7 +53,6 @@
         in_specs=in_specs or [VMEM] * len(operands),
         out_specs=[VMEM] * len(out_shape) if many else VMEM,
         compiler_params=LIMIT,
-        name=name,
     )(*operands)
 
 
@@ -112,7 +110,7 @@
                 out_ref[expert * RADIX + far] = out[expert * height : (expert + 1) * height]
 
     shape = jax.ShapeDtypeStruct((experts * RADIX, capacity * blocks, LANES), own_columns.dtype)
-    return call(kernel, "packed_rows", shape, ids, own_columns)
+    return call(kernel, shape, ids, own_columns)
 
 
 def chunk_order(chunks, capacity, blocks):
@@ -136,7 +134,7 @@
                 out_ref[group * rows : (group + 1) * rows, block * LANES : (block + 1) * LANES] = piece
 
     shape = jax.ShapeDtypeStruct((count * capacity, blocks * LANES), chunks.dtype)
-    return call(kernel, "wide_rows", shape, order, chunks)
+    return call(kernel, shape, order, chunks)
 
 
 def summed_chunks(own, others, order, capacity):
@@ -160,7 +158,7 @@
             out_ref[group * together : (group + 1) * together] = out
 
     shape = jax.ShapeDtypeStruct((total_rows // capacity, height, LANES), jnp.bfloat16)
-    return call(kernel, "summed_chunks", shape, order, own, *others)
+    return call(kernel, shape, order, own, *others)
 
 
 def weights_by_features(gate_weight, up_weight, quarter):
@@ -195,7 +193,7 @@
 
     shape = jax.ShapeDtypeStruct((parts, rows, width), jnp.bfloat16)
     specs = [SMEM] + [VMEM] * (len(sets) + parts)
-    return call(kernel, "gate_up_parts", shape, place, *sets, *weights, in_specs=specs)
+    return call(kernel, shape, place, *sets, *weights, in_specs=specs)
 
 
 def hidden_units(parts):
@@ -209,12 +207,12 @@
         gate, up = total[:, :width], total[:, width:]
         out_ref[...] = (gate / (1.0 + jnp.exp(-gate)) * up).astype(out_ref.dtype)
 
-    return call(kernel, "hidden_units", jax.ShapeDtypeStruct((rows, width), jnp.bfloat16), parts)
-
-
-def down_sets(hidden, w_down, count):
+    return call(kernel, jax.ShapeDtypeStruct((rows, width), jnp.bfloat16), parts)
+
+
+def down_sets(hidden, w_down, dtypes):
     parts, rows, _ = hidden.shape
-    set_rows = rows // count
+    set_rows = rows // len(dtypes)
     features = w_down.shape[1]
 
     def kernel(hidden_ref, w_ref, *out_refs):
@@ -223,17 +221,13 @@
         for place, ref in enumerate(out_refs):
             ref[...] = out[place * set_rows : (place + 1) * set_rows].astype(ref.dtype)
 
-    shapes = [
-        jax.ShapeDtypeStruct((set_rows, features), jnp.bfloat16 if place else jnp.float32)
-        for place in range(count)
-    ]
-    return call(kernel, "down_sets", shapes, hidden, w_down)
+    shapes = [jax.ShapeDtypeStruct((set_rows, features), dtype) for dtype in dtypes]
+    return call(kernel, shapes, hidden, w_down)
 
 
 def mixed_layers(returned, ids, route, own_columns, past_layers, dwa_weight, experts, capacity):
     tok_rows, features = own_columns.shape
     blocks = features // LANES
-    height = capacity * blocks
     depth = past_layers.shape[0]
 
     def kernel(dwa_ref, ids_ref, route_ref, own_ref, past_ref, in_ref, out_ref):
@@ -264,7 +258,6 @@
 
     return call(
         kernel,
-        "mixed_layers",
         jax.ShapeDtypeStruct((tok_rows, features), own_columns.dtype),
         dwa_weight,
         ids,
@@ -297,11 +290,23 @@
     place = lax.axis_index("tensor").reshape(1)
     arrived = far_exchange(packed_rows(ids, own_columns, experts, capacity))
     own_set = wide_rows(arrived, jnp.asarray(order, jnp.bfloat16), capacity)
-    sets = [own_set, *from_neighbours(own_set)]
-    partial = lax.all_to_all(gate_up_parts(sets, weights, place), "tensor", 0, 0, tiled=True)
-    hidden = lax.all_gather(hidden_units(partial), "tensor", axis=0, tiled=False)
-    own, *others = down_sets(hidden, down_weight[0], len(sets))
-    summed = summed_chunks(own, to_neighbours(others), jnp.asarray(order.T, jnp.bfloat16), capacity)
+    below, above, second = from_neighbours(own_set)
+
+    def hidden_part(sets):
+        partial = gate_up_parts(sets, weights, place)
+        return hidden_units(lax.all_to_all(partial, "tensor", 0, 0, tiled=True))
+
+    def outputs(hidden, dtypes):
+        wide = lax.all_gather(hidden, "tensor", axis=0, tiled=False)
+        return down_sets(wide, down_weight[0], dtypes)
+
+    near_hidden = hidden_part([own_set, below])
+    late_hidden = hidden_part([above, second])
+    above, second = outputs(late_hidden, [jnp.bfloat16] * 2)
+    near_hidden, above, second = lax.optimization_barrier((near_hidden, above, second))
+    own, below = outputs(near_hidden, [jnp.float32, jnp.bfloat16])
+    others = to_neighbours(below, above, second)
+    summed = summed_chunks(own, others, jnp.asarray(order.T, jnp.bfloat16), capacity)
     returned = far_exchange(summed)
     return mixed_layers(
         returned, ids, route, own_columns, past_layers, dwa_weight, experts, capacity

time: 175 us -> 187 us (1.069)
  starting transfers between devices: 62.6 us -> 69.3 us
  blocking collectives: 33.3 us -> 27.6 us
  waiting for transfers between devices: 65.5 us -> 70.8 us
  Pallas kernels: 7.75 us -> 9.93 us
    all_to_all x1 -> x0, blocking collectives: 21.8 us -> none  [per_device(): lax.all_to_all(gate_up_parts(sets, weights, place), 'tensor', 0, 0, tiled...]
    all_gather x1 -> x2, blocking collectives: 11.5 us -> 27.6 us  [outputs(): wide = lax.all_gather(hidden, 'tensor', axis=0, tiled=False)]
    all_to_all x0 -> x2, starting transfers between devices: none -> 8.52 us  [hidden_part(): return hidden_units(lax.all_to_all(partial, 'tensor', 0, 0, tiled=True))]
    ppermute x6, waiting for transfers between devices: 29.9 us -> 37.4 us  [shifted(): return lax.ppermute(shard, ('expert', 'dp'), pairs)]
    ppermute x6, starting transfers between devices: 24.5 us -> 21.4 us  [shifted(): return lax.ppermute(shard, ('expert', 'dp'), pairs)]
    pallas_call x7 -> x10, Pallas kernels: 7.75 us -> 9.93 us  [call(): pl.pallas_call(kernel, out_shape=out_shape, in_specs=in_specs or [VMEM] *...]
    all_to_all x2, waiting for transfers between devices: 35.6 us -> 33.4 us  [far_exchange(): lax.all_to_all(chunks, ('expert', 'dp'), 0, 0, tiled=True, axis_index_gro...]
  transfers between devices with their start and end apart: 11 -> 13, of which waited for: 8 -> 8; matrix products, arithmetic and copies ran while one was open for 2% -> 3% of each run, Pallas kernels for 0% -> 2%
where the time goes in v7:
time: 187 us; the launch traced here: 186 us
  waiting for transfers between devices  70.8 us (38%)
  starting transfers between devices  69.3 us (37%)
  blocking collectives  27.6 us (15%)
  Pallas kernels  9.93 us (5%)
  local copies, waits for them, and re-layouts  4.51 us (2%)
  other arithmetic  3.68 us (2%)
    ppermute x6, waiting for transfers between devices, shifted(): return lax.ppermute(shard, ('expert', 'dp'), pairs)  37.4 us
    all_to_all x2, waiting for transfers between devices, far_exchange(): lax.all_to_all(chunks, ('expert', 'dp'), 0, 0, tiled=True, axis_index_gro...  33.4 us
    all_to_all x2, starting transfers between devices, far_exchange(): lax.all_to_all(chunks, ('expert', 'dp'), 0, 0, tiled=True, axis_index_gro...  29.5 us
    all_gather x2, blocking collectives, outputs(): wide = lax.all_gather(hidden, 'tensor', axis=0, tiled=False)  27.6 us
    ppermute x6, starting transfers between devices, shifted(): return lax.ppermute(shard, ('expert', 'dp'), pairs)  21.4 us
    pallas_call x10, Pallas kernels, call(): pl.pallas_call(kernel, out_shape=out_shape, in_specs=in_specs or [VMEM] *...  9.93 us
    ppermute x3, starting transfers between devices, slab(): lax.ppermute(both, 'tensor', [(i, (i + shift) % parts) for i in range(par...  9.9 us
    all_to_all x2, starting transfers between devices, hidden_part(): return hidden_units(lax.all_to_all(partial, 'tensor', 0, 0, tiled=True))  8.52 us
  transfers between devices with their start and end apart: 13, of which 8 were waited for; matrix products, arithmetic and copies ran while one was open for 3% of the time, Pallas kernels for 2%

profile of v7, /device:TPU:1, one launch (start us, length us, event | category | flops | bytes accessed | tf_op | source)
XLA Modules:
  0.0 186.0 jit_solution(5463145560348441854)
XLA Ops:
  0.0 0.9 copy-done
  1.6 1.2 shard_map.100
  2.8 19.4 %all-to-all-start = ((bf16[32,48,128]{2,1,0:T(8,128)(2,1)}), bf16[32,48,128]{2,1,0:T(8,128)(2,1)S(1)}, u32[]{:S(2)}, u32[]{:S(2)}) async-start(bf16[32,48,128]{2,1,0:T(8,128)(2,1)} %shard_map.100), calls=%async_computation | async-start | bytes 786432 | tf_op jit(solution)/shard_map/all_to_all | solution.py:27
  22.2 2.1 %dynamic-slice_bitcast_fusion = (bf16[1024,128]{1,0:T(8,128)(2,1)S(1)}, bf16[1024,128]{1,0:T(8,128)(2,1)S(1)}, bf16[1024,128]{1,0:T(8,128)(2,1)S(1)}, bf16[1024,...) fusion(bf16[4,1024,128]{2,1,0:T(8,128)(2,1)S(1)} %bitcast.30, ...), kind=kLoop, calls=%fused_computation.4 | loop fusion | bytes 4194320 | tf_op jit(solution)/shard_map/jit(dynamic_index_in_dim)/squeeze | solution.py:171
  25.2 3.1 %collective-permute-start.1 = (bf16[1024,256]{1,0:T(8,128)(2,1)}, bf16[1024,256]{1,0:T(8,128)(2,1)S(1)}, u32[]{:S(2)}, u32[]{:S(2)}) collective-permute-start(bf16[1024,256]{1,0:T(8,128)(2,1)} %pad_maximum_fusion.1), channel_id=1, source_target_pairs={{0,1},{1,2},{2,3},{3,0},{4,5},{5,6},{6,7},{7,4},{8,9},{9,10},{10,1... | collective-permute-start | bytes 1572872 | tf_op jit(solution)/shard_map/ppermute | solution.py:175
  28.4 0.9 pad_maximum_fusion.2
  29.2 3.4 %collective-permute-start.2 = (bf16[1024,256]{1,0:T(8,128)(2,1)}, bf16[1024,256]{1,0:T(8,128)(2,1)S(1)}, u32[]{:S(2)}, u32[]{:S(2)}) collective-permute-start(bf16[1024,256]{1,0:T(8,128)(2,1)} %pad_maximum_fusion.2), channel_id=1, source_target_pairs={{0,3},{1,0},{2,1},{3,2},{4,7},{5,4},{6,5},{7,6},{8,11},{9,8},{10,9... | collective-permute-start | bytes 1572872 | tf_op jit(solution)/shard_map/ppermute | solution.py:175
  33.5 3.4 %collective-permute-start.3 = (bf16[1024,256]{1,0:T(8,128)(2,1)}, bf16[1024,256]{1,0:T(8,128)(2,1)S(1)}, u32[]{:S(2)}, u32[]{:S(2)}) collective-permute-start(bf16[1024,256]{1,0:T(8,128)(2,1)} %pad_maximum_fusion.3), channel_id=1, source_target_pairs={{0,2},{1,3},{2,0},{3,1},{4,6},{5,7},{6,4},{7,5},{8,10},{9,11},{10,... | collective-permute-start | bytes 1572872 | tf_op jit(solution)/shard_map/ppermute | solution.py:175
  36.9 7.9 %all-to-all-done.in_ref = bf16[32,48,128]{2,1,0:T(8,128)(2,1)S(1)} async-done(((bf16[32,48,128]{2,1,0:T(8,128)(2,1)}), bf16[32,48,128]{2,1,0:T(8,128)(2,1)S(1)}, u32[]{:S(2)}, u32[]{:S(2)}) %all-to-all-start) | async-done | bytes 393248 | tf_op jit(solution)/shard_map/all_to_all | solution.py:27
  45.3 7.0 %collective-permute-start.4 = (bf16[192,1024]{1,0:T(8,128)(2,1)S(1)}, bf16[192,1024]{1,0:T(8,128)(2,1)S(1)}, u32[]{:S(2)}, u32[]{:S(2)}) collective-permute-start(bf16[192,1024]{1,0:T(8,128)(2,1)S(1)} %shard_map.101.refs_0_), channel_id=1, source_target_pairs={{0,60},{4,0},{8,4},{12,8},{16,12},{20,16},{24,20},{28,24},{32,28},... | collective-permute-start | bytes 1179656 | tf_op jit(solution)/shard_map/ppermute | solution.py:37
  52.3 3.5 %collective-permute-start.5 = (bf16[192,1024]{1,0:T(8,128)(2,1)S(1)}, bf16[192,1024]{1,0:T(8,128)(2,1)S(1)}, u32[]{:S(2)}, u32[]{:S(2)}) collective-permute-start(bf16[192,1024]{1,0:T(8,128)(2,1)S(1)} %shard_map.101.refs_0_), channel_id=1, source_target_pairs={{0,8},{4,12},{8,16},{12,20},{16,24},{20,28},{24,32},{28,36},{32,40... | collective-permute-start | bytes 1179656 | tf_op jit(solution)/shard_map/ppermute | solution.py:37
  55.8 1.1 pad_maximum_fusion.refs_2_
  57.0 5.7 %collective-permute-done.4.refs_0_ = bf16[192,1024]{1,0:T(8,128)(2,1)S(1)} collective-permute-done((bf16[192,1024]{1,0:T(8,128)(2,1)S(1)}, bf16[192,1024]{1,0:T(8,128)(2,1)S(1)}, u32[]{:S(2)}, u32[]{:S(2)}) %collective-permute-start.4) | collective-permute-done | bytes 393248 | tf_op jit(solution)/shard_map/ppermute | solution.py:37
  62.7 8.2 %collective-permute-done.5.refs_1_ = bf16[192,1024]{1,0:T(8,128)(2,1)S(1)} collective-permute-done((bf16[192,1024]{1,0:T(8,128)(2,1)S(1)}, bf16[192,1024]{1,0:T(8,128)(2,1)S(1)}, u32[]{:S(2)}, u32[]{:S(2)}) %collective-permute-start.5) | collective-permute-done | bytes 393248 | tf_op jit(solution)/shard_map/ppermute | solution.py:37
  70.9 1.9 %shard_map.104 = bf16[4,384,256]{2,1,0:T(8,128)(2,1)} custom-call(s32[1]{0:T(128)} %bitcast.2.place_ref, bf16[192,1024]{1,0:T(8,128)(2,1)S(1)} %collective-permute-done.4.refs_0_, bf16[192,1024]{1,0:T(8,128)(2,1)S(1)} %collective-permute-done.5.refs_1_, bf16[1024,256]{1,0:T(8,128)(2,1)S(1)} %pad_maximum_fusion.refs_2_, ...), custom_call_target="tpu_custom_call" | custom-call | tf_op jit(solution)/shard_map/pallas_call | solution.py:50
  72.8 4.0 %all-to-all-start.2 = ((bf16[4,384,256]{2,1,0:T(8,128)(2,1)}), bf16[4,384,256]{2,1,0:T(8,128)(2,1)S(1)}, u32[]{:S(2)}, u32[]{:S(2)}) async-start(bf16[4,384,256]{2,1,0:T(8,128)(2,1)} %shard_map.104), calls=%async_computation.2 | async-start | bytes 1572864 | tf_op jit(solution)/shard_map/all_to_all | solution.py:297
  76.8 3.7 %collective-permute-start = (bf16[192,1024]{1,0:T(8,128)(2,1)S(1)}, bf16[192,1024]{1,0:T(8,128)(2,1)S(1)}, u32[]{:S(2)}, u32[]{:S(2)}) collective-permute-start(bf16[192,1024]{1,0:T(8,128)(2,1)S(1)} %shard_map.101.refs_0_), channel_id=1, source_target_pairs={{0,4},{4,8},{8,12},{12,16},{16,20},{20,24},{24,28},{28,32},{32,36}... | collective-permute-start | bytes 1179656 | tf_op jit(solution)/shard_map/ppermute | solution.py:37
  80.5 7.9 %collective-permute-done.refs_1_ = bf16[192,1024]{1,0:T(8,128)(2,1)S(1)} collective-permute-done((bf16[192,1024]{1,0:T(8,128)(2,1)S(1)}, bf16[192,1024]{1,0:T(8,128)(2,1)S(1)}, u32[]{:S(2)}, u32[]{:S(2)}) %collective-permute-start) | collective-permute-done | bytes 393248 | tf_op jit(solution)/shard_map/ppermute | solution.py:37
  88.4 1.9 %shard_map.102 = bf16[4,384,256]{2,1,0:T(8,128)(2,1)} custom-call(s32[1]{0:T(128)} %bitcast.2.place_ref, bf16[192,1024]{1,0:T(8,128)(2,1)S(1)} %shard_map.101.refs_0_, bf16[192,1024]{1,0:T(8,128)(2,1)S(1)} %collective-permute-done.refs_1_, bf16[1024,256]{1,0:T(8,128)(2,1)S(1)} %pad_maximum_fusion.refs_2_, ...), custom_call_target="tpu_custom_call" | custom-call | tf_op jit(solution)/shard_map/pallas_call | solution.py:50
  90.3 4.5 %all-to-all-start.1 = ((bf16[4,384,256]{2,1,0:T(8,128)(2,1)}), bf16[4,384,256]{2,1,0:T(8,128)(2,1)S(1)}, u32[]{:S(2)}, u32[]{:S(2)}) async-start(bf16[4,384,256]{2,1,0:T(8,128)(2,1)} %shard_map.102), calls=%async_computation.1 | async-start | bytes 1572864 | tf_op jit(solution)/shard_map/all_to_all | solution.py:297
  95.0 17.8 %all-gather = bf16[1536,128]{1,0:T(8,128)(2,1)S(1)} all-gather(bf16[384,128]{1,0:T(8,128)(2,1)S(1)} %shard_map.105), channel_id=2, replica_groups=mesh['expert'=8,'dp'=16,'tensor'=4] {'tensor'}, dimensions={0}, use_global_device_ids=true | all-gather | bytes 491520 | tf_op jit(solution)/shard_map/all_gather | solution.py:300
  113.5 9.8 %all-gather.1 = bf16[1536,128]{1,0:T(8,128)(2,1)S(1)} all-gather(bf16[384,128]{1,0:T(8,128)(2,1)S(1)} %shard_map.103), channel_id=3, replica_groups=mesh['expert'=8,'dp'=16,'tensor'=4] {'tensor'}, dimensions={0}, use_global_device_ids=true | all-gather | bytes 491520 | tf_op jit(solution)/shard_map/all_gather | solution.py:300
  123.9 1.9 %collective-permute-start.6 = (bf16[192,1024]{1,0:T(8,128)(2,1)S(1)}, bf16[192,1024]{1,0:T(8,128)(2,1)S(1)}, u32[]{:S(2)}, u32[]{:S(2)}) collective-permute-start(bf16[192,1024]{1,0:T(8,128)(2,1)S(1)} %get-tuple-element.16), channel_id=1, source_target_pairs={{0,60},{4,0},{8,4},{12,8},{16,12},{20,16},{24,20},{28,24},{32,28},... | collective-permute-start | bytes 1179656 | tf_op jit(solution)/shard_map/ppermute | solution.py:37
  125.8 3.4 %collective-permute-start.7 = (bf16[192,1024]{1,0:T(8,128)(2,1)S(1)}, bf16[192,1024]{1,0:T(8,128)(2,1)S(1)}, u32[]{:S(2)}, u32[]{:S(2)}) collective-permute-start(bf16[192,1024]{1,0:T(8,128)(2,1)S(1)} %get-tuple-element.17), channel_id=1, source_target_pairs={{0,4},{4,8},{8,12},{12,16},{16,20},{20,24},{24,28},{28,32},{32,36}... | collective-permute-start | bytes 1179656 | tf_op jit(solution)/shard_map/ppermute | solution.py:37
  129.2 1.9 %collective-permute-start.8 = (bf16[192,1024]{1,0:T(8,128)(2,1)S(1)}, bf16[192,1024]{1,0:T(8,128)(2,1)S(1)}, u32[]{:S(2)}, u32[]{:S(2)}) collective-permute-start(bf16[192,1024]{1,0:T(8,128)(2,1)S(1)} %get-tuple-element.18), channel_id=1, source_target_pairs={{0,56},{4,60},{8,0},{12,4},{16,8},{20,12},{24,16},{28,20},{32,24},... | collective-permute-start | bytes 1179656 | tf_op jit(solution)/shard_map/ppermute | solution.py:37
  131.1 2.2 %collective-permute-done.6.refs_0_ = bf16[192,1024]{1,0:T(8,128)(2,1)S(1)} collective-permute-done((bf16[192,1024]{1,0:T(8,128)(2,1)S(1)}, bf16[192,1024]{1,0:T(8,128)(2,1)S(1)}, u32[]{:S(2)}, u32[]{:S(2)}) %collective-permute-start.6) | collective-permute-done | bytes 393248 | tf_op jit(solution)/shard_map/ppermute | solution.py:37
  133.3 3.2 %collective-permute-done.7.refs_1_ = bf16[192,1024]{1,0:T(8,128)(2,1)S(1)} collective-permute-done((bf16[192,1024]{1,0:T(8,128)(2,1)S(1)}, bf16[192,1024]{1,0:T(8,128)(2,1)S(1)}, u32[]{:S(2)}, u32[]{:S(2)}) %collective-permute-start.7) | collective-permute-done | bytes 393248 | tf_op jit(solution)/shard_map/ppermute | solution.py:37
  136.5 10.2 %collective-permute-done.8.refs_2_ = bf16[192,1024]{1,0:T(8,128)(2,1)S(1)} collective-permute-done((bf16[192,1024]{1,0:T(8,128)(2,1)S(1)}, bf16[192,1024]{1,0:T(8,128)(2,1)S(1)}, u32[]{:S(2)}, u32[]{:S(2)}) %collective-permute-start.8) | collective-permute-done | bytes 393248 | tf_op jit(solution)/shard_map/ppermute | solution.py:37
  146.6 1.2 shard_map.108
  147.9 10.1 %all-to-all-start.3 = ((bf16[32,48,128]{2,1,0:T(8,128)(2,1)}), bf16[32,48,128]{2,1,0:T(8,128)(2,1)S(1)}, u32[]{:S(2)}, u32[]{:S(2)}) async-start(bf16[32,48,128]{2,1,0:T(8,128)(2,1)} %shard_map.108), calls=%async_computation.3 | async-start | bytes 786432 | tf_op jit(solution)/shard_map/all_to_all | solution.py:27
  158.8 25.5 %all-to-all-done.3.in_ref = bf16[32,48,128]{2,1,0:T(8,128)(2,1)S(1)} async-done(((bf16[32,48,128]{2,1,0:T(8,128)(2,1)}), bf16[32,48,128]{2,1,0:T(8,128)(2,1)S(1)}, u32[]{:S(2)}, u32[]{:S(2)}) %all-to-all-start.3) | async-done | bytes 393248 | tf_op jit(solution)/shard_map/all_to_all | solution.py:27
  184.3 1.8 shard_map.109
  (32 shorter events, 5.1 us)
Async XLA Ops:
  0.0 0.9 copy-start
  0.9 0.7 copy-start.5
  0.9 21.3 %copy-start.7 = (bf16[1,4096,128]{2,1,0:T(8,128)(2,1)S(1)}, bf16[1,4096,128]{2,1,0:T(8,128)(2,1)}, u32[]{:S(2)}) copy-start(bf16[1,4096,128]{2,1,0:T(8,128)(2,1)} %param.14) | copy-start | bytes 3145732
  2.8 42.0 %all-to-all-start = ((bf16[32,48,128]{2,1,0:T(8,128)(2,1)}), bf16[32,48,128]{2,1,0:T(8,128)(2,1)S(1)}, u32[]{:S(2)}, u32[]{:S(2)}) async-start(bf16[32,48,128]{2,1,0:T(8,128)(2,1)} %shard_map.100), calls=%async_computation | async-start | bytes 786432 | tf_op jit(solution)/shard_map/all_to_all | solution.py:27
  25.2 31.7 %collective-permute-start.1 = (bf16[1024,256]{1,0:T(8,128)(2,1)}, bf16[1024,256]{1,0:T(8,128)(2,1)S(1)}, u32[]{:S(2)}, u32[]{:S(2)}) collective-permute-start(bf16[1024,256]{1,0:T(8,128)(2,1)} %pad_maximum_fusion.1), channel_id=1, source_target_pairs={{0,1},{1,2},{2,3},{3,0},{4,5},{5,6},{6,7},{7,4},{8,9},{9,10},{10,1... | collective-permute-start | bytes 1572872 | tf_op jit(solution)/shard_map/ppermute | solution.py:175
  29.2 27.7 %collective-permute-start.2 = (bf16[1024,256]{1,0:T(8,128)(2,1)}, bf16[1024,256]{1,0:T(8,128)(2,1)S(1)}, u32[]{:S(2)}, u32[]{:S(2)}) collective-permute-start(bf16[1024,256]{1,0:T(8,128)(2,1)} %pad_maximum_fusion.2), channel_id=1, source_target_pairs={{0,3},{1,0},{2,1},{3,2},{4,7},{5,4},{6,5},{7,6},{8,11},{9,8},{10,9... | collective-permute-start | bytes 1572872 | tf_op jit(solution)/shard_map/ppermute | solution.py:175
  32.6 12.2 %copy-start.3 = (bf16[384,384]{1,0:T(8,128)(2,1)S(1)}, bf16[384,384]{1,0:T(8,128)(2,1)}, u32[]{:S(2)}) copy-start(bf16[384,384]{1,0:T(8,128)(2,1)} %constant.61.clone.order_ref) | copy-start | bytes 884740
  33.5 23.5 %collective-permute-start.3 = (bf16[1024,256]{1,0:T(8,128)(2,1)}, bf16[1024,256]{1,0:T(8,128)(2,1)S(1)}, u32[]{:S(2)}, u32[]{:S(2)}) collective-permute-start(bf16[1024,256]{1,0:T(8,128)(2,1)} %pad_maximum_fusion.3), channel_id=1, source_target_pairs={{0,2},{1,3},{2,0},{3,1},{4,6},{5,7},{6,4},{7,5},{8,10},{9,11},{10,... | collective-permute-start | bytes 1572872 | tf_op jit(solution)/shard_map/ppermute | solution.py:175
  45.3 17.4 %collective-permute-start.4 = (bf16[192,1024]{1,0:T(8,128)(2,1)S(1)}, bf16[192,1024]{1,0:T(8,128)(2,1)S(1)}, u32[]{:S(2)}, u32[]{:S(2)}) collective-permute-start(bf16[192,1024]{1,0:T(8,128)(2,1)S(1)} %shard_map.101.refs_0_), channel_id=1, source_target_pairs={{0,60},{4,0},{8,4},{12,8},{16,12},{20,16},{24,20},{28,24},{32,28},... | collective-permute-start | bytes 1179656 | tf_op jit(solution)/shard_map/ppermute | solution.py:37
  52.3 18.6 %collective-permute-start.5 = (bf16[192,1024]{1,0:T(8,128)(2,1)S(1)}, bf16[192,1024]{1,0:T(8,128)(2,1)S(1)}, u32[]{:S(2)}, u32[]{:S(2)}) collective-permute-start(bf16[192,1024]{1,0:T(8,128)(2,1)S(1)} %shard_map.101.refs_0_), channel_id=1, source_target_pairs={{0,8},{4,12},{8,16},{12,20},{16,24},{20,28},{24,32},{28,36},{32,40... | collective-permute-start | bytes 1179656 | tf_op jit(solution)/shard_map/ppermute | solution.py:37
  72.8 17.5 %all-to-all-start.2 = ((bf16[4,384,256]{2,1,0:T(8,128)(2,1)}), bf16[4,384,256]{2,1,0:T(8,128)(2,1)S(1)}, u32[]{:S(2)}, u32[]{:S(2)}) async-start(bf16[4,384,256]{2,1,0:T(8,128)(2,1)} %shard_map.104), calls=%async_computation.2 | async-start | bytes 1572864 | tf_op jit(solution)/shard_map/all_to_all | solution.py:297
  76.8 11.6 %collective-permute-start = (bf16[192,1024]{1,0:T(8,128)(2,1)S(1)}, bf16[192,1024]{1,0:T(8,128)(2,1)S(1)}, u32[]{:S(2)}, u32[]{:S(2)}) collective-permute-start(bf16[192,1024]{1,0:T(8,128)(2,1)S(1)} %shard_map.101.refs_0_), channel_id=1, source_target_pairs={{0,4},{4,8},{8,12},{12,16},{16,20},{20,24},{24,28},{28,32},{32,36}... | collective-permute-start | bytes 1179656 | tf_op jit(solution)/shard_map/ppermute | solution.py:37
  90.3 23.0 %all-to-all-start.1 = ((bf16[4,384,256]{2,1,0:T(8,128)(2,1)}), bf16[4,384,256]{2,1,0:T(8,128)(2,1)S(1)}, u32[]{:S(2)}, u32[]{:S(2)}) async-start(bf16[4,384,256]{2,1,0:T(8,128)(2,1)} %shard_map.102), calls=%async_computation.1 | async-start | bytes 1572864 | tf_op jit(solution)/shard_map/all_to_all | solution.py:297
  94.8 17.9 %copy-start.1 = (bf16[1,512,1024]{2,1,0:T(8,128)(2,1)S(1)}, bf16[1,512,1024]{2,1,0:T(8,128)(2,1)}, u32[]{:S(2)}) copy-start(bf16[1,512,1024]{2,1,0:T(8,128)(2,1)} %param.15) | copy-start | bytes 3145732
  123.3 23.4 %copy-start.2 = (bf16[384,384]{1,0:T(8,128)(2,1)S(1)}, bf16[384,384]{1,0:T(8,128)(2,1)}, u32[]{:S(2)}) copy-start(bf16[384,384]{1,0:T(8,128)(2,1)} %constant.62.clone.order_ref) | copy-start | bytes 884740
  123.9 9.4 %collective-permute-start.6 = (bf16[192,1024]{1,0:T(8,128)(2,1)S(1)}, bf16[192,1024]{1,0:T(8,128)(2,1)S(1)}, u32[]{:S(2)}, u32[]{:S(2)}) collective-permute-start(bf16[192,1024]{1,0:T(8,128)(2,1)S(1)} %get-tuple-element.16), channel_id=1, source_target_pairs={{0,60},{4,0},{8,4},{12,8},{16,12},{20,16},{24,20},{28,24},{32,28},... | collective-permute-start | bytes 1179656 | tf_op jit(solution)/shard_map/ppermute | solution.py:37
  125.8 10.7 %collective-permute-start.7 = (bf16[192,1024]{1,0:T(8,128)(2,1)S(1)}, bf16[192,1024]{1,0:T(8,128)(2,1)S(1)}, u32[]{:S(2)}, u32[]{:S(2)}) collective-permute-start(bf16[192,1024]{1,0:T(8,128)(2,1)S(1)} %get-tuple-element.17), channel_id=1, source_target_pairs={{0,4},{4,8},{8,12},{12,16},{16,20},{20,24},{24,28},{28,32},{32,36}... | collective-permute-start | bytes 1179656 | tf_op jit(solution)/shard_map/ppermute | solution.py:37
  129.2 17.5 %collective-permute-start.8 = (bf16[192,1024]{1,0:T(8,128)(2,1)S(1)}, bf16[192,1024]{1,0:T(8,128)(2,1)S(1)}, u32[]{:S(2)}, u32[]{:S(2)}) collective-permute-start(bf16[192,1024]{1,0:T(8,128)(2,1)S(1)} %get-tuple-element.18), channel_id=1, source_target_pairs={{0,56},{4,60},{8,0},{12,4},{16,8},{20,12},{24,16},{28,20},{32,24},... | collective-permute-start | bytes 1179656 | tf_op jit(solution)/shard_map/ppermute | solution.py:37
  147.9 36.4 %copy-start.4 = (bf16[8,16,1024]{2,1,0:T(8,128)(2,1)S(1)}, bf16[8,16,1024]{2,1,0:T(8,128)(2,1)}, u32[]{:S(2)}) copy-start(bf16[8,16,1024]{2,1,0:T(8,128)(2,1)} %past_ref.1) | copy-start | bytes 786436
  147.9 36.4 %all-to-all-start.3 = ((bf16[32,48,128]{2,1,0:T(8,128)(2,1)}), bf16[32,48,128]{2,1,0:T(8,128)(2,1)S(1)}, u32[]{:S(2)}, u32[]{:S(2)}) async-start(bf16[32,48,128]{2,1,0:T(8,128)(2,1)} %shard_map.108), calls=%async_computation.3 | async-start | bytes 786432 | tf_op jit(solution)/shard_map/all_to_all | solution.py:27
  158.0 0.7 copy-start.8
  158.7 25.6 %copy-start.6 = (f32[9]{0:T(128)S(1)}, f32[9]{0:T(128)}, u32[]{:S(2)}) copy-start(f32[9]{0:T(128)} %dwa_ref.1) | copy-start | bytes 112

commit v8 on v6

--- a/solution.py
+++ b/solution.py
@@ -8,10 +8,16 @@
 
 RADIX = 4
 LANES = 128
+TERMS = 3
 SHIFTS = (0, 1, 3, 2)
 LIMIT = pltpu.CompilerParams(vmem_limit_bytes=16 * 2**20)
+HBM = pl.BlockSpec(memory_space=pltpu.HBM)
 SMEM = pl.BlockSpec(memory_space=pltpu.SMEM)
 VMEM = pl.BlockSpec(memory_space=pltpu.VMEM)
+
+
+def in_hbm(array):
+    return pltpu.with_memory_space_constraint(array, pltpu.HBM)
 
 
 def far_groups():
@@ -96,14 +102,21 @@
     return jnp.concatenate(pieces, axis=0)
 
 
-def packed_rows(ids, own_columns, experts, capacity):
-    tok_rows, features = own_columns.shape
-    blocks = features // LANES
-
-    def kernel(ids_ref, in_ref, out_ref):
+def packed_rows(ids, tokens, first_column, quarter, experts, capacity):
+    tok_rows = tokens.shape[0]
+    blocks = quarter // LANES
+
+    def kernel(first_ref, ids_in_ref, tokens_ref, out_ref, own_ref, ids_ref, named, arrived):
+        first = pl.multiple_of(first_ref[0], LANES)
+        ids_copy = pltpu.make_async_copy(ids_in_ref, ids_ref, named)
+        copy = pltpu.make_async_copy(tokens_ref.at[:, pl.ds(first, quarter)], own_ref, arrived)
+        ids_copy.start()
+        copy.start()
+        ids_copy.wait()
         slots = assigned_slots(ids_ref[...], experts, tok_rows)
         chosen = placed(slots, [1.0] * len(slots), capacity, tok_rows).astype(jnp.bfloat16)
-        tall = [in_ref[:, block * LANES : (block + 1) * LANES] for block in range(blocks)]
+        copy.wait()
+        tall = [own_ref[:, block * LANES : (block + 1) * LANES] for block in range(blocks)]
         out = jnp.dot(chosen, jnp.concatenate(tall, axis=0), preferred_element_type=jnp.float32)
         out = out.astype(out_ref.dtype)
         height = capacity * blocks
@@ -111,8 +124,18 @@
             for far in range(RADIX):
                 out_ref[expert * RADIX + far] = out[expert * height : (expert + 1) * height]
 
-    shape = jax.ShapeDtypeStruct((experts * RADIX, capacity * blocks, LANES), own_columns.dtype)
-    return call(kernel, "packed_rows", shape, ids, own_columns)
+    return pl.pallas_call(
+        kernel,
+        out_shape=[
+            jax.ShapeDtypeStruct((experts * RADIX, capacity * blocks, LANES), tokens.dtype),
+            jax.ShapeDtypeStruct((tok_rows, quarter), tokens.dtype),
+        ],
+        in_specs=[SMEM, HBM, HBM],
+        out_specs=[VMEM, VMEM],
+        scratch_shapes=[pltpu.VMEM(ids.shape, ids.dtype), pltpu.SemaphoreType.DMA, pltpu.SemaphoreType.DMA],
+        compiler_params=LIMIT,
+        name="packed_rows",
+    )(first_column, ids, tokens)
 
 
 def chunk_order(chunks, capacity, blocks):
@@ -230,13 +253,39 @@
     return call(kernel, "down_sets", shapes, hidden, w_down)
 
 
-def mixed_layers(returned, ids, route, own_columns, past_layers, dwa_weight, experts, capacity):
+def mix_terms(ids, route, own_columns, past_layers, dwa_weight, experts, capacity):
     tok_rows, features = own_columns.shape
-    blocks = features // LANES
-    height = capacity * blocks
+    height = capacity * (features // LANES)
     depth = past_layers.shape[0]
 
-    def kernel(dwa_ref, ids_ref, route_ref, own_ref, past_ref, in_ref, out_ref):
+    def kernel(dwa_ref, ids_ref, route_ref, own_ref, past_ref, terms_ref, base_ref):
+        slots = assigned_slots(ids_ref[...], experts, tok_rows)
+        route = route_ref[...]
+        total = sum(route[place : place + 1, :] for place in range(len(slots)))
+        shares = [dwa_ref[depth] * (route[place : place + 1, :] / total) for place in range(len(slots))]
+        rest = placed(slots, shares, capacity, tok_rows)
+        for place in range(TERMS):
+            term = rest.astype(jnp.bfloat16)
+            rest = rest - term.astype(jnp.float32)
+            terms_ref[place] = term
+        base = dwa_ref[depth] * own_ref[...].astype(jnp.float32)
+        for layer in range(depth):
+            base += dwa_ref[layer] * past_ref[layer].astype(jnp.float32)
+        base_ref[...] = base
+
+    shapes = [
+        jax.ShapeDtypeStruct((TERMS, experts * height, LANES), jnp.bfloat16),
+        jax.ShapeDtypeStruct((tok_rows, features), jnp.float32),
+    ]
+    operands = (dwa_weight, ids, route, own_columns, past_layers)
+    return call(kernel, "mix_terms", shapes, *operands, in_specs=[SMEM] + [VMEM] * 4)
+
+
+def mixed_layers(returned, terms, base, dtype):
+    tok_rows, features = base.shape
+    experts = returned.shape[0] // RADIX
+
+    def kernel(terms_ref, base_ref, in_ref, out_ref):
         outs = []
         for expert in range(experts):
             total = in_ref[expert * RADIX].astype(jnp.float32)
@@ -244,36 +293,18 @@
                 total += in_ref[expert * RADIX + far].astype(jnp.float32)
             outs.append(total.astype(jnp.bfloat16))
         outs = jnp.concatenate(outs, axis=0)
-        slots = assigned_slots(ids_ref[...], experts, tok_rows)
-        route = route_ref[...]
-        total = sum(route[place : place + 1, :] for place in range(len(slots)))
-        shares = [route[place : place + 1, :] / total for place in range(len(slots))]
-        rest = placed(slots, shares, capacity, tok_rows)
-        mix = jnp.zeros((blocks * tok_rows, LANES), jnp.float32)
-        for _ in range(3):
-            term = rest.astype(jnp.bfloat16)
-            rest = rest - term.astype(jnp.float32)
-            mix += lax.dot_general(term, outs, (((0,), (0,)), ((), ())), preferred_element_type=jnp.float32)
-        for block in range(blocks):
+        mix = jnp.zeros((features // LANES * tok_rows, LANES), jnp.float32)
+        for place in range(TERMS):
+            mix += lax.dot_general(
+                terms_ref[place], outs, (((0,), (0,)), ((), ())), preferred_element_type=jnp.float32
+            )
+        for block in range(features // LANES):
             lanes = slice(block * LANES, (block + 1) * LANES)
-            current = own_ref[:, lanes].astype(jnp.float32) + mix[block * tok_rows : (block + 1) * tok_rows]
-            value = dwa_ref[depth] * current
-            for layer in range(depth):
-                value += dwa_ref[layer] * past_ref[layer, :, lanes].astype(jnp.float32)
+            value = base_ref[:, lanes] + mix[block * tok_rows : (block + 1) * tok_rows]
             out_ref[:, lanes] = value.astype(out_ref.dtype)
 
-    return call(
-        kernel,
-        "mixed_layers",
-        jax.ShapeDtypeStruct((tok_rows, features), own_columns.dtype),
-        dwa_weight,
-        ids,
-        route,
-        own_columns,
-        past_layers,
-        returned,
-        in_specs=[SMEM] + [VMEM] * 5,
-    )
+    shape = jax.ShapeDtypeStruct((tok_rows, features), dtype)
+    return call(kernel, "mixed_layers", shape, terms, base, returned)
 
 
 def per_device(
@@ -290,22 +321,21 @@
     order = chunk_order(together, capacity, blocks)
     ids = expert_ids.T
     route = jnp.tile(route_weight.T, (1, blocks))
-    first_column = lax.axis_index("tensor") * quarter
-    own_columns = lax.dynamic_slice_in_dim(tokens, first_column, quarter, 1)
-
     weights = weights_by_features(gate_weight, up_weight, quarter)
     place = lax.axis_index("tensor").reshape(1)
-    arrived = far_exchange(packed_rows(ids, own_columns, experts, capacity))
+    packed, own_columns = packed_rows(in_hbm(ids), in_hbm(tokens), place * quarter, quarter, experts, capacity)
+    arrived = far_exchange(packed)
     own_set = wide_rows(arrived, jnp.asarray(order, jnp.bfloat16), capacity)
     sets = [own_set, *from_neighbours(own_set)]
     partial = lax.all_to_all(gate_up_parts(sets, weights, place), "tensor", 0, 0, tiled=True)
     hidden = lax.all_gather(hidden_units(partial), "tensor", axis=0, tiled=False)
     own, *others = down_sets(hidden, down_weight[0], len(sets))
-    summed = summed_chunks(own, to_neighbours(others), jnp.asarray(order.T, jnp.bfloat16), capacity)
-    returned = far_exchange(summed)
-    return mixed_layers(
-        returned, ids, route, own_columns, past_layers, dwa_weight, experts, capacity
-    )
+    route, own = lax.optimization_barrier((route, own))
+    terms, base = mix_terms(ids, route, own_columns, past_layers, dwa_weight, experts, capacity)
+    others = to_neighbours(others)
+    own, terms, base = lax.optimization_barrier((own, terms, base))
+    returned = far_exchange(summed_chunks(own, others, jnp.asarray(order.T, jnp.bfloat16), capacity))
+    return mixed_layers(returned, terms, base, tokens.dtype)
 
 
 def solution(mesh):

time: 175 us -> 173 us (0.989)
  blocking collectives: 33.3 us -> 68 us
  waiting for transfers between devices: 65.5 us -> 38.9 us
  starting transfers between devices: 62.6 us -> 53.2 us
    all_to_all x0 -> x1, blocking collectives: none -> 34.7 us  [far_exchange(): lax.all_to_all(chunks, ('expert', 'dp'), 0, 0, tiled=True, axis_index_gro...]
    all_to_all x2 -> x1, waiting for transfers between devices: 35.6 us -> 9.51 us  [far_exchange(): lax.all_to_all(chunks, ('expert', 'dp'), 0, 0, tiled=True, axis_index_gro...]
    all_to_all x2 -> x1, starting transfers between devices: 28.2 us -> 19.4 us  [far_exchange(): lax.all_to_all(chunks, ('expert', 'dp'), 0, 0, tiled=True, axis_index_gro...]
    pallas_call x0 -> x1, Pallas kernels: none -> 2 us  [packed_rows(): pl.pallas_call(kernel, out_shape=[jax.ShapeDtypeStruct((experts * RADIX,...]
  transfers between devices with their start and end apart: 11 -> 10, of which waited for: 8 -> 7; matrix products, arithmetic and copies ran while one was open for 2% -> 2% of each run, Pallas kernels for 0% -> 1%
where the time goes in v8:
time: 173 us; the launch traced here: 172 us
  blocking collectives  68 us (39%)
  starting transfers between devices  53.2 us (31%)
  waiting for transfers between devices  38.9 us (22%)
  Pallas kernels  8.55 us (5%)
  other arithmetic  1.84 us (1%)
    all_to_all x1, blocking collectives, far_exchange(): lax.all_to_all(chunks, ('expert', 'dp'), 0, 0, tiled=True, axis_index_gro...  34.7 us
    ppermute x6, waiting for transfers between devices, shifted(): return lax.ppermute(shard, ('expert', 'dp'), pairs)  29.4 us
    ppermute x6, starting transfers between devices, shifted(): return lax.ppermute(shard, ('expert', 'dp'), pairs)  23.9 us
    all_to_all x1, blocking collectives, per_device(): lax.all_to_all(gate_up_parts(sets, weights, place), 'tensor', 0, 0, tiled...  21.8 us
    all_to_all x1, starting transfers between devices, far_exchange(): lax.all_to_all(chunks, ('expert', 'dp'), 0, 0, tiled=True, axis_index_gro...  19.4 us
    all_gather x1, blocking collectives, per_device(): lax.all_gather(hidden_units(partial), 'tensor', axis=0, tiled=False)  11.5 us
    ppermute x3, starting transfers between devices, slab(): lax.ppermute(both, 'tensor', [(i, (i + shift) % parts) for i in range(par...  9.91 us
    all_to_all x1, waiting for transfers between devices, far_exchange(): lax.all_to_all(chunks, ('expert', 'dp'), 0, 0, tiled=True, axis_index_gro...  9.51 us
  transfers between devices with their start and end apart: 10, of which 7 were waited for; matrix products, arithmetic and copies ran while one was open for 2% of the time, Pallas kernels for 1%

profile of v8, /device:TPU:1, one launch (start us, length us, event | category | flops | bytes accessed | tf_op | source)
XLA Modules:
  0.0 172.2 jit_solution(3550336253535236300)
XLA Ops:
  0.0 2.0 %packed_rows.1 = (bf16[32,48,128]{2,1,0:T(8,128)(2,1)}, bf16[16,1024]{1,0:T(8,128)(2,1)S(1)}) custom-call(s32[1]{0:T(128)S(6)} %mul.3.first_ref, s32[2,16]{1,0:T(2,128)} %bitcast.25, bf16[16,4096]{1,0:T(8,128)(2,1)} %tokens_ref.1), custom_call_target="tpu_custom_call" | custom-call | tf_op jit(solution)/shard_map/packed_rows/pallas_call | solution.py:127
  2.0 19.4 %all-to-all-start = ((bf16[32,48,128]{2,1,0:T(8,128)(2,1)}), bf16[32,48,128]{2,1,0:T(8,128)(2,1)S(1)}, u32[]{:S(2)}, u32[]{:S(2)}) async-start(bf16[32,48,128]{2,1,0:T(8,128)(2,1)} %get-tuple-element.18), calls=%async_computation | async-start | bytes 786432 | tf_op jit(solution)/shard_map/all_to_all | solution.py:33
  21.5 1.3 dynamic-slice_bitcast_fusion
  22.8 0.9 pad_maximum_fusion.3
  23.7 4.6 %collective-permute-start.5 = (bf16[1024,256]{1,0:T(8,128)(2,1)}, bf16[1024,256]{1,0:T(8,128)(2,1)S(1)}, u32[]{:S(2)}, u32[]{:S(2)}) collective-permute-start(bf16[1024,256]{1,0:T(8,128)(2,1)} %pad_maximum_fusion.3), channel_id=1, source_target_pairs={{0,2},{1,3},{2,0},{3,1},{4,6},{5,7},{6,4},{7,5},{8,10},{9,11},{10,... | collective-permute-start | bytes 1572872 | tf_op jit(solution)/shard_map/ppermute | solution.py:200
  28.4 2.8 %collective-permute-start.4 = (bf16[1024,256]{1,0:T(8,128)(2,1)S(1)}, bf16[1024,256]{1,0:T(8,128)(2,1)S(1)}, u32[]{:S(2)}, u32[]{:S(2)}) collective-permute-start(bf16[1024,256]{1,0:T(8,128)(2,1)S(1)} %pad_maximum_fusion.2), channel_id=1, source_target_pairs={{0,3},{1,0},{2,1},{3,2},{4,7},{5,4},{6,5},{7,6},{8,11},{9,8},{10,9... | collective-permute-start | bytes 1572872 | tf_op jit(solution)/shard_map/ppermute | solution.py:200
  31.2 0.9 pad_maximum_fusion.1
  32.0 2.5 %collective-permute-start.3 = (bf16[1024,256]{1,0:T(8,128)(2,1)}, bf16[1024,256]{1,0:T(8,128)(2,1)S(1)}, u32[]{:S(2)}, u32[]{:S(2)}) collective-permute-start(bf16[1024,256]{1,0:T(8,128)(2,1)} %pad_maximum_fusion.1), channel_id=1, source_target_pairs={{0,1},{1,2},{2,3},{3,0},{4,5},{5,6},{6,7},{7,4},{8,9},{9,10},{10,1... | collective-permute-start | bytes 1572872 | tf_op jit(solution)/shard_map/ppermute | solution.py:200
  34.5 9.5 %all-to-all-done.in_ref = bf16[32,48,128]{2,1,0:T(8,128)(2,1)S(1)} async-done(((bf16[32,48,128]{2,1,0:T(8,128)(2,1)}), bf16[32,48,128]{2,1,0:T(8,128)(2,1)S(1)}, u32[]{:S(2)}, u32[]{:S(2)}) %all-to-all-start) | async-done | bytes 393248 | tf_op jit(solution)/shard_map/all_to_all | solution.py:33
  44.0 0.5 wide_rows.1.refs_0_
  44.5 9.0 %collective-permute-start = (bf16[192,1024]{1,0:T(8,128)(2,1)S(1)}, bf16[192,1024]{1,0:T(8,128)(2,1)S(1)}, u32[]{:S(2)}, u32[]{:S(2)}) collective-permute-start(bf16[192,1024]{1,0:T(8,128)(2,1)S(1)} %wide_rows.1.refs_0_), channel_id=1, source_target_pairs={{0,4},{4,8},{8,12},{12,16},{16,20},{20,24},{24,28},{28,32},{32,36}... | collective-permute-start | bytes 1179656 | tf_op jit(solution)/shard_map/ppermute | solution.py:43
  53.6 1.9 %collective-permute-start.1 = (bf16[192,1024]{1,0:T(8,128)(2,1)S(1)}, bf16[192,1024]{1,0:T(8,128)(2,1)S(1)}, u32[]{:S(2)}, u32[]{:S(2)}) collective-permute-start(bf16[192,1024]{1,0:T(8,128)(2,1)S(1)} %wide_rows.1.refs_0_), channel_id=1, source_target_pairs={{0,60},{4,0},{8,4},{12,8},{16,12},{20,16},{24,20},{28,24},{32,28},... | collective-permute-start | bytes 1179656 | tf_op jit(solution)/shard_map/ppermute | solution.py:43
  55.5 2.9 %collective-permute-start.2 = (bf16[192,1024]{1,0:T(8,128)(2,1)S(1)}, bf16[192,1024]{1,0:T(8,128)(2,1)S(1)}, u32[]{:S(2)}, u32[]{:S(2)}) collective-permute-start(bf16[192,1024]{1,0:T(8,128)(2,1)S(1)} %wide_rows.1.refs_0_), channel_id=1, source_target_pairs={{0,8},{4,12},{8,16},{12,20},{16,24},{20,28},{24,32},{28,36},{32,40... | collective-permute-start | bytes 1179656 | tf_op jit(solution)/shard_map/ppermute | solution.py:43
  58.5 4.8 %collective-permute-done.refs_1_ = bf16[192,1024]{1,0:T(8,128)(2,1)S(1)} collective-permute-done((bf16[192,1024]{1,0:T(8,128)(2,1)S(1)}, bf16[192,1024]{1,0:T(8,128)(2,1)S(1)}, u32[]{:S(2)}, u32[]{:S(2)}) %collective-permute-start) | collective-permute-done | bytes 393248 | tf_op jit(solution)/shard_map/ppermute | solution.py:43
  63.3 2.5 %collective-permute-done.1.refs_2_ = bf16[192,1024]{1,0:T(8,128)(2,1)S(1)} collective-permute-done((bf16[192,1024]{1,0:T(8,128)(2,1)S(1)}, bf16[192,1024]{1,0:T(8,128)(2,1)S(1)}, u32[]{:S(2)}, u32[]{:S(2)}) %collective-permute-start.1) | collective-permute-done | bytes 393248 | tf_op jit(solution)/shard_map/ppermute | solution.py:43
  65.8 8.3 %collective-permute-done.2.refs_3_ = bf16[192,1024]{1,0:T(8,128)(2,1)S(1)} collective-permute-done((bf16[192,1024]{1,0:T(8,128)(2,1)S(1)}, bf16[192,1024]{1,0:T(8,128)(2,1)S(1)}, u32[]{:S(2)}, u32[]{:S(2)}) %collective-permute-start.2) | collective-permute-done | bytes 393248 | tf_op jit(solution)/shard_map/ppermute | solution.py:43
  74.1 1.9 %gate_up_parts.1 = bf16[4,768,256]{2,1,0:T(8,128)(2,1)S(1)} custom-call(s32[1]{0:T(128)} %bitcast.1.place_ref, bf16[192,1024]{1,0:T(8,128)(2,1)S(1)} %wide_rows.1.refs_0_, bf16[192,1024]{1,0:T(8,128)(2,1)S(1)} %collective-permute-done.refs_1_, bf16[192,1024]{1,0:T(8,128)(2,1)S(1)} %collective-permute-done.1.refs_2_, ...), custom_call_target="tpu_custom_call" | custom-call | tf_op jit(solution)/shard_map/gate_up_parts/pallas_call | solution.py:57
  76.0 21.8 %all_to_all.15.in_ref = bf16[4,768,256]{2,1,0:T(8,128)(2,1)S(1)} all-to-all(bf16[4,768,256]{2,1,0:T(8,128)(2,1)S(1)} %gate_up_parts.1), channel_id=1, replica_groups=mesh['expert'=8,'dp'=16,'tensor'=4] {'tensor'}, dimensions={0} | all-to-all | bytes 3145728 | tf_op jit(solution)/shard_map/all_to_all | solution.py:330
  97.8 0.3 hidden_units.1
  98.1 11.5 %all-gather = bf16[3072,128]{1,0:T(8,128)(2,1)S(1)} all-gather(bf16[768,128]{1,0:T(8,128)(2,1)S(1)} %hidden_units.1), channel_id=2, replica_groups=mesh['expert'=8,'dp'=16,'tensor'=4] {'tensor'}, dimensions={0}, use_global_device_ids=true | all-gather | bytes 983040 | tf_op jit(solution)/shard_map/all_gather | solution.py:331
  109.6 1.6 down_sets.1
  111.2 2.8 %collective-permute-start.6 = (bf16[192,1024]{1,0:T(8,128)(2,1)}, bf16[192,1024]{1,0:T(8,128)(2,1)S(1)}, u32[]{:S(2)}, u32[]{:S(2)}) collective-permute-start(bf16[192,1024]{1,0:T(8,128)(2,1)} %get-tuple-element.28), channel_id=1, source_target_pairs={{0,60},{4,0},{8,4},{12,8},{16,12},{20,16},{24,20},{28,24},{32,28},... | collective-permute-start | bytes 1179656 | tf_op jit(solution)/shard_map/ppermute | solution.py:43
  114.0 2.5 %collective-permute-start.7 = (bf16[192,1024]{1,0:T(8,128)(2,1)S(1)}, bf16[192,1024]{1,0:T(8,128)(2,1)S(1)}, u32[]{:S(2)}, u32[]{:S(2)}) collective-permute-start(bf16[192,1024]{1,0:T(8,128)(2,1)S(1)} %get-tuple-element.29), channel_id=1, source_target_pairs={{0,4},{4,8},{8,12},{12,16},{16,20},{20,24},{24,28},{28,32},{32,36}... | collective-permute-start | bytes 1179656 | tf_op jit(solution)/shard_map/ppermute | solution.py:43
  116.5 4.7 %collective-permute-start.8 = (bf16[192,1024]{1,0:T(8,128)(2,1)S(1)}, bf16[192,1024]{1,0:T(8,128)(2,1)S(1)}, u32[]{:S(2)}, u32[]{:S(2)}) collective-permute-start(bf16[192,1024]{1,0:T(8,128)(2,1)S(1)} %get-tuple-element.30), channel_id=1, source_target_pairs={{0,56},{4,60},{8,0},{12,4},{16,8},{20,12},{24,16},{28,20},{32,24},... | collective-permute-start | bytes 1179656 | tf_op jit(solution)/shard_map/ppermute | solution.py:43
  121.3 0.1 tile.10.route_ref
  121.4 0.9 mix_terms.1
  122.3 0.2 collective-permute-done.6.refs_0_
  122.5 1.2 collective-permute-done.7.refs_1_
  123.7 12.4 %collective-permute-done.8.refs_2_ = bf16[192,1024]{1,0:T(8,128)(2,1)S(1)} collective-permute-done((bf16[192,1024]{1,0:T(8,128)(2,1)S(1)}, bf16[192,1024]{1,0:T(8,128)(2,1)S(1)}, u32[]{:S(2)}, u32[]{:S(2)}) %collective-permute-start.8) | collective-permute-done | bytes 393248 | tf_op jit(solution)/shard_map/ppermute | solution.py:43
  136.1 0.5 summed_chunks.1
  136.6 34.7 %all_to_all.16.in_ref = bf16[32,48,128]{2,1,0:T(8,128)(2,1)S(1)} all-to-all(bf16[32,48,128]{2,1,0:T(8,128)(2,1)S(1)} %summed_chunks.1), channel_id=1, replica_groups={{0,16,32,48,64,80,96,112,128,144,160,176,192,208,224,240,256,272,288,30..., dimensions={0} | all-to-all | bytes 786432 | tf_op jit(solution)/shard_map/all_to_all | solution.py:33
  171.4 0.9 mixed_layers.1
  (22 shorter events, 0.2 us)
Async XLA Ops:
  0.0 21.5 %copy-start.6 = (bf16[1,4096,128]{2,1,0:T(8,128)(2,1)S(1)}, bf16[1,4096,128]{2,1,0:T(8,128)(2,1)}, u32[]{:S(2)}) copy-start(bf16[1,4096,128]{2,1,0:T(8,128)(2,1)} %param.14) | copy-start | bytes 3145732
  2.0 42.0 %all-to-all-start = ((bf16[32,48,128]{2,1,0:T(8,128)(2,1)}), bf16[32,48,128]{2,1,0:T(8,128)(2,1)S(1)}, u32[]{:S(2)}, u32[]{:S(2)}) async-start(bf16[32,48,128]{2,1,0:T(8,128)(2,1)} %get-tuple-element.18), calls=%async_computation | async-start | bytes 786432 | tf_op jit(solution)/shard_map/all_to_all | solution.py:33
  22.8 21.2 %copy-start.2 = (bf16[384,384]{1,0:T(8,128)(2,1)S(1)}, bf16[384,384]{1,0:T(8,128)(2,1)}, u32[]{:S(2)}) copy-start(bf16[384,384]{1,0:T(8,128)(2,1)} %constant.58.clone.order_ref) | copy-start | bytes 884740
  23.7 31.8 %collective-permute-start.5 = (bf16[1024,256]{1,0:T(8,128)(2,1)}, bf16[1024,256]{1,0:T(8,128)(2,1)S(1)}, u32[]{:S(2)}, u32[]{:S(2)}) collective-permute-start(bf16[1024,256]{1,0:T(8,128)(2,1)} %pad_maximum_fusion.3), channel_id=1, source_target_pairs={{0,2},{1,3},{2,0},{3,1},{4,6},{5,7},{6,4},{7,5},{8,10},{9,11},{10,... | collective-permute-start | bytes 1572872 | tf_op jit(solution)/shard_map/ppermute | solution.py:200
  28.4 30.1 %collective-permute-start.4 = (bf16[1024,256]{1,0:T(8,128)(2,1)S(1)}, bf16[1024,256]{1,0:T(8,128)(2,1)S(1)}, u32[]{:S(2)}, u32[]{:S(2)}) collective-permute-start(bf16[1024,256]{1,0:T(8,128)(2,1)S(1)} %pad_maximum_fusion.2), channel_id=1, source_target_pairs={{0,3},{1,0},{2,1},{3,2},{4,7},{5,4},{6,5},{7,6},{8,11},{9,8},{10,9... | collective-permute-start | bytes 1572872 | tf_op jit(solution)/shard_map/ppermute | solution.py:200
  32.0 26.5 %collective-permute-start.3 = (bf16[1024,256]{1,0:T(8,128)(2,1)}, bf16[1024,256]{1,0:T(8,128)(2,1)S(1)}, u32[]{:S(2)}, u32[]{:S(2)}) collective-permute-start(bf16[1024,256]{1,0:T(8,128)(2,1)} %pad_maximum_fusion.1), channel_id=1, source_target_pairs={{0,1},{1,2},{2,3},{3,0},{4,5},{5,6},{6,7},{7,4},{8,9},{9,10},{10,1... | collective-permute-start | bytes 1572872 | tf_op jit(solution)/shard_map/ppermute | solution.py:200
  44.5 18.8 %collective-permute-start = (bf16[192,1024]{1,0:T(8,128)(2,1)S(1)}, bf16[192,1024]{1,0:T(8,128)(2,1)S(1)}, u32[]{:S(2)}, u32[]{:S(2)}) collective-permute-start(bf16[192,1024]{1,0:T(8,128)(2,1)S(1)} %wide_rows.1.refs_0_), channel_id=1, source_target_pairs={{0,4},{4,8},{8,12},{12,16},{16,20},{20,24},{24,28},{28,32},{32,36}... | collective-permute-start | bytes 1179656 | tf_op jit(solution)/shard_map/ppermute | solution.py:43
  53.6 12.3 %collective-permute-start.1 = (bf16[192,1024]{1,0:T(8,128)(2,1)S(1)}, bf16[192,1024]{1,0:T(8,128)(2,1)S(1)}, u32[]{:S(2)}, u32[]{:S(2)}) collective-permute-start(bf16[192,1024]{1,0:T(8,128)(2,1)S(1)} %wide_rows.1.refs_0_), channel_id=1, source_target_pairs={{0,60},{4,0},{8,4},{12,8},{16,12},{20,16},{24,20},{28,24},{32,28},... | collective-permute-start | bytes 1179656 | tf_op jit(solution)/shard_map/ppermute | solution.py:43
  55.5 18.6 %collective-permute-start.2 = (bf16[192,1024]{1,0:T(8,128)(2,1)S(1)}, bf16[192,1024]{1,0:T(8,128)(2,1)S(1)}, u32[]{:S(2)}, u32[]{:S(2)}) collective-permute-start(bf16[192,1024]{1,0:T(8,128)(2,1)S(1)} %wide_rows.1.refs_0_), channel_id=1, source_target_pairs={{0,8},{4,12},{8,16},{12,20},{16,24},{20,28},{24,32},{28,36},{32,40... | collective-permute-start | bytes 1179656 | tf_op jit(solution)/shard_map/ppermute | solution.py:43
  97.8 11.9 %copy-start = (bf16[1,512,1024]{2,1,0:T(8,128)(2,1)S(1)}, bf16[1,512,1024]{2,1,0:T(8,128)(2,1)}, u32[]{:S(2)}) copy-start(bf16[1,512,1024]{2,1,0:T(8,128)(2,1)} %param.15) | copy-start | bytes 3145732
  98.0 23.2 %copy-start.7 = (f32[16,2]{0,1:T(2,128)S(1)}, f32[16,2]{0,1:T(2,128)}, u32[]{:S(2)}) copy-start(f32[16,2]{0,1:T(2,128)} %param.12) | copy-start | bytes 388
  98.1 23.3 %copy-start.3 = (bf16[8,16,1024]{2,1,0:T(8,128)(2,1)S(1)}, bf16[8,16,1024]{2,1,0:T(8,128)(2,1)}, u32[]{:S(2)}) copy-start(bf16[8,16,1024]{2,1,0:T(8,128)(2,1)} %past_ref.1) | copy-start | bytes 786436
  98.1 23.3 %copy-start.4 = (s32[16,2]{0,1:T(2,128)S(1)}, s32[16,2]{0,1:T(2,128)}, u32[]{:S(2)}) copy-start(s32[16,2]{0,1:T(2,128)} %param.11) | copy-start | bytes 388
  98.1 23.3 %copy-start.5 = (f32[9]{0:T(128)S(1)}, f32[9]{0:T(128)}, u32[]{:S(2)}) copy-start(f32[9]{0:T(128)} %dwa_ref.1) | copy-start | bytes 112
  98.1 38.0 %copy-start.1 = (bf16[384,384]{1,0:T(8,128)(2,1)S(1)}, bf16[384,384]{1,0:T(8,128)(2,1)}, u32[]{:S(2)}) copy-start(bf16[384,384]{1,0:T(8,128)(2,1)} %constant.59.clone.order_ref) | copy-start | bytes 884740
  111.2 11.3 %collective-permute-start.6 = (bf16[192,1024]{1,0:T(8,128)(2,1)}, bf16[192,1024]{1,0:T(8,128)(2,1)S(1)}, u32[]{:S(2)}, u32[]{:S(2)}) collective-permute-start(bf16[192,1024]{1,0:T(8,128)(2,1)} %get-tuple-element.28), channel_id=1, source_target_pairs={{0,60},{4,0},{8,4},{12,8},{16,12},{20,16},{24,20},{28,24},{32,28},... | collective-permute-start | bytes 1179656 | tf_op jit(solution)/shard_map/ppermute | solution.py:43
  114.0 9.7 %collective-permute-start.7 = (bf16[192,1024]{1,0:T(8,128)(2,1)S(1)}, bf16[192,1024]{1,0:T(8,128)(2,1)S(1)}, u32[]{:S(2)}, u32[]{:S(2)}) collective-permute-start(bf16[192,1024]{1,0:T(8,128)(2,1)S(1)} %get-tuple-element.29), channel_id=1, source_target_pairs={{0,4},{4,8},{8,12},{12,16},{16,20},{20,24},{24,28},{28,32},{32,36}... | collective-permute-start | bytes 1179656 | tf_op jit(solution)/shard_map/ppermute | solution.py:43
  116.5 19.6 %collective-permute-start.8 = (bf16[192,1024]{1,0:T(8,128)(2,1)S(1)}, bf16[192,1024]{1,0:T(8,128)(2,1)S(1)}, u32[]{:S(2)}, u32[]{:S(2)}) collective-permute-start(bf16[192,1024]{1,0:T(8,128)(2,1)S(1)} %get-tuple-element.30), channel_id=1, source_target_pairs={{0,56},{4,60},{8,0},{12,4},{16,8},{20,12},{24,16},{28,20},{32,24},... | collective-permute-start | bytes 1179656 | tf_op jit(solution)/shard_map/ppermute | solution.py:43

commit v9 on v8

--- a/solution.py
+++ b/solution.py
@@ -43,16 +43,27 @@
     return lax.ppermute(shard, ("expert", "dp"), pairs)
 
 
-def from_neighbours(shard):
-    return [shifted(shard, 1, 1), shifted(shard, -1, -1), shifted(shard, 2, -2)]
-
-
-def to_neighbours(shards):
-    below, above, second = shards
-    return [shifted(below, -1, -1), shifted(above, 1, 1), shifted(second, -2, 2)]
-
-
-def call(kernel, name, out_shape, *operands, in_specs=None):
+def forward(shard):
+    return shifted(shard, 1, -1)
+
+
+def backward(shard):
+    return shifted(shard, -1, 1)
+
+
+def window_sets(own):
+    first, other = forward(own), backward(own)
+    return [own, first, other, forward(first)]
+
+
+def returned_sums(first, other, second):
+    relayed = backward(second)
+    other = forward(other)
+    first = (first + relayed.astype(jnp.float32)).astype(jnp.bfloat16)
+    return [backward(first), other]
+
+
+def call(kernel, out_shape, *operands, in_specs=None):
     many = isinstance(out_shape, list)
     return pl.pallas_call(
         kernel,
@@ -60,7 +71,6 @@
         in_specs=in_specs or [VMEM] * len(operands),
         out_specs=[VMEM] * len(out_shape) if many else VMEM,
         compiler_params=LIMIT,
-        name=name,
     )(*operands)
 
 
@@ -159,7 +169,7 @@
                 out_ref[group * rows : (group + 1) * rows, block * LANES : (block + 1) * LANES] = piece
 
     shape = jax.ShapeDtypeStruct((count * capacity, blocks * LANES), chunks.dtype)
-    return call(kernel, "wide_rows", shape, order, chunks)
+    return call(kernel, shape, order, chunks)
 
 
 def summed_chunks(own, others, order, capacity):
@@ -183,7 +193,7 @@
             out_ref[group * together : (group + 1) * together] = out
 
     shape = jax.ShapeDtypeStruct((total_rows // capacity, height, LANES), jnp.bfloat16)
-    return call(kernel, "summed_chunks", shape, order, own, *others)
+    return call(kernel, shape, order, own, *others)
 
 
 def weights_by_features(gate_weight, up_weight, quarter):
@@ -218,7 +228,7 @@
 
     shape = jax.ShapeDtypeStruct((parts, rows, width), jnp.bfloat16)
     specs = [SMEM] + [VMEM] * (len(sets) + parts)
-    return call(kernel, "gate_up_parts", shape, place, *sets, *weights, in_specs=specs)
+    return call(kernel, shape, place, *sets, *weights, in_specs=specs)
 
 
 def hidden_units(parts):
@@ -232,12 +242,12 @@
         gate, up = total[:, :width], total[:, width:]
         out_ref[...] = (gate / (1.0 + jnp.exp(-gate)) * up).astype(out_ref.dtype)
 
-    return call(kernel, "hidden_units", jax.ShapeDtypeStruct((rows, width), jnp.bfloat16), parts)
-
-
-def down_sets(hidden, w_down, count):
+    return call(kernel, jax.ShapeDtypeStruct((rows, width), jnp.bfloat16), parts)
+
+
+def down_sets(hidden, w_down, dtypes):
     parts, rows, _ = hidden.shape
-    set_rows = rows // count
+    set_rows = rows // len(dtypes)
     features = w_down.shape[1]
 
     def kernel(hidden_ref, w_ref, *out_refs):
@@ -246,11 +256,8 @@
         for place, ref in enumerate(out_refs):
             ref[...] = out[place * set_rows : (place + 1) * set_rows].astype(ref.dtype)
 
-    shapes = [
-        jax.ShapeDtypeStruct((set_rows, features), jnp.bfloat16 if place else jnp.float32)
-        for place in range(count)
-    ]
-    return call(kernel, "down_sets", shapes, hidden, w_down)
+    shapes = [jax.ShapeDtypeStruct((set_rows, features), dtype) for dtype in dtypes]
+    return call(kernel, shapes, hidden, w_down)
 
 
 def mix_terms(ids, route, own_columns, past_layers, dwa_weight, experts, capacity):
@@ -278,7 +285,7 @@
         jax.ShapeDtypeStruct((tok_rows, features), jnp.float32),
     ]
     operands = (dwa_weight, ids, route, own_columns, past_layers)
-    return call(kernel, "mix_terms", shapes, *operands, in_specs=[SMEM] + [VMEM] * 4)
+    return call(kernel, shapes, *operands, in_specs=[SMEM] + [VMEM] * 4)
 
 
 def mixed_layers(returned, terms, base, dtype):
@@ -304,7 +311,7 @@
             out_ref[:, lanes] = value.astype(out_ref.dtype)
 
     shape = jax.ShapeDtypeStruct((tok_rows, features), dtype)
-    return call(kernel, "mixed_layers", shape, terms, base, returned)
+    return call(kernel, shape, terms, base, returned)
 
 
 def per_device(
@@ -326,13 +333,13 @@
     packed, own_columns = packed_rows(in_hbm(ids), in_hbm(tokens), place * quarter, quarter, experts, capacity)
     arrived = far_exchange(packed)
     own_set = wide_rows(arrived, jnp.asarray(order, jnp.bfloat16), capacity)
-    sets = [own_set, *from_neighbours(own_set)]
+    sets = window_sets(own_set)
     partial = lax.all_to_all(gate_up_parts(sets, weights, place), "tensor", 0, 0, tiled=True)
     hidden = lax.all_gather(hidden_units(partial), "tensor", axis=0, tiled=False)
-    own, *others = down_sets(hidden, down_weight[0], len(sets))
+    own, *others = down_sets(hidden, down_weight[0], [jnp.float32] * 2 + [jnp.bfloat16] * 2)
     route, own = lax.optimization_barrier((route, own))
     terms, base = mix_terms(ids, route, own_columns, past_layers, dwa_weight, experts, capacity)
-    others = to_neighbours(others)
+    others = returned_sums(*others)
     own, terms, base = lax.optimization_barrier((own, terms, base))
     returned = far_exchange(summed_chunks(own, others, jnp.asarray(order.T, jnp.bfloat16), capacity))
     return mixed_layers(returned, terms, base, tokens.dtype)

time: 173 us -> 179 us (1.035)
  the two profiles are of different devices: /device:TPU:1 before, /device:TPU:65 now
where the time goes in v9:
time: 179 us; the launch traced here: 178 us
  blocking collectives  73.6 us (41%)
  waiting for transfers between devices  49.5 us (28%)
  starting transfers between devices  43.3 us (24%)
  Pallas kernels  7.9 us (4%)
  local copies, waits for them, and re-layouts  2.32 us (1%)
    all_to_all x1, blocking collectives, far_exchange(): lax.all_to_all(chunks, ('expert', 'dp'), 0, 0, tiled=True, axis_index_gro...  38.2 us
    all_to_all x1, waiting for transfers between devices, far_exchange(): lax.all_to_all(chunks, ('expert', 'dp'), 0, 0, tiled=True, axis_index_gro...  26.8 us
    all_to_all x1, blocking collectives, per_device(): lax.all_to_all(gate_up_parts(sets, weights, place), 'tensor', 0, 0, tiled...  23.6 us
    all_to_all x1, starting transfers between devices, far_exchange(): lax.all_to_all(chunks, ('expert', 'dp'), 0, 0, tiled=True, axis_index_gro...  16.8 us
    ppermute x6, starting transfers between devices, shifted(): return lax.ppermute(shard, ('expert', 'dp'), pairs)  16.6 us
    ppermute x6, waiting for transfers between devices, shifted(): return lax.ppermute(shard, ('expert', 'dp'), pairs)  11.8 us
    all_gather x1, blocking collectives, per_device(): lax.all_gather(hidden_units(partial), 'tensor', axis=0, tiled=False)  11.8 us
    ppermute x3, waiting for transfers between devices, slab(): lax.ppermute(both, 'tensor', [(i, (i + shift) % parts) for i in range(par...  11 us
  transfers between devices with their start and end apart: 10, of which 6 were waited for; matrix products, arithmetic and copies ran while one was open for 2% of the time, Pallas kernels for 1%

profile of v9, /device:TPU:65, one launch (start us, length us, event | category | flops | bytes accessed | tf_op | source)
XLA Modules:
  0.0 178.4 jit_solution(7736115331484980357)
XLA Ops:
  0.0 2.0 %packed_rows.1 = (bf16[32,48,128]{2,1,0:T(8,128)(2,1)}, bf16[16,1024]{1,0:T(8,128)(2,1)S(1)}) custom-call(s32[1]{0:T(128)S(6)} %mul.3.first_ref, s32[2,16]{1,0:T(2,128)} %bitcast.25, bf16[16,4096]{1,0:T(8,128)(2,1)} %tokens_ref.1), custom_call_target="tpu_custom_call" | custom-call | tf_op jit(solution)/shard_map/packed_rows/pallas_call | solution.py:137
  2.0 16.8 %all-to-all-start = ((bf16[32,48,128]{2,1,0:T(8,128)(2,1)}), bf16[32,48,128]{2,1,0:T(8,128)(2,1)S(1)}, u32[]{:S(2)}, u32[]{:S(2)}) async-start(bf16[32,48,128]{2,1,0:T(8,128)(2,1)} %get-tuple-element.18), calls=%async_computation | async-start | bytes 786432 | tf_op jit(solution)/shard_map/all_to_all | solution.py:33
  18.9 2.2 %dynamic-slice_bitcast_fusion = (bf16[1024,128]{1,0:T(8,128)(2,1)}, bf16[1024,128]{1,0:T(8,128)(2,1)S(1)}, bf16[1024,128]{1,0:T(8,128)(2,1)S(1)}, bf16[1024,128]...) fusion(bf16[4,1024,128]{2,1,0:T(8,128)(2,1)S(1)} %bitcast.27, ...), kind=kLoop, calls=%fused_computation.5 | loop fusion | bytes 4194320 | tf_op jit(solution)/shard_map/jit(dynamic_index_in_dim)/squeeze | solution.py:206
  21.0 26.8 %all-to-all-done.in_ref = bf16[32,48,128]{2,1,0:T(8,128)(2,1)S(1)} async-done(((bf16[32,48,128]{2,1,0:T(8,128)(2,1)}), bf16[32,48,128]{2,1,0:T(8,128)(2,1)S(1)}, u32[]{:S(2)}, u32[]{:S(2)}) %all-to-all-start) | async-done | bytes 393248 | tf_op jit(solution)/shard_map/all_to_all | solution.py:33
  47.8 0.5 shard_map.100.refs_0_
  48.3 2.6 %collective-permute-start = (bf16[192,1024]{1,0:T(8,128)(2,1)S(1)}, bf16[192,1024]{1,0:T(8,128)(2,1)S(1)}, u32[]{:S(2)}, u32[]{:S(2)}) collective-permute-start(bf16[192,1024]{1,0:T(8,128)(2,1)S(1)} %shard_map.100.refs_0_), channel_id=1, source_target_pairs={{0,4},{4,8},{8,12},{12,16},{16,20},{20,24},{24,28},{28,32},{32,36}... | collective-permute-start | bytes 1179656 | tf_op jit(solution)/shard_map/ppermute | solution.py:43
  50.9 1.1 pad_maximum_fusion.3
  52.0 4.6 %collective-permute-start.5 = (bf16[1024,256]{1,0:T(8,128)(2,1)S(1)}, bf16[1024,256]{1,0:T(8,128)(2,1)S(1)}, u32[]{:S(2)}, u32[]{:S(2)}) collective-permute-start(bf16[1024,256]{1,0:T(8,128)(2,1)S(1)} %pad_maximum_fusion.3), channel_id=1, source_target_pairs={{0,2},{1,3},{2,0},{3,1},{4,6},{5,7},{6,4},{7,5},{8,10},{9,11},{10,... | collective-permute-start | bytes 1572872 | tf_op jit(solution)/shard_map/ppermute | solution.py:210
  56.7 0.1 pad_maximum_fusion.2
  56.7 2.8 %collective-permute-start.4 = (bf16[1024,256]{1,0:T(8,128)(2,1)S(1)}, bf16[1024,256]{1,0:T(8,128)(2,1)S(1)}, u32[]{:S(2)}, u32[]{:S(2)}) collective-permute-start(bf16[1024,256]{1,0:T(8,128)(2,1)S(1)} %pad_maximum_fusion.2), channel_id=1, source_target_pairs={{0,3},{1,0},{2,1},{3,2},{4,7},{5,4},{6,5},{7,6},{8,11},{9,8},{10,9... | collective-permute-start | bytes 1572872 | tf_op jit(solution)/shard_map/ppermute | solution.py:210
  59.6 2.5 %collective-permute-start.3 = (bf16[1024,256]{1,0:T(8,128)(2,1)S(1)}, bf16[1024,256]{1,0:T(8,128)(2,1)S(1)}, u32[]{:S(2)}, u32[]{:S(2)}) collective-permute-start(bf16[1024,256]{1,0:T(8,128)(2,1)S(1)} %pad_maximum_fusion.1), channel_id=1, source_target_pairs={{0,1},{1,2},{2,3},{3,0},{4,5},{5,6},{6,7},{7,4},{8,9},{9,10},{10,1... | collective-permute-start | bytes 1572872 | tf_op jit(solution)/shard_map/ppermute | solution.py:210
  62.1 2.7 %collective-permute-start.1 = (bf16[192,1024]{1,0:T(8,128)(2,1)S(1)}, bf16[192,1024]{1,0:T(8,128)(2,1)S(1)}, u32[]{:S(2)}, u32[]{:S(2)}) collective-permute-start(bf16[192,1024]{1,0:T(8,128)(2,1)S(1)} %shard_map.100.refs_0_), channel_id=1, source_target_pairs={{0,60},{4,0},{8,4},{12,8},{16,12},{20,16},{24,20},{28,24},{32,28},... | collective-permute-start | bytes 1179656 | tf_op jit(solution)/shard_map/ppermute | solution.py:43
  64.8 2.6 %collective-permute-start.2 = (bf16[192,1024]{1,0:T(8,128)(2,1)S(1)}, bf16[192,1024]{1,0:T(8,128)(2,1)S(1)}, u32[]{:S(2)}, u32[]{:S(2)}) collective-permute-start(bf16[192,1024]{1,0:T(8,128)(2,1)S(1)} %collective-permute-done.refs_1_), channel_id=1, source_target_pairs={{0,4},{4,8},{8,12},{12,16},{16,20},{20,24},{24,28},{28,32},{32,36}... | collective-permute-start | bytes 1179656 | tf_op jit(solution)/shard_map/ppermute | solution.py:43
  67.5 1.6 collective-permute-done.5.refs_7_
  69.0 9.4 %collective-permute-done.4.refs_6_ = bf16[1024,256]{1,0:T(8,128)(2,1)S(1)} collective-permute-done((bf16[1024,256]{1,0:T(8,128)(2,1)S(1)}, bf16[1024,256]{1,0:T(8,128)(2,1)S(1)}, u32[]{:S(2)}, u32[]{:S(2)}) %collective-permute-start.4) | collective-permute-done | bytes 524320 | tf_op jit(solution)/shard_map/ppermute | solution.py:210
  78.4 1.9 %shard_map.101 = bf16[4,768,256]{2,1,0:T(8,128)(2,1)S(1)} custom-call(s32[1]{0:T(128)} %bitcast.1.place_ref, bf16[192,1024]{1,0:T(8,128)(2,1)S(1)} %shard_map.100.refs_0_, bf16[192,1024]{1,0:T(8,128)(2,1)S(1)} %collective-permute-done.refs_1_, bf16[192,1024]{1,0:T(8,128)(2,1)S(1)} %collective-permute-done.1.refs_2_, ...), custom_call_target="tpu_custom_call" | custom-call | tf_op jit(solution)/shard_map/pallas_call | solution.py:68
  80.3 23.6 %all_to_all.15.in_ref = bf16[4,768,256]{2,1,0:T(8,128)(2,1)S(1)} all-to-all(bf16[4,768,256]{2,1,0:T(8,128)(2,1)S(1)} %shard_map.101), channel_id=1, replica_groups=mesh['expert'=8,'dp'=16,'tensor'=4] {'tensor'}, dimensions={0} | all-to-all | bytes 3145728 | tf_op jit(solution)/shard_map/all_to_all | solution.py:337
  103.9 0.3 shard_map.102
  104.2 11.8 %all-gather = bf16[3072,128]{1,0:T(8,128)(2,1)S(1)} all-gather(bf16[768,128]{1,0:T(8,128)(2,1)S(1)} %shard_map.102), channel_id=2, replica_groups=mesh['expert'=8,'dp'=16,'tensor'=4] {'tensor'}, dimensions={0}, use_global_device_ids=true | all-gather | bytes 983040 | tf_op jit(solution)/shard_map/all_gather | solution.py:338
  116.0 1.0 shard_map.103
  117.0 3.5 %collective-permute-start.6 = (bf16[192,1024]{1,0:T(8,128)(2,1)S(1)}, bf16[192,1024]{1,0:T(8,128)(2,1)S(1)}, u32[]{:S(2)}, u32[]{:S(2)}) collective-permute-start(bf16[192,1024]{1,0:T(8,128)(2,1)S(1)} %get-tuple-element.29), channel_id=1, source_target_pairs={{0,60},{4,0},{8,4},{12,8},{16,12},{20,16},{24,20},{28,24},{32,28},... | collective-permute-start | bytes 1179656 | tf_op jit(solution)/shard_map/ppermute | solution.py:43
  120.5 2.2 %collective-permute-start.8 = (bf16[192,1024]{1,0:T(8,128)(2,1)S(1)}, bf16[192,1024]{1,0:T(8,128)(2,1)S(1)}, u32[]{:S(2)}, u32[]{:S(2)}) collective-permute-start(bf16[192,1024]{1,0:T(8,128)(2,1)S(1)} %get-tuple-element.30), channel_id=1, source_target_pairs={{0,4},{4,8},{8,12},{12,16},{16,20},{20,24},{24,28},{28,32},{32,36}... | collective-permute-start | bytes 1179656 | tf_op jit(solution)/shard_map/ppermute | solution.py:43
  122.7 3.2 %collective-permute-done.6 = bf16[192,1024]{1,0:T(8,128)(2,1)S(1)} collective-permute-done((bf16[192,1024]{1,0:T(8,128)(2,1)S(1)}, bf16[192,1024]{1,0:T(8,128)(2,1)S(1)}, u32[]{:S(2)}, u32[]{:S(2)}) %collective-permute-start.6) | collective-permute-done | bytes 393248 | tf_op jit(solution)/shard_map/ppermute | solution.py:43
  125.9 0.1 add_convert_fusion
  126.0 3.1 %collective-permute-start.7 = (bf16[192,1024]{1,0:T(8,128)(2,1)S(1)}, bf16[192,1024]{1,0:T(8,128)(2,1)S(1)}, u32[]{:S(2)}, u32[]{:S(2)}) collective-permute-start(bf16[192,1024]{1,0:T(8,128)(2,1)S(1)} %add_convert_fusion), channel_id=1, source_target_pairs={{0,60},{4,0},{8,4},{12,8},{16,12},{20,16},{24,20},{28,24},{32,28},... | collective-permute-start | bytes 1179656 | tf_op jit(solution)/shard_map/ppermute | solution.py:43
  129.1 0.1 tile.10.route_ref
  129.2 0.9 shard_map.104
  130.2 2.0 %collective-permute-done.8.refs_1_ = bf16[192,1024]{1,0:T(8,128)(2,1)S(1)} collective-permute-done((bf16[192,1024]{1,0:T(8,128)(2,1)S(1)}, bf16[192,1024]{1,0:T(8,128)(2,1)S(1)}, u32[]{:S(2)}, u32[]{:S(2)}) %collective-permute-start.8) | collective-permute-done | bytes 393248 | tf_op jit(solution)/shard_map/ppermute | solution.py:43
  132.2 6.6 %collective-permute-done.7.refs_0_ = bf16[192,1024]{1,0:T(8,128)(2,1)S(1)} collective-permute-done((bf16[192,1024]{1,0:T(8,128)(2,1)S(1)}, bf16[192,1024]{1,0:T(8,128)(2,1)S(1)}, u32[]{:S(2)}, u32[]{:S(2)}) %collective-permute-start.7) | collective-permute-done | bytes 393248 | tf_op jit(solution)/shard_map/ppermute | solution.py:43
  138.7 0.5 shard_map.105
  139.2 38.2 %all_to_all.16.in_ref = bf16[32,48,128]{2,1,0:T(8,128)(2,1)S(1)} all-to-all(bf16[32,48,128]{2,1,0:T(8,128)(2,1)S(1)} %shard_map.105), channel_id=1, replica_groups={{0,16,32,48,64,80,96,112,128,144,160,176,192,208,224,240,256,272,288,30..., dimensions={0} | all-to-all | bytes 786432 | tf_op jit(solution)/shard_map/all_to_all | solution.py:33
  177.5 0.9 shard_map.106
  (23 shorter events, 0.2 us)
Async XLA Ops:
  0.0 18.8 %copy-start.6 = (bf16[1,4096,128]{2,1,0:T(8,128)(2,1)S(1)}, bf16[1,4096,128]{2,1,0:T(8,128)(2,1)}, u32[]{:S(2)}) copy-start(bf16[1,4096,128]{2,1,0:T(8,128)(2,1)} %param.14) | copy-start | bytes 3145732
  2.0 45.8 %all-to-all-start = ((bf16[32,48,128]{2,1,0:T(8,128)(2,1)}), bf16[32,48,128]{2,1,0:T(8,128)(2,1)S(1)}, u32[]{:S(2)}, u32[]{:S(2)}) async-start(bf16[32,48,128]{2,1,0:T(8,128)(2,1)} %get-tuple-element.18), calls=%async_computation | async-start | bytes 786432 | tf_op jit(solution)/shard_map/all_to_all | solution.py:33
  18.8 29.0 %copy-start.2 = (bf16[384,384]{1,0:T(8,128)(2,1)S(1)}, bf16[384,384]{1,0:T(8,128)(2,1)}, u32[]{:S(2)}) copy-start(bf16[384,384]{1,0:T(8,128)(2,1)} %constant.58.clone.order_ref) | copy-start | bytes 884740
  48.3 16.5 %collective-permute-start = (bf16[192,1024]{1,0:T(8,128)(2,1)S(1)}, bf16[192,1024]{1,0:T(8,128)(2,1)S(1)}, u32[]{:S(2)}, u32[]{:S(2)}) collective-permute-start(bf16[192,1024]{1,0:T(8,128)(2,1)S(1)} %shard_map.100.refs_0_), channel_id=1, source_target_pairs={{0,4},{4,8},{8,12},{12,16},{16,20},{20,24},{24,28},{28,32},{32,36}... | collective-permute-start | bytes 1179656 | tf_op jit(solution)/shard_map/ppermute | solution.py:43
  52.0 17.0 %collective-permute-start.5 = (bf16[1024,256]{1,0:T(8,128)(2,1)S(1)}, bf16[1024,256]{1,0:T(8,128)(2,1)S(1)}, u32[]{:S(2)}, u32[]{:S(2)}) collective-permute-start(bf16[1024,256]{1,0:T(8,128)(2,1)S(1)} %pad_maximum_fusion.3), channel_id=1, source_target_pairs={{0,2},{1,3},{2,0},{3,1},{4,6},{5,7},{6,4},{7,5},{8,10},{9,11},{10,... | collective-permute-start | bytes 1572872 | tf_op jit(solution)/shard_map/ppermute | solution.py:210
  56.7 21.7 %collective-permute-start.4 = (bf16[1024,256]{1,0:T(8,128)(2,1)S(1)}, bf16[1024,256]{1,0:T(8,128)(2,1)S(1)}, u32[]{:S(2)}, u32[]{:S(2)}) collective-permute-start(bf16[1024,256]{1,0:T(8,128)(2,1)S(1)} %pad_maximum_fusion.2), channel_id=1, source_target_pairs={{0,3},{1,0},{2,1},{3,2},{4,7},{5,4},{6,5},{7,6},{8,11},{9,8},{10,9... | collective-permute-start | bytes 1572872 | tf_op jit(solution)/shard_map/ppermute | solution.py:210
  59.6 18.8 %collective-permute-start.3 = (bf16[1024,256]{1,0:T(8,128)(2,1)S(1)}, bf16[1024,256]{1,0:T(8,128)(2,1)S(1)}, u32[]{:S(2)}, u32[]{:S(2)}) collective-permute-start(bf16[1024,256]{1,0:T(8,128)(2,1)S(1)} %pad_maximum_fusion.1), channel_id=1, source_target_pairs={{0,1},{1,2},{2,3},{3,0},{4,5},{5,6},{6,7},{7,4},{8,9},{9,10},{10,1... | collective-permute-start | bytes 1572872 | tf_op jit(solution)/shard_map/ppermute | solution.py:210
  62.1 16.3 %collective-permute-start.1 = (bf16[192,1024]{1,0:T(8,128)(2,1)S(1)}, bf16[192,1024]{1,0:T(8,128)(2,1)S(1)}, u32[]{:S(2)}, u32[]{:S(2)}) collective-permute-start(bf16[192,1024]{1,0:T(8,128)(2,1)S(1)} %shard_map.100.refs_0_), channel_id=1, source_target_pairs={{0,60},{4,0},{8,4},{12,8},{16,12},{20,16},{24,20},{28,24},{32,28},... | collective-permute-start | bytes 1179656 | tf_op jit(solution)/shard_map/ppermute | solution.py:43
  64.8 13.6 %collective-permute-start.2 = (bf16[192,1024]{1,0:T(8,128)(2,1)S(1)}, bf16[192,1024]{1,0:T(8,128)(2,1)S(1)}, u32[]{:S(2)}, u32[]{:S(2)}) collective-permute-start(bf16[192,1024]{1,0:T(8,128)(2,1)S(1)} %collective-permute-done.refs_1_), channel_id=1, source_target_pairs={{0,4},{4,8},{8,12},{12,16},{16,20},{20,24},{24,28},{28,32},{32,36}... | collective-permute-start | bytes 1179656 | tf_op jit(solution)/shard_map/ppermute | solution.py:43
  103.9 12.1 %copy-start = (bf16[1,512,1024]{2,1,0:T(8,128)(2,1)S(1)}, bf16[1,512,1024]{2,1,0:T(8,128)(2,1)}, u32[]{:S(2)}) copy-start(bf16[1,512,1024]{2,1,0:T(8,128)(2,1)} %param.15) | copy-start | bytes 3145732
  116.0 13.1 %copy-start.7 = (f32[16,2]{0,1:T(2,128)S(1)}, f32[16,2]{0,1:T(2,128)}, u32[]{:S(2)}) copy-start(f32[16,2]{0,1:T(2,128)} %param.12) | copy-start | bytes 388
  116.0 13.2 %copy-start.3 = (bf16[8,16,1024]{2,1,0:T(8,128)(2,1)S(1)}, bf16[8,16,1024]{2,1,0:T(8,128)(2,1)}, u32[]{:S(2)}) copy-start(bf16[8,16,1024]{2,1,0:T(8,128)(2,1)} %past_ref.1) | copy-start | bytes 786436
  116.0 13.2 %copy-start.4 = (s32[16,2]{0,1:T(2,128)S(1)}, s32[16,2]{0,1:T(2,128)}, u32[]{:S(2)}) copy-start(s32[16,2]{0,1:T(2,128)} %param.11) | copy-start | bytes 388
  116.0 13.2 %copy-start.5 = (f32[9]{0:T(128)S(1)}, f32[9]{0:T(128)}, u32[]{:S(2)}) copy-start(f32[9]{0:T(128)} %dwa_ref.1) | copy-start | bytes 112
  116.0 22.7 %copy-start.1 = (bf16[384,384]{1,0:T(8,128)(2,1)S(1)}, bf16[384,384]{1,0:T(8,128)(2,1)}, u32[]{:S(2)}) copy-start(bf16[384,384]{1,0:T(8,128)(2,1)} %constant.59.clone.order_ref) | copy-start | bytes 884740
  117.0 8.9 %collective-permute-start.6 = (bf16[192,1024]{1,0:T(8,128)(2,1)S(1)}, bf16[192,1024]{1,0:T(8,128)(2,1)S(1)}, u32[]{:S(2)}, u32[]{:S(2)}) collective-permute-start(bf16[192,1024]{1,0:T(8,128)(2,1)S(1)} %get-tuple-element.29), channel_id=1, source_target_pairs={{0,60},{4,0},{8,4},{12,8},{16,12},{20,16},{24,20},{28,24},{32,28},... | collective-permute-start | bytes 1179656 | tf_op jit(solution)/shard_map/ppermute | solution.py:43
  120.5 11.7 %collective-permute-start.8 = (bf16[192,1024]{1,0:T(8,128)(2,1)S(1)}, bf16[192,1024]{1,0:T(8,128)(2,1)S(1)}, u32[]{:S(2)}, u32[]{:S(2)}) collective-permute-start(bf16[192,1024]{1,0:T(8,128)(2,1)S(1)} %get-tuple-element.30), channel_id=1, source_target_pairs={{0,4},{4,8},{8,12},{12,16},{16,20},{20,24},{24,28},{28,32},{32,36}... | collective-permute-start | bytes 1179656 | tf_op jit(solution)/shard_map/ppermute | solution.py:43
  126.0 12.7 %collective-permute-start.7 = (bf16[192,1024]{1,0:T(8,128)(2,1)S(1)}, bf16[192,1024]{1,0:T(8,128)(2,1)S(1)}, u32[]{:S(2)}, u32[]{:S(2)}) collective-permute-start(bf16[192,1024]{1,0:T(8,128)(2,1)S(1)} %add_convert_fusion), channel_id=1, source_target_pairs={{0,60},{4,0},{8,4},{12,8},{16,12},{20,16},{24,20},{28,24},{32,28},... | collective-permute-start | bytes 1179656 | tf_op jit(solution)/shard_map/ppermute | solution.py:43

commit v10 on v9

--- a/solution.py
+++ b/solution.py
@@ -9,7 +9,6 @@
 RADIX = 4
 LANES = 128
 TERMS = 3
-SHIFTS = (0, 1, 3, 2)
 LIMIT = pltpu.CompilerParams(vmem_limit_bytes=16 * 2**20)
 HBM = pl.BlockSpec(memory_space=pltpu.HBM)
 SMEM = pl.BlockSpec(memory_space=pltpu.SMEM)
@@ -196,53 +195,73 @@
     return call(kernel, shape, order, own, *others)
 
 
+def along_tensor(shard, even_shift, odd_shift):
+    experts, count = lax.axis_size("expert"), lax.axis_size("tensor")
+    pairs = []
+    for expert in range(experts):
+        shift = odd_shift if expert % 2 else even_shift
+        for place in range(count):
+            pairs.append((expert * count + place, expert * count + (place + shift) % count))
+    return lax.ppermute(shard, ("expert", "tensor"), pairs)
+
+
 def weights_by_features(gate_weight, up_weight, quarter):
     parts = lax.axis_size("tensor")
     here = lax.axis_index("tensor")
+    step = jnp.where(lax.axis_index("expert") % 2 == 0, 1, parts - 1)
     slabs = [w.reshape(parts, quarter, -1) for w in (gate_weight, up_weight)]
 
     def slab(shift):
         place = (here + shift) % parts
         both = [lax.dynamic_index_in_dim(w, place, 0, keepdims=False) for w in slabs]
-        both = jnp.concatenate(both, axis=1)
-        if shift == 0:
-            return both
-        return lax.ppermute(both, "tensor", [(i, (i + shift) % parts) for i in range(parts)])
-
-    return [slab(shift) for shift in SHIFTS]
-
-
-def gate_up_parts(sets, weights, place):
-    parts = len(weights)
+        return jnp.concatenate(both, axis=1)
+
+    moves = [(parts - step, -1, 1), (step, 1, -1), (parts // 2, 2, 2)]
+    weights = [slab(0)]
+    for shift, even, odd in moves:
+        weights.append(along_tensor(slab(shift), even, odd))
+    return weights
+
+
+def gate_up_parts(sets, weights):
     width = weights[0].shape[1]
     set_rows = sets[0].shape[0]
     rows = set_rows * len(sets)
 
-    def kernel(place_ref, *refs):
-        set_refs, w_refs, out_ref = refs[: len(sets)], refs[len(sets) : -1], refs[-1]
+    def kernel(*refs):
+        set_refs, refs = refs[: len(sets)], refs[len(sets) :]
+        w_refs, out_refs = refs[: len(weights)], refs[len(weights) :]
         stacked = jnp.concatenate([ref[...] for ref in set_refs], axis=0)
-        for shift, w_ref in zip(SHIFTS, w_refs):
-            part = (place_ref[0] + (parts - shift)) % parts
+        for w_ref, out_ref in zip(w_refs, out_refs):
             out = jnp.dot(stacked, w_ref[...], preferred_element_type=jnp.float32)
-            out_ref[part] = out.astype(out_ref.dtype)
-
-    shape = jax.ShapeDtypeStruct((parts, rows, width), jnp.bfloat16)
-    specs = [SMEM] + [VMEM] * (len(sets) + parts)
-    return call(kernel, shape, place, *sets, *weights, in_specs=specs)
-
-
-def hidden_units(parts):
-    count, rows, both = parts.shape
+            out_ref[...] = out.astype(out_ref.dtype)
+
+    dtypes = [jnp.float32] * 2 + [jnp.bfloat16] * 2
+    shapes = [jax.ShapeDtypeStruct((rows, width), dtype) for dtype in dtypes]
+    return call(kernel, shapes, *sets, *weights)
+
+
+def tensor_sums(following, previous, opposite):
+    relayed = along_tensor(opposite, 1, -1)
+    previous = along_tensor(previous, -1, 1)
+    following = (following + relayed.astype(jnp.float32)).astype(jnp.bfloat16)
+    return [along_tensor(following, 1, -1), previous]
+
+
+def hidden_units(own, others):
+    rows, both = own.shape
     width = both // 2
 
-    def kernel(in_ref, out_ref):
-        total = in_ref[0].astype(jnp.float32)
-        for part in range(1, count):
-            total += in_ref[part].astype(jnp.float32)
+    def kernel(own_ref, *refs):
+        other_refs, out_ref = refs[:-1], refs[-1]
+        total = own_ref[...]
+        for ref in other_refs:
+            total += ref[...].astype(jnp.float32)
         gate, up = total[:, :width], total[:, width:]
         out_ref[...] = (gate / (1.0 + jnp.exp(-gate)) * up).astype(out_ref.dtype)
 
-    return call(kernel, jax.ShapeDtypeStruct((rows, width), jnp.bfloat16), parts)
+    shape = jax.ShapeDtypeStruct((rows, width), jnp.bfloat16)
+    return call(kernel, shape, own, *others)
 
 
 def down_sets(hidden, w_down, dtypes):
@@ -334,8 +353,8 @@
     arrived = far_exchange(packed)
     own_set = wide_rows(arrived, jnp.asarray(order, jnp.bfloat16), capacity)
     sets = window_sets(own_set)
-    partial = lax.all_to_all(gate_up_parts(sets, weights, place), "tensor", 0, 0, tiled=True)
-    hidden = lax.all_gather(hidden_units(partial), "tensor", axis=0, tiled=False)
+    own, *others = gate_up_parts(sets, weights)
+    hidden = lax.all_gather(hidden_units(own, tensor_sums(*others)), "tensor", axis=0, tiled=False)
     own, *others = down_sets(hidden, down_weight[0], [jnp.float32] * 2 + [jnp.bfloat16] * 2)
     route, own = lax.optimization_barrier((route, own))
     terms, base = mix_terms(ids, route, own_columns, past_layers, dwa_weight, experts, capacity)

time: 179 us -> 175 us (0.978)
  the two profiles are of different devices: /device:TPU:65 before, /device:TPU:75 now
where the time goes in v10:
time: 175 us
  waiting for transfers between devices  58.2 us (33%)
  blocking collectives  54.9 us (31%)
  starting transfers between devices  50.7 us (29%)
  Pallas kernels  7.73 us (4%)
  local copies, waits for them, and re-layouts  2.3 us (1%)
    all_to_all x1, blocking collectives, far_exchange(): lax.all_to_all(chunks, ('expert', 'dp'), 0, 0, tiled=True, axis_index_gro...  40.1 us
    all_to_all x1, waiting for transfers between devices, far_exchange(): lax.all_to_all(chunks, ('expert', 'dp'), 0, 0, tiled=True, axis_index_gro...  25.8 us
    ppermute x6, waiting for transfers between devices, along_tensor(): return lax.ppermute(shard, ('expert', 'tensor'), pairs)  21.8 us
    ppermute x6, starting transfers between devices, along_tensor(): return lax.ppermute(shard, ('expert', 'tensor'), pairs)  17.6 us
    all_to_all x1, starting transfers between devices, far_exchange(): lax.all_to_all(chunks, ('expert', 'dp'), 0, 0, tiled=True, axis_index_gro...  16.8 us
    ppermute x6, starting transfers between devices, shifted(): return lax.ppermute(shard, ('expert', 'dp'), pairs)  16.2 us
    all_gather x1, blocking collectives, per_device(): lax.all_gather(hidden_units(own, tensor_sums(*others)), 'tensor', axis=0,...  14.8 us
    ppermute x6, waiting for transfers between devices, shifted(): return lax.ppermute(shard, ('expert', 'dp'), pairs)  10.6 us
  transfers between devices with their start and end apart: 13, of which 10 were waited for; matrix products, arithmetic and copies ran while one was open for 2% of the time, Pallas kernels for 1%

profile of v10, /device:TPU:75, one launch (start us, length us, event | category | flops | bytes accessed | tf_op | source)
XLA Modules:
  0.0 174.6 jit_solution(16297491840159501182)
XLA Ops:
  0.0 2.0 %packed_rows.1 = (bf16[32,48,128]{2,1,0:T(8,128)(2,1)}, bf16[16,1024]{1,0:T(8,128)(2,1)S(1)}) custom-call(s32[1]{0:T(128)} %bitcast.1.first_ref, s32[2,16]{1,0:T(2,128)} %bitcast.25, bf16[16,4096]{1,0:T(8,128)(2,1)} %tokens_ref.1), custom_call_target="tpu_custom_call" | custom-call | tf_op jit(solution)/shard_map/packed_rows/pallas_call | solution.py:136
  2.0 16.8 %all-to-all-start = ((bf16[32,48,128]{2,1,0:T(8,128)(2,1)}), bf16[32,48,128]{2,1,0:T(8,128)(2,1)S(1)}, u32[]{:S(2)}, u32[]{:S(2)}) async-start(bf16[32,48,128]{2,1,0:T(8,128)(2,1)} %get-tuple-element.22), calls=%async_computation | async-start | bytes 786432 | tf_op jit(solution)/shard_map/all_to_all | solution.py:32
  18.9 2.2 %dynamic-slice_bitcast_fusion = (bf16[1024,128]{1,0:T(8,128)(2,1)}, bf16[1024,128]{1,0:T(8,128)(2,1)S(1)}, bf16[1024,128]{1,0:T(8,128)(2,1)S(1)}, bf16[1024,128]...) fusion(bf16[4,1024,128]{2,1,0:T(8,128)(2,1)S(1)} %bitcast.27, ...), kind=kLoop, calls=%fused_computation.6 | loop fusion | bytes 4194320 | tf_op jit(solution)/shard_map/jit(dynamic_index_in_dim)/squeeze | solution.py:216
  21.1 25.8 %all-to-all-done.in_ref = bf16[32,48,128]{2,1,0:T(8,128)(2,1)S(1)} async-done(((bf16[32,48,128]{2,1,0:T(8,128)(2,1)}), bf16[32,48,128]{2,1,0:T(8,128)(2,1)S(1)}, u32[]{:S(2)}, u32[]{:S(2)}) %all-to-all-start) | async-done | bytes 393248 | tf_op jit(solution)/shard_map/all_to_all | solution.py:32
  46.9 0.5 shard_map.100.refs_0_
  47.4 2.6 %collective-permute-start = (bf16[192,1024]{1,0:T(8,128)(2,1)S(1)}, bf16[192,1024]{1,0:T(8,128)(2,1)S(1)}, u32[]{:S(2)}, u32[]{:S(2)}) collective-permute-start(bf16[192,1024]{1,0:T(8,128)(2,1)S(1)} %shard_map.100.refs_0_), channel_id=1, source_target_pairs={{0,4},{4,8},{8,12},{12,16},{16,20},{20,24},{24,28},{28,32},{32,36}... | collective-permute-start | bytes 1179656 | tf_op jit(solution)/shard_map/ppermute | solution.py:42
  50.1 3.8 %collective-permute-start.5 = (bf16[1024,256]{1,0:T(8,128)(2,1)S(1)}, bf16[1024,256]{1,0:T(8,128)(2,1)S(1)}, u32[]{:S(2)}, u32[]{:S(2)}) collective-permute-start(bf16[1024,256]{1,0:T(8,128)(2,1)S(1)} %pad_maximum_fusion.3), channel_id=1, source_target_pairs={{0,2},{1,3},{2,0},{3,1},{64,66},{65,67},{66,64},{67,65},{128,130},... | collective-permute-start | bytes 1572872 | tf_op jit(solution)/shard_map/ppermute | solution.py:205
  53.9 3.1 %collective-permute-start.4 = (bf16[1024,256]{1,0:T(8,128)(2,1)S(1)}, bf16[1024,256]{1,0:T(8,128)(2,1)S(1)}, u32[]{:S(2)}, u32[]{:S(2)}) collective-permute-start(bf16[1024,256]{1,0:T(8,128)(2,1)S(1)} %pad_maximum_fusion.2), channel_id=1, source_target_pairs={{0,1},{1,2},{2,3},{3,0},{64,67},{65,64},{66,65},{67,66},{128,129},... | collective-permute-start | bytes 1572872 | tf_op jit(solution)/shard_map/ppermute | solution.py:205
  57.1 2.2 %collective-permute-start.3 = (bf16[1024,256]{1,0:T(8,128)(2,1)S(1)}, bf16[1024,256]{1,0:T(8,128)(2,1)S(1)}, u32[]{:S(2)}, u32[]{:S(2)}) collective-permute-start(bf16[1024,256]{1,0:T(8,128)(2,1)S(1)} %pad_maximum_fusion.1), channel_id=1, source_target_pairs={{0,3},{1,0},{2,1},{3,2},{64,65},{65,66},{66,67},{67,64},{128,131},... | collective-permute-start | bytes 1572872 | tf_op jit(solution)/shard_map/ppermute | solution.py:205
  59.3 2.7 %collective-permute-start.1 = (bf16[192,1024]{1,0:T(8,128)(2,1)S(1)}, bf16[192,1024]{1,0:T(8,128)(2,1)S(1)}, u32[]{:S(2)}, u32[]{:S(2)}) collective-permute-start(bf16[192,1024]{1,0:T(8,128)(2,1)S(1)} %shard_map.100.refs_0_), channel_id=1, source_target_pairs={{0,60},{4,0},{8,4},{12,8},{16,12},{20,16},{24,20},{28,24},{32,28},... | collective-permute-start | bytes 1179656 | tf_op jit(solution)/shard_map/ppermute | solution.py:42
  62.0 2.6 %collective-permute-start.2 = (bf16[192,1024]{1,0:T(8,128)(2,1)S(1)}, bf16[192,1024]{1,0:T(8,128)(2,1)S(1)}, u32[]{:S(2)}, u32[]{:S(2)}) collective-permute-start(bf16[192,1024]{1,0:T(8,128)(2,1)S(1)} %collective-permute-done.refs_1_), channel_id=1, source_target_pairs={{0,4},{4,8},{8,12},{12,16},{16,20},{20,24},{24,28},{28,32},{32,36}... | collective-permute-start | bytes 1179656 | tf_op jit(solution)/shard_map/ppermute | solution.py:42
  64.7 2.5 %collective-permute-done.5.refs_7_ = bf16[1024,256]{1,0:T(8,128)(2,1)S(1)} collective-permute-done((bf16[1024,256]{1,0:T(8,128)(2,1)S(1)}, bf16[1024,256]{1,0:T(8,128)(2,1)S(1)}, u32[]{:S(2)}, u32[]{:S(2)}) %collective-permute-start.5) | collective-permute-done | bytes 524320 | tf_op jit(solution)/shard_map/ppermute | solution.py:205
  67.2 10.1 %collective-permute-done.4.refs_6_ = bf16[1024,256]{1,0:T(8,128)(2,1)S(1)} collective-permute-done((bf16[1024,256]{1,0:T(8,128)(2,1)S(1)}, bf16[1024,256]{1,0:T(8,128)(2,1)S(1)}, u32[]{:S(2)}, u32[]{:S(2)}) %collective-permute-start.4) | collective-permute-done | bytes 524320 | tf_op jit(solution)/shard_map/ppermute | solution.py:205
  77.4 1.8 %shard_map.101 = (f32[768,256]{1,0:T(8,128)S(1)}, f32[768,256]{1,0:T(8,128)S(1)}, bf16[768,256]{1,0:T(8,128)(2,1)S(1)}, bf16[768,256]{1,0:T(8,128)(2,1)S(1)}) custom-call(bf16[192,1024]{1,0:T(8,128)(2,1)S(1)} %shard_map.100.refs_0_, bf16[192,1024]{1,0:T(8,128)(2,1)S(1)} %collective-permute-done.refs_1_, ...), custom_call_target="tpu_custom_call" | custom-call | tf_op jit(solution)/shard_map/pallas_call | solution.py:67
  79.2 2.1 %collective-permute-start.6 = (bf16[768,256]{1,0:T(8,128)(2,1)S(1)}, bf16[768,256]{1,0:T(8,128)(2,1)S(1)}, u32[]{:S(2)}, u32[]{:S(2)}) collective-permute-start(bf16[768,256]{1,0:T(8,128)(2,1)S(1)} %get-tuple-element.25), channel_id=1, source_target_pairs={{0,1},{1,2},{2,3},{3,0},{64,67},{65,64},{66,65},{67,66},{128,129},... | collective-permute-start | bytes 1179656 | tf_op jit(solution)/shard_map/ppermute | solution.py:205
  81.3 3.2 %collective-permute-start.8 = (bf16[768,256]{1,0:T(8,128)(2,1)S(1)}, bf16[768,256]{1,0:T(8,128)(2,1)S(1)}, u32[]{:S(2)}, u32[]{:S(2)}) collective-permute-start(bf16[768,256]{1,0:T(8,128)(2,1)S(1)} %get-tuple-element.26), channel_id=1, source_target_pairs={{0,3},{1,0},{2,1},{3,2},{64,65},{65,66},{66,67},{67,64},{128,131},... | collective-permute-start | bytes 1179656 | tf_op jit(solution)/shard_map/ppermute | solution.py:205
  84.5 3.6 %collective-permute-done.6 = bf16[768,256]{1,0:T(8,128)(2,1)S(1)} collective-permute-done((bf16[768,256]{1,0:T(8,128)(2,1)S(1)}, bf16[768,256]{1,0:T(8,128)(2,1)S(1)}, u32[]{:S(2)}, u32[]{:S(2)}) %collective-permute-start.6) | collective-permute-done | bytes 393248 | tf_op jit(solution)/shard_map/ppermute | solution.py:205
  88.2 3.3 %collective-permute-start.7 = (bf16[768,256]{1,0:T(8,128)(2,1)S(1)}, bf16[768,256]{1,0:T(8,128)(2,1)S(1)}, u32[]{:S(2)}, u32[]{:S(2)}) collective-permute-start(bf16[768,256]{1,0:T(8,128)(2,1)S(1)} %add_convert_fusion.1), channel_id=1, source_target_pairs={{0,1},{1,2},{2,3},{3,0},{64,67},{65,64},{66,65},{67,66},{128,129},... | collective-permute-start | bytes 1179656 | tf_op jit(solution)/shard_map/ppermute | solution.py:205
  91.4 1.4 collective-permute-done.8.refs_1_
  92.8 4.2 %collective-permute-done.7.refs_0_ = bf16[768,256]{1,0:T(8,128)(2,1)S(1)} collective-permute-done((bf16[768,256]{1,0:T(8,128)(2,1)S(1)}, bf16[768,256]{1,0:T(8,128)(2,1)S(1)}, u32[]{:S(2)}, u32[]{:S(2)}) %collective-permute-start.7) | collective-permute-done | bytes 393248 | tf_op jit(solution)/shard_map/ppermute | solution.py:205
  97.2 14.8 %all-gather = bf16[3072,128]{1,0:T(8,128)(2,1)S(1)} all-gather(bf16[768,128]{1,0:T(8,128)(2,1)S(1)} %shard_map.102), channel_id=2, replica_groups=mesh['expert'=8,'dp'=16,'tensor'=4] {'tensor'}, dimensions={0}, use_global_device_ids=true | all-gather | bytes 983040 | tf_op jit(solution)/shard_map/all_gather | solution.py:357
  112.0 1.0 shard_map.103
  113.0 3.2 %collective-permute-start.9 = (bf16[192,1024]{1,0:T(8,128)(2,1)S(1)}, bf16[192,1024]{1,0:T(8,128)(2,1)S(1)}, u32[]{:S(2)}, u32[]{:S(2)}) collective-permute-start(bf16[192,1024]{1,0:T(8,128)(2,1)S(1)} %get-tuple-element.37), channel_id=1, source_target_pairs={{0,60},{4,0},{8,4},{12,8},{16,12},{20,16},{24,20},{28,24},{32,28},... | collective-permute-start | bytes 1179656 | tf_op jit(solution)/shard_map/ppermute | solution.py:42
  116.2 2.0 %collective-permute-start.11 = (bf16[192,1024]{1,0:T(8,128)(2,1)S(1)}, bf16[192,1024]{1,0:T(8,128)(2,1)S(1)}, u32[]{:S(2)}, u32[]{:S(2)}) collective-permute-start(bf16[192,1024]{1,0:T(8,128)(2,1)S(1)} %get-tuple-element.38), channel_id=1, source_target_pairs={{0,4},{4,8},{8,12},{12,16},{16,20},{20,24},{24,28},{28,32},{32,36}... | collective-permute-start | bytes 1179656 | tf_op jit(solution)/shard_map/ppermute | solution.py:42
  118.3 3.5 %collective-permute-done.9 = bf16[192,1024]{1,0:T(8,128)(2,1)S(1)} collective-permute-done((bf16[192,1024]{1,0:T(8,128)(2,1)S(1)}, bf16[192,1024]{1,0:T(8,128)(2,1)S(1)}, u32[]{:S(2)}, u32[]{:S(2)}) %collective-permute-start.9) | collective-permute-done | bytes 393248 | tf_op jit(solution)/shard_map/ppermute | solution.py:42
  121.9 3.1 %collective-permute-start.10 = (bf16[192,1024]{1,0:T(8,128)(2,1)S(1)}, bf16[192,1024]{1,0:T(8,128)(2,1)S(1)}, u32[]{:S(2)}, u32[]{:S(2)}) collective-permute-start(bf16[192,1024]{1,0:T(8,128)(2,1)S(1)} %add_convert_fusion), channel_id=1, source_target_pairs={{0,60},{4,0},{8,4},{12,8},{16,12},{20,16},{24,20},{28,24},{32,28},... | collective-permute-start | bytes 1179656 | tf_op jit(solution)/shard_map/ppermute | solution.py:42
  125.1 0.9 shard_map.104
  126.1 2.5 %collective-permute-done.11.refs_1_ = bf16[192,1024]{1,0:T(8,128)(2,1)S(1)} collective-permute-done((bf16[192,1024]{1,0:T(8,128)(2,1)S(1)}, bf16[192,1024]{1,0:T(8,128)(2,1)S(1)}, u32[]{:S(2)}, u32[]{:S(2)}) %collective-permute-start.11) | collective-permute-done | bytes 393248 | tf_op jit(solution)/shard_map/ppermute | solution.py:42
  128.6 4.5 %collective-permute-done.10.refs_0_ = bf16[192,1024]{1,0:T(8,128)(2,1)S(1)} collective-permute-done((bf16[192,1024]{1,0:T(8,128)(2,1)S(1)}, bf16[192,1024]{1,0:T(8,128)(2,1)S(1)}, u32[]{:S(2)}, u32[]{:S(2)}) %collective-permute-start.10) | collective-permute-done | bytes 393248 | tf_op jit(solution)/shard_map/ppermute | solution.py:42
  133.1 0.5 shard_map.105
  133.6 40.1 %all_to_all.10.in_ref = bf16[32,48,128]{2,1,0:T(8,128)(2,1)S(1)} all-to-all(bf16[32,48,128]{2,1,0:T(8,128)(2,1)S(1)} %shard_map.105), channel_id=1, replica_groups={{0,16,32,48,64,80,96,112,128,144,160,176,192,208,224,240,256,272,288,30..., dimensions={0} | all-to-all | bytes 786432 | tf_op jit(solution)/shard_map/all_to_all | solution.py:32
  173.7 0.9 shard_map.106
  (33 shorter events, 0.8 us)
Async XLA Ops:
  0.0 18.9 %copy-start.6 = (bf16[1,4096,128]{2,1,0:T(8,128)(2,1)S(1)}, bf16[1,4096,128]{2,1,0:T(8,128)(2,1)}, u32[]{:S(2)}) copy-start(bf16[1,4096,128]{2,1,0:T(8,128)(2,1)} %param.14) | copy-start | bytes 3145732
  2.0 44.9 %all-to-all-start = ((bf16[32,48,128]{2,1,0:T(8,128)(2,1)}), bf16[32,48,128]{2,1,0:T(8,128)(2,1)S(1)}, u32[]{:S(2)}, u32[]{:S(2)}) async-start(bf16[32,48,128]{2,1,0:T(8,128)(2,1)} %get-tuple-element.22), calls=%async_computation | async-start | bytes 786432 | tf_op jit(solution)/shard_map/all_to_all | solution.py:32
  18.9 28.0 %copy-start.2 = (bf16[384,384]{1,0:T(8,128)(2,1)S(1)}, bf16[384,384]{1,0:T(8,128)(2,1)}, u32[]{:S(2)}) copy-start(bf16[384,384]{1,0:T(8,128)(2,1)} %constant.73.clone.order_ref) | copy-start | bytes 884740
  21.1 28.9 %copy-start.7 = (bf16[1024,128]{1,0:T(8,128)(2,1)S(1)}, bf16[1024,128]{1,0:T(8,128)(2,1)}, u32[]{:S(2)}) copy-start(bf16[1024,128]{1,0:T(8,128)(2,1)} %get-tuple-element.43) | copy-start | bytes 786436
  21.1 28.9 %copy-start.8 = (bf16[1024,128]{1,0:T(8,128)(2,1)S(1)}, bf16[1024,128]{1,0:T(8,128)(2,1)}, u32[]{:S(2)}) copy-start(bf16[1024,128]{1,0:T(8,128)(2,1)} %get-tuple-element.50) | copy-start | bytes 786436
  47.4 14.6 %collective-permute-start = (bf16[192,1024]{1,0:T(8,128)(2,1)S(1)}, bf16[192,1024]{1,0:T(8,128)(2,1)S(1)}, u32[]{:S(2)}, u32[]{:S(2)}) collective-permute-start(bf16[192,1024]{1,0:T(8,128)(2,1)S(1)} %shard_map.100.refs_0_), channel_id=1, source_target_pairs={{0,4},{4,8},{8,12},{12,16},{16,20},{20,24},{24,28},{28,32},{32,36}... | collective-permute-start | bytes 1179656 | tf_op jit(solution)/shard_map/ppermute | solution.py:42
  50.1 17.1 %collective-permute-start.5 = (bf16[1024,256]{1,0:T(8,128)(2,1)S(1)}, bf16[1024,256]{1,0:T(8,128)(2,1)S(1)}, u32[]{:S(2)}, u32[]{:S(2)}) collective-permute-start(bf16[1024,256]{1,0:T(8,128)(2,1)S(1)} %pad_maximum_fusion.3), channel_id=1, source_target_pairs={{0,2},{1,3},{2,0},{3,1},{64,66},{65,67},{66,64},{67,65},{128,130},... | collective-permute-start | bytes 1572872 | tf_op jit(solution)/shard_map/ppermute | solution.py:205
  53.9 23.4 %collective-permute-start.4 = (bf16[1024,256]{1,0:T(8,128)(2,1)S(1)}, bf16[1024,256]{1,0:T(8,128)(2,1)S(1)}, u32[]{:S(2)}, u32[]{:S(2)}) collective-permute-start(bf16[1024,256]{1,0:T(8,128)(2,1)S(1)} %pad_maximum_fusion.2), channel_id=1, source_target_pairs={{0,1},{1,2},{2,3},{3,0},{64,67},{65,64},{66,65},{67,66},{128,129},... | collective-permute-start | bytes 1572872 | tf_op jit(solution)/shard_map/ppermute | solution.py:205
  57.1 20.4 %collective-permute-start.3 = (bf16[1024,256]{1,0:T(8,128)(2,1)S(1)}, bf16[1024,256]{1,0:T(8,128)(2,1)S(1)}, u32[]{:S(2)}, u32[]{:S(2)}) collective-permute-start(bf16[1024,256]{1,0:T(8,128)(2,1)S(1)} %pad_maximum_fusion.1), channel_id=1, source_target_pairs={{0,3},{1,0},{2,1},{3,2},{64,65},{65,66},{66,67},{67,64},{128,131},... | collective-permute-start | bytes 1572872 | tf_op jit(solution)/shard_map/ppermute | solution.py:205
  59.3 18.1 %collective-permute-start.1 = (bf16[192,1024]{1,0:T(8,128)(2,1)S(1)}, bf16[192,1024]{1,0:T(8,128)(2,1)S(1)}, u32[]{:S(2)}, u32[]{:S(2)}) collective-permute-start(bf16[192,1024]{1,0:T(8,128)(2,1)S(1)} %shard_map.100.refs_0_), channel_id=1, source_target_pairs={{0,60},{4,0},{8,4},{12,8},{16,12},{20,16},{24,20},{28,24},{32,28},... | collective-permute-start | bytes 1179656 | tf_op jit(solution)/shard_map/ppermute | solution.py:42
  62.0 15.4 %collective-permute-start.2 = (bf16[192,1024]{1,0:T(8,128)(2,1)S(1)}, bf16[192,1024]{1,0:T(8,128)(2,1)S(1)}, u32[]{:S(2)}, u32[]{:S(2)}) collective-permute-start(bf16[192,1024]{1,0:T(8,128)(2,1)S(1)} %collective-permute-done.refs_1_), channel_id=1, source_target_pairs={{0,4},{4,8},{8,12},{12,16},{16,20},{20,24},{24,28},{28,32},{32,36}... | collective-permute-start | bytes 1179656 | tf_op jit(solution)/shard_map/ppermute | solution.py:42
  79.2 8.9 %collective-permute-start.6 = (bf16[768,256]{1,0:T(8,128)(2,1)S(1)}, bf16[768,256]{1,0:T(8,128)(2,1)S(1)}, u32[]{:S(2)}, u32[]{:S(2)}) collective-permute-start(bf16[768,256]{1,0:T(8,128)(2,1)S(1)} %get-tuple-element.25), channel_id=1, source_target_pairs={{0,1},{1,2},{2,3},{3,0},{64,67},{65,64},{66,65},{67,66},{128,129},... | collective-permute-start | bytes 1179656 | tf_op jit(solution)/shard_map/ppermute | solution.py:205
  81.3 11.5 %collective-permute-start.8 = (bf16[768,256]{1,0:T(8,128)(2,1)S(1)}, bf16[768,256]{1,0:T(8,128)(2,1)S(1)}, u32[]{:S(2)}, u32[]{:S(2)}) collective-permute-start(bf16[768,256]{1,0:T(8,128)(2,1)S(1)} %get-tuple-element.26), channel_id=1, source_target_pairs={{0,3},{1,0},{2,1},{3,2},{64,65},{65,66},{66,67},{67,64},{128,131},... | collective-permute-start | bytes 1179656 | tf_op jit(solution)/shard_map/ppermute | solution.py:205
  88.2 8.8 %collective-permute-start.7 = (bf16[768,256]{1,0:T(8,128)(2,1)S(1)}, bf16[768,256]{1,0:T(8,128)(2,1)S(1)}, u32[]{:S(2)}, u32[]{:S(2)}) collective-permute-start(bf16[768,256]{1,0:T(8,128)(2,1)S(1)} %add_convert_fusion.1), channel_id=1, source_target_pairs={{0,1},{1,2},{2,3},{3,0},{64,67},{65,64},{66,65},{67,66},{128,129},... | collective-permute-start | bytes 1179656 | tf_op jit(solution)/shard_map/ppermute | solution.py:205
  97.0 15.0 %copy-start = (bf16[1,512,1024]{2,1,0:T(8,128)(2,1)S(1)}, bf16[1,512,1024]{2,1,0:T(8,128)(2,1)}, u32[]{:S(2)}) copy-start(bf16[1,512,1024]{2,1,0:T(8,128)(2,1)} %param.15) | copy-start | bytes 3145732
  113.0 8.8 %collective-permute-start.9 = (bf16[192,1024]{1,0:T(8,128)(2,1)S(1)}, bf16[192,1024]{1,0:T(8,128)(2,1)S(1)}, u32[]{:S(2)}, u32[]{:S(2)}) collective-permute-start(bf16[192,1024]{1,0:T(8,128)(2,1)S(1)} %get-tuple-element.37), channel_id=1, source_target_pairs={{0,60},{4,0},{8,4},{12,8},{16,12},{20,16},{24,20},{28,24},{32,28},... | collective-permute-start | bytes 1179656 | tf_op jit(solution)/shard_map/ppermute | solution.py:42
  116.2 12.3 %collective-permute-start.11 = (bf16[192,1024]{1,0:T(8,128)(2,1)S(1)}, bf16[192,1024]{1,0:T(8,128)(2,1)S(1)}, u32[]{:S(2)}, u32[]{:S(2)}) collective-permute-start(bf16[192,1024]{1,0:T(8,128)(2,1)S(1)} %get-tuple-element.38), channel_id=1, source_target_pairs={{0,4},{4,8},{8,12},{12,16},{16,20},{20,24},{24,28},{28,32},{32,36}... | collective-permute-start | bytes 1179656 | tf_op jit(solution)/shard_map/ppermute | solution.py:42
  121.8 3.2 %copy-start.9 = (f32[16,2]{0,1:T(2,128)S(1)}, f32[16,2]{0,1:T(2,128)}, u32[]{:S(2)}) copy-start(f32[16,2]{0,1:T(2,128)} %param.12) | copy-start | bytes 388
  121.8 3.3 %copy-start.3 = (bf16[8,16,1024]{2,1,0:T(8,128)(2,1)S(1)}, bf16[8,16,1024]{2,1,0:T(8,128)(2,1)}, u32[]{:S(2)}) copy-start(bf16[8,16,1024]{2,1,0:T(8,128)(2,1)} %past_ref.1) | copy-start | bytes 786436
  121.8 3.3 %copy-start.4 = (s32[16,2]{0,1:T(2,128)S(1)}, s32[16,2]{0,1:T(2,128)}, u32[]{:S(2)}) copy-start(s32[16,2]{0,1:T(2,128)} %param.11) | copy-start | bytes 388
  121.8 3.3 %copy-start.5 = (f32[9]{0:T(128)S(1)}, f32[9]{0:T(128)}, u32[]{:S(2)}) copy-start(f32[9]{0:T(128)} %dwa_ref.1) | copy-start | bytes 112
  121.9 11.2 %copy-start.1 = (bf16[384,384]{1,0:T(8,128)(2,1)S(1)}, bf16[384,384]{1,0:T(8,128)(2,1)}, u32[]{:S(2)}) copy-start(bf16[384,384]{1,0:T(8,128)(2,1)} %constant.74.clone.order_ref) | copy-start | bytes 884740
  121.9 11.2 %collective-permute-start.10 = (bf16[192,1024]{1,0:T(8,128)(2,1)S(1)}, bf16[192,1024]{1,0:T(8,128)(2,1)S(1)}, u32[]{:S(2)}, u32[]{:S(2)}) collective-permute-start(bf16[192,1024]{1,0:T(8,128)(2,1)S(1)} %add_convert_fusion), channel_id=1, source_target_pairs={{0,60},{4,0},{8,4},{12,8},{16,12},{20,16},{24,20},{28,24},{32,28},... | collective-permute-start | bytes 1179656 | tf_op jit(solution)/shard_map/ppermute | solution.py:42

commit v11 on v9

--- a/solution.py
+++ b/solution.py
@@ -82,15 +82,18 @@
     return jnp.dot(ids.astype(jnp.float32), spread, preferred_element_type=jnp.float32)
 
 
-def assigned_slots(ids, experts, tok_rows):
+def earlier_tokens(tok_rows):
+    source = lax.broadcasted_iota(jnp.int32, (LANES, LANES), 0)
+    token = lax.broadcasted_iota(jnp.int32, (LANES, LANES), 1) % tok_rows
+    return (source < token).astype(jnp.float32)
+
+
+def assigned_slots(ids, experts, before):
     ids = repeated_ids(ids)
     choices, lanes = ids.shape
     expert = lax.broadcasted_iota(jnp.int32, (experts, lanes), 0).astype(jnp.float32)
     chosen = [ids[place : place + 1, :] == expert for place in range(choices)]
     named = sum(mask.astype(jnp.float32) for mask in chosen)
-    source = lax.broadcasted_iota(jnp.int32, (lanes, lanes), 0)
-    token = lax.broadcasted_iota(jnp.int32, (lanes, lanes), 1) % tok_rows
-    before = (source < token).astype(jnp.float32)
     earlier = jnp.dot(named, before, preferred_element_type=jnp.float32)
     return [jnp.where(mask, earlier, -1.0) for mask in chosen]
 
@@ -122,8 +125,9 @@
         copy = pltpu.make_async_copy(tokens_ref.at[:, pl.ds(first, quarter)], own_ref, arrived)
         ids_copy.start()
         copy.start()
+        before = earlier_tokens(tok_rows)
         ids_copy.wait()
-        slots = assigned_slots(ids_ref[...], experts, tok_rows)
+        slots = assigned_slots(ids_ref[...], experts, before)
         chosen = placed(slots, [1.0] * len(slots), capacity, tok_rows).astype(jnp.bfloat16)
         copy.wait()
         tall = [own_ref[:, block * LANES : (block + 1) * LANES] for block in range(blocks)]
@@ -245,13 +249,14 @@
     return call(kernel, jax.ShapeDtypeStruct((rows, width), jnp.bfloat16), parts)
 
 
-def down_sets(hidden, w_down, dtypes):
+def down_sets(hidden, w_down, count, places, dtypes):
     parts, rows, _ = hidden.shape
-    set_rows = rows // len(dtypes)
+    set_rows = rows // count
     features = w_down.shape[1]
 
     def kernel(hidden_ref, w_ref, *out_refs):
-        wide = jnp.concatenate([hidden_ref[part] for part in range(parts)], axis=1)
+        taken = slice(places[0] * set_rows, (places[-1] + 1) * set_rows)
+        wide = jnp.concatenate([hidden_ref[part, taken, :] for part in range(parts)], axis=1)
         out = jnp.dot(wide, w_ref[...], preferred_element_type=jnp.float32)
         for place, ref in enumerate(out_refs):
             ref[...] = out[place * set_rows : (place + 1) * set_rows].astype(ref.dtype)
@@ -266,7 +271,7 @@
     depth = past_layers.shape[0]
 
     def kernel(dwa_ref, ids_ref, route_ref, own_ref, past_ref, terms_ref, base_ref):
-        slots = assigned_slots(ids_ref[...], experts, tok_rows)
+        slots = assigned_slots(ids_ref[...], experts, earlier_tokens(tok_rows))
         route = route_ref[...]
         total = sum(route[place : place + 1, :] for place in range(len(slots)))
         shares = [dwa_ref[depth] * (route[place : place + 1, :] / total) for place in range(len(slots))]
@@ -336,10 +341,13 @@
     sets = window_sets(own_set)
     partial = lax.all_to_all(gate_up_parts(sets, weights, place), "tensor", 0, 0, tiled=True)
     hidden = lax.all_gather(hidden_units(partial), "tensor", axis=0, tiled=False)
-    own, *others = down_sets(hidden, down_weight[0], [jnp.float32] * 2 + [jnp.bfloat16] * 2)
+    count = len(sets)
+    other, second = down_sets(hidden, down_weight[0], count, range(2, count), [jnp.bfloat16] * 2)
+    hidden, other, second = lax.optimization_barrier((hidden, other, second))
+    own, first = down_sets(hidden, down_weight[0], count, range(2), [jnp.float32] * 2)
     route, own = lax.optimization_barrier((route, own))
     terms, base = mix_terms(ids, route, own_columns, past_layers, dwa_weight, experts, capacity)
-    others = returned_sums(*others)
+    others = returned_sums(first, other, second)
     own, terms, base = lax.optimization_barrier((own, terms, base))
     returned = far_exchange(summed_chunks(own, others, jnp.asarray(order.T, jnp.bfloat16), capacity))
     return mixed_layers(returned, terms, base, tokens.dtype)

time: 179 us -> 179 us (level)
    pallas_call x7 -> x8, Pallas kernels: 5.91 us -> 6.05 us  [call(): pl.pallas_call(kernel, out_shape=out_shape, in_specs=in_specs or [VMEM] *...]
where the time goes in v11:
time: 179 us
  blocking collectives  74.3 us (42%)
  waiting for transfers between devices  48.6 us (27%)
  starting transfers between devices  43.7 us (24%)
  Pallas kernels  8.03 us (4%)
  local copies, waits for them, and re-layouts  2.32 us (1%)
    all_to_all x1, blocking collectives, far_exchange(): lax.all_to_all(chunks, ('expert', 'dp'), 0, 0, tiled=True, axis_index_gro...  38.9 us
    all_to_all x1, waiting for transfers between devices, far_exchange(): lax.all_to_all(chunks, ('expert', 'dp'), 0, 0, tiled=True, axis_index_gro...  26.8 us
    all_to_all x1, blocking collectives, per_device(): lax.all_to_all(gate_up_parts(sets, weights, place), 'tensor', 0, 0, tiled...  23.6 us
    ppermute x6, starting transfers between devices, shifted(): return lax.ppermute(shard, ('expert', 'dp'), pairs)  17 us
    all_to_all x1, starting transfers between devices, far_exchange(): lax.all_to_all(chunks, ('expert', 'dp'), 0, 0, tiled=True, axis_index_gro...  16.8 us
    all_gather x1, blocking collectives, per_device(): lax.all_gather(hidden_units(partial), 'tensor', axis=0, tiled=False)  11.8 us
    ppermute x3, waiting for transfers between devices, slab(): lax.ppermute(both, 'tensor', [(i, (i + shift) % parts) for i in range(par...  10.9 us
    ppermute x6, waiting for transfers between devices, shifted(): return lax.ppermute(shard, ('expert', 'dp'), pairs)  10.9 us
  transfers between devices with their start and end apart: 10, of which 6 were waited for; matrix products, arithmetic and copies ran while one was open for 2% of the time, Pallas kernels for 1%

profile of v11, /device:TPU:65, one launch (start us, length us, event | category | flops | bytes accessed | tf_op | source)
XLA Modules:
  0.0 178.6 jit_solution(16952357061700809641)
XLA Ops:
  0.0 2.0 %packed_rows.1 = (bf16[32,48,128]{2,1,0:T(8,128)(2,1)}, bf16[16,1024]{1,0:T(8,128)(2,1)S(1)}) custom-call(s32[1]{0:T(128)S(6)} %mul.3.first_ref, s32[2,16]{1,0:T(2,128)} %bitcast.27, bf16[16,4096]{1,0:T(8,128)(2,1)} %tokens_ref.1), custom_call_target="tpu_custom_call" | custom-call | tf_op jit(solution)/shard_map/packed_rows/pallas_call | solution.py:141
  2.0 16.8 %all-to-all-start = ((bf16[32,48,128]{2,1,0:T(8,128)(2,1)}), bf16[32,48,128]{2,1,0:T(8,128)(2,1)S(1)}, u32[]{:S(2)}, u32[]{:S(2)}) async-start(bf16[32,48,128]{2,1,0:T(8,128)(2,1)} %get-tuple-element.21), calls=%async_computation | async-start | bytes 786432 | tf_op jit(solution)/shard_map/all_to_all | solution.py:33
  18.8 2.2 %dynamic-slice_bitcast_fusion = (bf16[1024,128]{1,0:T(8,128)(2,1)}, bf16[1024,128]{1,0:T(8,128)(2,1)S(1)}, bf16[1024,128]{1,0:T(8,128)(2,1)S(1)}, bf16[1024,128]...) fusion(bf16[4,1024,128]{2,1,0:T(8,128)(2,1)S(1)} %bitcast.29, ...), kind=kLoop, calls=%fused_computation.5 | loop fusion | bytes 4194320 | tf_op jit(solution)/shard_map/jit(dynamic_index_in_dim)/squeeze | solution.py:210
  21.0 26.8 %all-to-all-done.in_ref = bf16[32,48,128]{2,1,0:T(8,128)(2,1)S(1)} async-done(((bf16[32,48,128]{2,1,0:T(8,128)(2,1)}), bf16[32,48,128]{2,1,0:T(8,128)(2,1)S(1)}, u32[]{:S(2)}, u32[]{:S(2)}) %all-to-all-start) | async-done | bytes 393248 | tf_op jit(solution)/shard_map/all_to_all | solution.py:33
  47.8 0.5 shard_map.100.refs_0_
  48.3 2.6 %collective-permute-start = (bf16[192,1024]{1,0:T(8,128)(2,1)S(1)}, bf16[192,1024]{1,0:T(8,128)(2,1)S(1)}, u32[]{:S(2)}, u32[]{:S(2)}) collective-permute-start(bf16[192,1024]{1,0:T(8,128)(2,1)S(1)} %shard_map.100.refs_0_), channel_id=1, source_target_pairs={{0,4},{4,8},{8,12},{12,16},{16,20},{20,24},{24,28},{28,32},{32,36}... | collective-permute-start | bytes 1179656 | tf_op jit(solution)/shard_map/ppermute | solution.py:43
  50.9 1.1 pad_maximum_fusion.3
  52.0 4.7 %collective-permute-start.5 = (bf16[1024,256]{1,0:T(8,128)(2,1)S(1)}, bf16[1024,256]{1,0:T(8,128)(2,1)S(1)}, u32[]{:S(2)}, u32[]{:S(2)}) collective-permute-start(bf16[1024,256]{1,0:T(8,128)(2,1)S(1)} %pad_maximum_fusion.3), channel_id=1, source_target_pairs={{0,2},{1,3},{2,0},{3,1},{4,6},{5,7},{6,4},{7,5},{8,10},{9,11},{10,... | collective-permute-start | bytes 1572872 | tf_op jit(solution)/shard_map/ppermute | solution.py:214
  56.7 2.8 %collective-permute-start.4 = (bf16[1024,256]{1,0:T(8,128)(2,1)S(1)}, bf16[1024,256]{1,0:T(8,128)(2,1)S(1)}, u32[]{:S(2)}, u32[]{:S(2)}) collective-permute-start(bf16[1024,256]{1,0:T(8,128)(2,1)S(1)} %pad_maximum_fusion.2), channel_id=1, source_target_pairs={{0,3},{1,0},{2,1},{3,2},{4,7},{5,4},{6,5},{7,6},{8,11},{9,8},{10,9... | collective-permute-start | bytes 1572872 | tf_op jit(solution)/shard_map/ppermute | solution.py:214
  59.6 2.5 %collective-permute-start.3 = (bf16[1024,256]{1,0:T(8,128)(2,1)S(1)}, bf16[1024,256]{1,0:T(8,128)(2,1)S(1)}, u32[]{:S(2)}, u32[]{:S(2)}) collective-permute-start(bf16[1024,256]{1,0:T(8,128)(2,1)S(1)} %pad_maximum_fusion.1), channel_id=1, source_target_pairs={{0,1},{1,2},{2,3},{3,0},{4,5},{5,6},{6,7},{7,4},{8,9},{9,10},{10,1... | collective-permute-start | bytes 1572872 | tf_op jit(solution)/shard_map/ppermute | solution.py:214
  62.1 2.7 %collective-permute-start.1 = (bf16[192,1024]{1,0:T(8,128)(2,1)S(1)}, bf16[192,1024]{1,0:T(8,128)(2,1)S(1)}, u32[]{:S(2)}, u32[]{:S(2)}) collective-permute-start(bf16[192,1024]{1,0:T(8,128)(2,1)S(1)} %shard_map.100.refs_0_), channel_id=1, source_target_pairs={{0,60},{4,0},{8,4},{12,8},{16,12},{20,16},{24,20},{28,24},{32,28},... | collective-permute-start | bytes 1179656 | tf_op jit(solution)/shard_map/ppermute | solution.py:43
  64.8 2.6 %collective-permute-start.2 = (bf16[192,1024]{1,0:T(8,128)(2,1)S(1)}, bf16[192,1024]{1,0:T(8,128)(2,1)S(1)}, u32[]{:S(2)}, u32[]{:S(2)}) collective-permute-start(bf16[192,1024]{1,0:T(8,128)(2,1)S(1)} %collective-permute-done.refs_1_), channel_id=1, source_target_pairs={{0,4},{4,8},{8,12},{12,16},{16,20},{20,24},{24,28},{28,32},{32,36}... | collective-permute-start | bytes 1179656 | tf_op jit(solution)/shard_map/ppermute | solution.py:43
  67.5 1.6 collective-permute-done.5.refs_7_
  69.0 9.4 %collective-permute-done.4.refs_6_ = bf16[1024,256]{1,0:T(8,128)(2,1)S(1)} collective-permute-done((bf16[1024,256]{1,0:T(8,128)(2,1)S(1)}, bf16[1024,256]{1,0:T(8,128)(2,1)S(1)}, u32[]{:S(2)}, u32[]{:S(2)}) %collective-permute-start.4) | collective-permute-done | bytes 524320 | tf_op jit(solution)/shard_map/ppermute | solution.py:214
  78.4 1.9 %shard_map.101 = bf16[4,768,256]{2,1,0:T(8,128)(2,1)S(1)} custom-call(s32[1]{0:T(128)} %bitcast.1.place_ref, bf16[192,1024]{1,0:T(8,128)(2,1)S(1)} %shard_map.100.refs_0_, bf16[192,1024]{1,0:T(8,128)(2,1)S(1)} %collective-permute-done.refs_1_, bf16[192,1024]{1,0:T(8,128)(2,1)S(1)} %collective-permute-done.1.refs_2_, ...), custom_call_target="tpu_custom_call" | custom-call | tf_op jit(solution)/shard_map/pallas_call | solution.py:68
  80.3 23.6 %all_to_all.15.in_ref = bf16[4,768,256]{2,1,0:T(8,128)(2,1)S(1)} all-to-all(bf16[4,768,256]{2,1,0:T(8,128)(2,1)S(1)} %shard_map.101), channel_id=1, replica_groups=mesh['expert'=8,'dp'=16,'tensor'=4] {'tensor'}, dimensions={0} | all-to-all | bytes 3145728 | tf_op jit(solution)/shard_map/all_to_all | solution.py:342
  103.9 0.3 shard_map.102
  104.2 11.8 %all-gather = bf16[3072,128]{1,0:T(8,128)(2,1)S(1)} all-gather(bf16[768,128]{1,0:T(8,128)(2,1)S(1)} %shard_map.102), channel_id=2, replica_groups=mesh['expert'=8,'dp'=16,'tensor'=4] {'tensor'}, dimensions={0}, use_global_device_ids=true | all-gather | bytes 983040 | tf_op jit(solution)/shard_map/all_gather | solution.py:343
  116.0 0.6 shard_map.103
  116.6 3.8 %collective-permute-start.6 = (bf16[192,1024]{1,0:T(8,128)(2,1)S(1)}, bf16[192,1024]{1,0:T(8,128)(2,1)S(1)}, u32[]{:S(2)}, u32[]{:S(2)}) collective-permute-start(bf16[192,1024]{1,0:T(8,128)(2,1)S(1)} %get-tuple-element.35), channel_id=1, source_target_pairs={{0,60},{4,0},{8,4},{12,8},{16,12},{20,16},{24,20},{28,24},{32,28},... | collective-permute-start | bytes 1179656 | tf_op jit(solution)/shard_map/ppermute | solution.py:43
  120.4 0.6 shard_map.104
  121.0 2.0 %collective-permute-start.8 = (bf16[192,1024]{1,0:T(8,128)(2,1)S(1)}, bf16[192,1024]{1,0:T(8,128)(2,1)S(1)}, u32[]{:S(2)}, u32[]{:S(2)}) collective-permute-start(bf16[192,1024]{1,0:T(8,128)(2,1)S(1)} %get-tuple-element.36), channel_id=1, source_target_pairs={{0,4},{4,8},{8,12},{12,16},{16,20},{20,24},{24,28},{28,32},{32,36}... | collective-permute-start | bytes 1179656 | tf_op jit(solution)/shard_map/ppermute | solution.py:43
  123.0 2.6 %collective-permute-done.6 = bf16[192,1024]{1,0:T(8,128)(2,1)S(1)} collective-permute-done((bf16[192,1024]{1,0:T(8,128)(2,1)S(1)}, bf16[192,1024]{1,0:T(8,128)(2,1)S(1)}, u32[]{:S(2)}, u32[]{:S(2)}) %collective-permute-start.6) | collective-permute-done | bytes 393248 | tf_op jit(solution)/shard_map/ppermute | solution.py:43
  125.6 0.1 add_convert_fusion
  125.7 3.3 %collective-permute-start.7 = (bf16[192,1024]{1,0:T(8,128)(2,1)S(1)}, bf16[192,1024]{1,0:T(8,128)(2,1)S(1)}, u32[]{:S(2)}, u32[]{:S(2)}) collective-permute-start(bf16[192,1024]{1,0:T(8,128)(2,1)S(1)} %add_convert_fusion), channel_id=1, source_target_pairs={{0,60},{4,0},{8,4},{12,8},{16,12},{20,16},{24,20},{28,24},{32,28},... | collective-permute-start | bytes 1179656 | tf_op jit(solution)/shard_map/ppermute | solution.py:43
  129.1 0.1 tile.10.route_ref
  129.2 0.9 shard_map.105
  130.1 3.3 %collective-permute-done.8.refs_1_ = bf16[192,1024]{1,0:T(8,128)(2,1)S(1)} collective-permute-done((bf16[192,1024]{1,0:T(8,128)(2,1)S(1)}, bf16[192,1024]{1,0:T(8,128)(2,1)S(1)}, u32[]{:S(2)}, u32[]{:S(2)}) %collective-permute-start.8) | collective-permute-done | bytes 393248 | tf_op jit(solution)/shard_map/ppermute | solution.py:43
  133.4 4.9 %collective-permute-done.7.refs_0_ = bf16[192,1024]{1,0:T(8,128)(2,1)S(1)} collective-permute-done((bf16[192,1024]{1,0:T(8,128)(2,1)S(1)}, bf16[192,1024]{1,0:T(8,128)(2,1)S(1)}, u32[]{:S(2)}, u32[]{:S(2)}) %collective-permute-start.7) | collective-permute-done | bytes 393248 | tf_op jit(solution)/shard_map/ppermute | solution.py:43
  138.3 0.5 shard_map.106
  138.8 38.9 %all_to_all.16.in_ref = bf16[32,48,128]{2,1,0:T(8,128)(2,1)S(1)} all-to-all(bf16[32,48,128]{2,1,0:T(8,128)(2,1)S(1)} %shard_map.106), channel_id=1, replica_groups={{0,16,32,48,64,80,96,112,128,144,160,176,192,208,224,240,256,272,288,30..., dimensions={0} | all-to-all | bytes 786432 | tf_op jit(solution)/shard_map/all_to_all | solution.py:33
  177.7 0.9 shard_map.107
  (24 shorter events, 0.2 us)
Async XLA Ops:
  0.0 18.8 %copy-start.6 = (bf16[1,4096,128]{2,1,0:T(8,128)(2,1)S(1)}, bf16[1,4096,128]{2,1,0:T(8,128)(2,1)}, u32[]{:S(2)}) copy-start(bf16[1,4096,128]{2,1,0:T(8,128)(2,1)} %param.14) | copy-start | bytes 3145732
  2.0 45.8 %all-to-all-start = ((bf16[32,48,128]{2,1,0:T(8,128)(2,1)}), bf16[32,48,128]{2,1,0:T(8,128)(2,1)S(1)}, u32[]{:S(2)}, u32[]{:S(2)}) async-start(bf16[32,48,128]{2,1,0:T(8,128)(2,1)} %get-tuple-element.21), calls=%async_computation | async-start | bytes 786432 | tf_op jit(solution)/shard_map/all_to_all | solution.py:33
  18.8 29.0 %copy-start.2 = (bf16[384,384]{1,0:T(8,128)(2,1)S(1)}, bf16[384,384]{1,0:T(8,128)(2,1)}, u32[]{:S(2)}) copy-start(bf16[384,384]{1,0:T(8,128)(2,1)} %constant.58.clone.order_ref) | copy-start | bytes 884740
  48.3 16.5 %collective-permute-start = (bf16[192,1024]{1,0:T(8,128)(2,1)S(1)}, bf16[192,1024]{1,0:T(8,128)(2,1)S(1)}, u32[]{:S(2)}, u32[]{:S(2)}) collective-permute-start(bf16[192,1024]{1,0:T(8,128)(2,1)S(1)} %shard_map.100.refs_0_), channel_id=1, source_target_pairs={{0,4},{4,8},{8,12},{12,16},{16,20},{20,24},{24,28},{28,32},{32,36}... | collective-permute-start | bytes 1179656 | tf_op jit(solution)/shard_map/ppermute | solution.py:43
  52.0 17.0 %collective-permute-start.5 = (bf16[1024,256]{1,0:T(8,128)(2,1)S(1)}, bf16[1024,256]{1,0:T(8,128)(2,1)S(1)}, u32[]{:S(2)}, u32[]{:S(2)}) collective-permute-start(bf16[1024,256]{1,0:T(8,128)(2,1)S(1)} %pad_maximum_fusion.3), channel_id=1, source_target_pairs={{0,2},{1,3},{2,0},{3,1},{4,6},{5,7},{6,4},{7,5},{8,10},{9,11},{10,... | collective-permute-start | bytes 1572872 | tf_op jit(solution)/shard_map/ppermute | solution.py:214
  56.7 21.7 %collective-permute-start.4 = (bf16[1024,256]{1,0:T(8,128)(2,1)S(1)}, bf16[1024,256]{1,0:T(8,128)(2,1)S(1)}, u32[]{:S(2)}, u32[]{:S(2)}) collective-permute-start(bf16[1024,256]{1,0:T(8,128)(2,1)S(1)} %pad_maximum_fusion.2), channel_id=1, source_target_pairs={{0,3},{1,0},{2,1},{3,2},{4,7},{5,4},{6,5},{7,6},{8,11},{9,8},{10,9... | collective-permute-start | bytes 1572872 | tf_op jit(solution)/shard_map/ppermute | solution.py:214
  59.6 18.8 %collective-permute-start.3 = (bf16[1024,256]{1,0:T(8,128)(2,1)S(1)}, bf16[1024,256]{1,0:T(8,128)(2,1)S(1)}, u32[]{:S(2)}, u32[]{:S(2)}) collective-permute-start(bf16[1024,256]{1,0:T(8,128)(2,1)S(1)} %pad_maximum_fusion.1), channel_id=1, source_target_pairs={{0,1},{1,2},{2,3},{3,0},{4,5},{5,6},{6,7},{7,4},{8,9},{9,10},{10,1... | collective-permute-start | bytes 1572872 | tf_op jit(solution)/shard_map/ppermute | solution.py:214
  62.1 16.3 %collective-permute-start.1 = (bf16[192,1024]{1,0:T(8,128)(2,1)S(1)}, bf16[192,1024]{1,0:T(8,128)(2,1)S(1)}, u32[]{:S(2)}, u32[]{:S(2)}) collective-permute-start(bf16[192,1024]{1,0:T(8,128)(2,1)S(1)} %shard_map.100.refs_0_), channel_id=1, source_target_pairs={{0,60},{4,0},{8,4},{12,8},{16,12},{20,16},{24,20},{28,24},{32,28},... | collective-permute-start | bytes 1179656 | tf_op jit(solution)/shard_map/ppermute | solution.py:43
  64.8 13.6 %collective-permute-start.2 = (bf16[192,1024]{1,0:T(8,128)(2,1)S(1)}, bf16[192,1024]{1,0:T(8,128)(2,1)S(1)}, u32[]{:S(2)}, u32[]{:S(2)}) collective-permute-start(bf16[192,1024]{1,0:T(8,128)(2,1)S(1)} %collective-permute-done.refs_1_), channel_id=1, source_target_pairs={{0,4},{4,8},{8,12},{12,16},{16,20},{20,24},{24,28},{28,32},{32,36}... | collective-permute-start | bytes 1179656 | tf_op jit(solution)/shard_map/ppermute | solution.py:43
  103.9 12.1 %copy-start = (bf16[1,512,1024]{2,1,0:T(8,128)(2,1)S(1)}, bf16[1,512,1024]{2,1,0:T(8,128)(2,1)}, u32[]{:S(2)}) copy-start(bf16[1,512,1024]{2,1,0:T(8,128)(2,1)} %param.15) | copy-start | bytes 3145732
  116.6 12.5 %copy-start.7 = (f32[16,2]{0,1:T(2,128)S(1)}, f32[16,2]{0,1:T(2,128)}, u32[]{:S(2)}) copy-start(f32[16,2]{0,1:T(2,128)} %param.12) | copy-start | bytes 388
  116.6 12.6 %copy-start.3 = (bf16[8,16,1024]{2,1,0:T(8,128)(2,1)S(1)}, bf16[8,16,1024]{2,1,0:T(8,128)(2,1)}, u32[]{:S(2)}) copy-start(bf16[8,16,1024]{2,1,0:T(8,128)(2,1)} %past_ref.1) | copy-start | bytes 786436
  116.6 12.6 %copy-start.4 = (s32[16,2]{0,1:T(2,128)S(1)}, s32[16,2]{0,1:T(2,128)}, u32[]{:S(2)}) copy-start(s32[16,2]{0,1:T(2,128)} %param.11) | copy-start | bytes 388
  116.6 12.6 %copy-start.5 = (f32[9]{0:T(128)S(1)}, f32[9]{0:T(128)}, u32[]{:S(2)}) copy-start(f32[9]{0:T(128)} %dwa_ref.1) | copy-start | bytes 112
  116.6 21.7 %copy-start.1 = (bf16[384,384]{1,0:T(8,128)(2,1)S(1)}, bf16[384,384]{1,0:T(8,128)(2,1)}, u32[]{:S(2)}) copy-start(bf16[384,384]{1,0:T(8,128)(2,1)} %constant.59.clone.order_ref) | copy-start | bytes 884740
  116.6 9.0 %collective-permute-start.6 = (bf16[192,1024]{1,0:T(8,128)(2,1)S(1)}, bf16[192,1024]{1,0:T(8,128)(2,1)S(1)}, u32[]{:S(2)}, u32[]{:S(2)}) collective-permute-start(bf16[192,1024]{1,0:T(8,128)(2,1)S(1)} %get-tuple-element.35), channel_id=1, source_target_pairs={{0,60},{4,0},{8,4},{12,8},{16,12},{20,16},{24,20},{28,24},{32,28},... | collective-permute-start | bytes 1179656 | tf_op jit(solution)/shard_map/ppermute | solution.py:43
  121.0 12.4 %collective-permute-start.8 = (bf16[192,1024]{1,0:T(8,128)(2,1)S(1)}, bf16[192,1024]{1,0:T(8,128)(2,1)S(1)}, u32[]{:S(2)}, u32[]{:S(2)}) collective-permute-start(bf16[192,1024]{1,0:T(8,128)(2,1)S(1)} %get-tuple-element.36), channel_id=1, source_target_pairs={{0,4},{4,8},{8,12},{12,16},{16,20},{20,24},{24,28},{28,32},{32,36}... | collective-permute-start | bytes 1179656 | tf_op jit(solution)/shard_map/ppermute | solution.py:43
  125.7 12.6 %collective-permute-start.7 = (bf16[192,1024]{1,0:T(8,128)(2,1)S(1)}, bf16[192,1024]{1,0:T(8,128)(2,1)S(1)}, u32[]{:S(2)}, u32[]{:S(2)}) collective-permute-start(bf16[192,1024]{1,0:T(8,128)(2,1)S(1)} %add_convert_fusion), channel_id=1, source_target_pairs={{0,60},{4,0},{8,4},{12,8},{16,12},{20,16},{24,20},{28,24},{32,28},... | collective-permute-start | bytes 1179656 | tf_op jit(solution)/shard_map/ppermute | solution.py:43

commit v12 on v10

--- a/solution.py
+++ b/solution.py
@@ -81,15 +81,18 @@
     return jnp.dot(ids.astype(jnp.float32), spread, preferred_element_type=jnp.float32)
 
 
-def assigned_slots(ids, experts, tok_rows):
+def earlier_tokens(tok_rows):
+    source = lax.broadcasted_iota(jnp.int32, (LANES, LANES), 0)
+    token = lax.broadcasted_iota(jnp.int32, (LANES, LANES), 1) % tok_rows
+    return (source < token).astype(jnp.float32)
+
+
+def assigned_slots(ids, experts, before):
     ids = repeated_ids(ids)
     choices, lanes = ids.shape
     expert = lax.broadcasted_iota(jnp.int32, (experts, lanes), 0).astype(jnp.float32)
     chosen = [ids[place : place + 1, :] == expert for place in range(choices)]
     named = sum(mask.astype(jnp.float32) for mask in chosen)
-    source = lax.broadcasted_iota(jnp.int32, (lanes, lanes), 0)
-    token = lax.broadcasted_iota(jnp.int32, (lanes, lanes), 1) % tok_rows
-    before = (source < token).astype(jnp.float32)
     earlier = jnp.dot(named, before, preferred_element_type=jnp.float32)
     return [jnp.where(mask, earlier, -1.0) for mask in chosen]
 
@@ -121,8 +124,9 @@
         copy = pltpu.make_async_copy(tokens_ref.at[:, pl.ds(first, quarter)], own_ref, arrived)
         ids_copy.start()
         copy.start()
+        before = earlier_tokens(tok_rows)
         ids_copy.wait()
-        slots = assigned_slots(ids_ref[...], experts, tok_rows)
+        slots = assigned_slots(ids_ref[...], experts, before)
         chosen = placed(slots, [1.0] * len(slots), capacity, tok_rows).astype(jnp.bfloat16)
         copy.wait()
         tall = [own_ref[:, block * LANES : (block + 1) * LANES] for block in range(blocks)]
@@ -223,7 +227,7 @@
     return weights
 
 
-def gate_up_parts(sets, weights):
+def gate_up_parts(sets, weights, dtypes):
     width = weights[0].shape[1]
     set_rows = sets[0].shape[0]
     rows = set_rows * len(sets)
@@ -236,7 +240,6 @@
             out = jnp.dot(stacked, w_ref[...], preferred_element_type=jnp.float32)
             out_ref[...] = out.astype(out_ref.dtype)
 
-    dtypes = [jnp.float32] * 2 + [jnp.bfloat16] * 2
     shapes = [jax.ShapeDtypeStruct((rows, width), dtype) for dtype in dtypes]
     return call(kernel, shapes, *sets, *weights)
 
@@ -264,13 +267,14 @@
     return call(kernel, shape, own, *others)
 
 
-def down_sets(hidden, w_down, dtypes):
+def down_sets(hidden, w_down, count, places, dtypes):
     parts, rows, _ = hidden.shape
-    set_rows = rows // len(dtypes)
+    set_rows = rows // count
     features = w_down.shape[1]
 
     def kernel(hidden_ref, w_ref, *out_refs):
-        wide = jnp.concatenate([hidden_ref[part] for part in range(parts)], axis=1)
+        taken = slice(places[0] * set_rows, (places[-1] + 1) * set_rows)
+        wide = jnp.concatenate([hidden_ref[part, taken, :] for part in range(parts)], axis=1)
         out = jnp.dot(wide, w_ref[...], preferred_element_type=jnp.float32)
         for place, ref in enumerate(out_refs):
             ref[...] = out[place * set_rows : (place + 1) * set_rows].astype(ref.dtype)
@@ -285,7 +289,7 @@
     depth = past_layers.shape[0]
 
     def kernel(dwa_ref, ids_ref, route_ref, own_ref, past_ref, terms_ref, base_ref):
-        slots = assigned_slots(ids_ref[...], experts, tok_rows)
+        slots = assigned_slots(ids_ref[...], experts, earlier_tokens(tok_rows))
         route = route_ref[...]
         total = sum(route[place : place + 1, :] for place in range(len(slots)))
         shares = [dwa_ref[depth] * (route[place : place + 1, :] / total) for place in range(len(slots))]
@@ -353,12 +357,19 @@
     arrived = far_exchange(packed)
     own_set = wide_rows(arrived, jnp.asarray(order, jnp.bfloat16), capacity)
     sets = window_sets(own_set)
-    own, *others = gate_up_parts(sets, weights)
-    hidden = lax.all_gather(hidden_units(own, tensor_sums(*others)), "tensor", axis=0, tiled=False)
-    own, *others = down_sets(hidden, down_weight[0], [jnp.float32] * 2 + [jnp.bfloat16] * 2)
+    *weights, far_weights = weights
+    (opposite,) = gate_up_parts(sets, [far_weights], [jnp.bfloat16])
+    sets, opposite = lax.optimization_barrier((sets, opposite))
+    own, following, previous = gate_up_parts(sets, weights, [jnp.float32] * 2 + [jnp.bfloat16])
+    units = hidden_units(own, tensor_sums(following, previous, opposite))
+    hidden = lax.all_gather(units, "tensor", axis=0, tiled=False)
+    count = len(sets)
+    other, second = down_sets(hidden, down_weight[0], count, range(2, count), [jnp.bfloat16] * 2)
+    hidden, other, second = lax.optimization_barrier((hidden, other, second))
+    own, first = down_sets(hidden, down_weight[0], count, range(2), [jnp.float32] * 2)
     route, own = lax.optimization_barrier((route, own))
     terms, base = mix_terms(ids, route, own_columns, past_layers, dwa_weight, experts, capacity)
-    others = returned_sums(*others)
+    others = returned_sums(first, other, second)
     own, terms, base = lax.optimization_barrier((own, terms, base))
     returned = far_exchange(summed_chunks(own, others, jnp.asarray(order.T, jnp.bfloat16), capacity))
     return mixed_layers(returned, terms, base, tokens.dtype)

time: 175 us -> 174 us (level)
  the two profiles are of different devices: /device:TPU:75 before, /device:TPU:1 now
where the time goes in v12:
time: 174 us; the launch traced here: 173 us
  starting transfers between devices  60.8 us (35%)
  waiting for transfers between devices  52.2 us (30%)
  blocking collectives  50.1 us (29%)
  Pallas kernels  7.95 us (5%)
    all_to_all x1, blocking collectives, far_exchange(): lax.all_to_all(chunks, ('expert', 'dp'), 0, 0, tiled=True, axis_index_gro...  37.4 us
    all_to_all x1, waiting for transfers between devices, far_exchange(): lax.all_to_all(chunks, ('expert', 'dp'), 0, 0, tiled=True, axis_index_gro...  22.6 us
    ppermute x6, starting transfers between devices, shifted(): return lax.ppermute(shard, ('expert', 'dp'), pairs)  22.1 us
    all_to_all x1, starting transfers between devices, far_exchange(): lax.all_to_all(chunks, ('expert', 'dp'), 0, 0, tiled=True, axis_index_gro...  19.5 us
    ppermute x6, starting transfers between devices, along_tensor(): return lax.ppermute(shard, ('expert', 'tensor'), pairs)  19.2 us
    ppermute x6, waiting for transfers between devices, along_tensor(): return lax.ppermute(shard, ('expert', 'tensor'), pairs)  16.6 us
    ppermute x6, waiting for transfers between devices, shifted(): return lax.ppermute(shard, ('expert', 'dp'), pairs)  13.1 us
    all_gather x1, blocking collectives, per_device(): hidden = lax.all_gather(units, 'tensor', axis=0, tiled=False)  12.7 us
  transfers between devices with their start and end apart: 13, of which 9 were waited for; matrix products, arithmetic and copies ran while one was open for 1% of the time, Pallas kernels for 2%

profile of v12, /device:TPU:1, one launch (start us, length us, event | category | flops | bytes accessed | tf_op | source)
XLA Modules:
  0.0 173.3 jit_solution(10733977609939942836)
XLA Ops:
  0.0 1.9 %packed_rows.1 = (bf16[32,48,128]{2,1,0:T(8,128)(2,1)}, bf16[16,1024]{1,0:T(8,128)(2,1)S(1)}) custom-call(s32[1]{0:T(128)} %bitcast.1.first_ref, s32[2,16]{1,0:T(2,128)} %bitcast.27, bf16[16,4096]{1,0:T(8,128)(2,1)} %tokens_ref.1), custom_call_target="tpu_custom_call" | custom-call | tf_op jit(solution)/shard_map/packed_rows/pallas_call | solution.py:140
  1.9 19.5 %all-to-all-start = ((bf16[32,48,128]{2,1,0:T(8,128)(2,1)}), bf16[32,48,128]{2,1,0:T(8,128)(2,1)S(1)}, u32[]{:S(2)}, u32[]{:S(2)}) async-start(bf16[32,48,128]{2,1,0:T(8,128)(2,1)} %get-tuple-element.29), calls=%async_computation | async-start | bytes 786432 | tf_op jit(solution)/shard_map/all_to_all | solution.py:32
  21.5 22.6 %all-to-all-done.in_ref = bf16[32,48,128]{2,1,0:T(8,128)(2,1)S(1)} async-done(((bf16[32,48,128]{2,1,0:T(8,128)(2,1)}), bf16[32,48,128]{2,1,0:T(8,128)(2,1)S(1)}, u32[]{:S(2)}, u32[]{:S(2)}) %all-to-all-start) | async-done | bytes 393248 | tf_op jit(solution)/shard_map/all_to_all | solution.py:32
  44.6 7.0 %collective-permute-start = (bf16[192,1024]{1,0:T(8,128)(2,1)S(1)}, bf16[192,1024]{1,0:T(8,128)(2,1)S(1)}, u32[]{:S(2)}, u32[]{:S(2)}) collective-permute-start(bf16[192,1024]{1,0:T(8,128)(2,1)S(1)} %shard_map.100.refs_0_), channel_id=1, source_target_pairs={{0,4},{4,8},{8,12},{12,16},{16,20},{20,24},{24,28},{28,32},{32,36}... | collective-permute-start | bytes 1179656 | tf_op jit(solution)/shard_map/ppermute | solution.py:42
  51.6 1.4 dynamic-slice_bitcast_fusion
  53.0 4.7 %collective-permute-start.3 = (bf16[1024,256]{1,0:T(8,128)(2,1)S(1)}, bf16[1024,256]{1,0:T(8,128)(2,1)S(1)}, u32[]{:S(2)}, u32[]{:S(2)}) collective-permute-start(bf16[1024,256]{1,0:T(8,128)(2,1)S(1)} %pad_maximum_fusion), channel_id=1, source_target_pairs={{0,2},{1,3},{2,0},{3,1},{64,66},{65,67},{66,64},{67,65},{128,130},... | collective-permute-start | bytes 1572872 | tf_op jit(solution)/shard_map/ppermute | solution.py:209
  57.7 3.9 %collective-permute-start.1 = (bf16[192,1024]{1,0:T(8,128)(2,1)S(1)}, bf16[192,1024]{1,0:T(8,128)(2,1)S(1)}, u32[]{:S(2)}, u32[]{:S(2)}) collective-permute-start(bf16[192,1024]{1,0:T(8,128)(2,1)S(1)} %shard_map.100.refs_0_), channel_id=1, source_target_pairs={{0,60},{4,0},{8,4},{12,8},{16,12},{20,16},{24,20},{28,24},{32,28},... | collective-permute-start | bytes 1179656 | tf_op jit(solution)/shard_map/ppermute | solution.py:42
  61.6 2.6 %collective-permute-start.2 = (bf16[192,1024]{1,0:T(8,128)(2,1)S(1)}, bf16[192,1024]{1,0:T(8,128)(2,1)S(1)}, u32[]{:S(2)}, u32[]{:S(2)}) collective-permute-start(bf16[192,1024]{1,0:T(8,128)(2,1)S(1)} %collective-permute-done.refs_1_), channel_id=1, source_target_pairs={{0,4},{4,8},{8,12},{12,16},{16,20},{20,24},{24,28},{28,32},{32,36}... | collective-permute-start | bytes 1179656 | tf_op jit(solution)/shard_map/ppermute | solution.py:42
  64.3 2.8 %collective-permute-start.5 = (bf16[1024,256]{1,0:T(8,128)(2,1)S(1)}, bf16[1024,256]{1,0:T(8,128)(2,1)S(1)}, u32[]{:S(2)}, u32[]{:S(2)}) collective-permute-start(bf16[1024,256]{1,0:T(8,128)(2,1)S(1)} %pad_maximum_fusion.3), channel_id=1, source_target_pairs={{0,1},{1,2},{2,3},{3,0},{64,67},{65,64},{66,65},{67,66},{128,129},... | collective-permute-start | bytes 1572872 | tf_op jit(solution)/shard_map/ppermute | solution.py:209
  67.1 2.5 %collective-permute-start.4 = (bf16[1024,256]{1,0:T(8,128)(2,1)S(1)}, bf16[1024,256]{1,0:T(8,128)(2,1)S(1)}, u32[]{:S(2)}, u32[]{:S(2)}) collective-permute-start(bf16[1024,256]{1,0:T(8,128)(2,1)S(1)} %pad_maximum_fusion.2), channel_id=1, source_target_pairs={{0,3},{1,0},{2,1},{3,2},{64,65},{65,66},{66,67},{67,64},{128,131},... | collective-permute-start | bytes 1572872 | tf_op jit(solution)/shard_map/ppermute | solution.py:209
  69.7 2.6 %collective-permute-done.2.refs_3_ = bf16[192,1024]{1,0:T(8,128)(2,1)S(1)} collective-permute-done((bf16[192,1024]{1,0:T(8,128)(2,1)S(1)}, bf16[192,1024]{1,0:T(8,128)(2,1)S(1)}, u32[]{:S(2)}, u32[]{:S(2)}) %collective-permute-start.2) | collective-permute-done | bytes 393248 | tf_op jit(solution)/shard_map/ppermute | solution.py:42
  72.3 0.6 shard_map.101
  72.8 2.8 %collective-permute-start.6 = (bf16[768,256]{1,0:T(8,128)(2,1)S(1)}, bf16[768,256]{1,0:T(8,128)(2,1)S(1)}, u32[]{:S(2)}, u32[]{:S(2)}) collective-permute-start(bf16[768,256]{1,0:T(8,128)(2,1)S(1)} %shard_map.101), channel_id=1, source_target_pairs={{0,1},{1,2},{2,3},{3,0},{64,67},{65,64},{66,65},{67,66},{128,129},... | collective-permute-start | bytes 1179656 | tf_op jit(solution)/shard_map/ppermute | solution.py:209
  75.7 4.1 %collective-permute-done.5.refs_6_ = bf16[1024,256]{1,0:T(8,128)(2,1)S(1)} collective-permute-done((bf16[1024,256]{1,0:T(8,128)(2,1)S(1)}, bf16[1024,256]{1,0:T(8,128)(2,1)S(1)}, u32[]{:S(2)}, u32[]{:S(2)}) %collective-permute-start.5) | collective-permute-done | bytes 524320 | tf_op jit(solution)/shard_map/ppermute | solution.py:209
  79.8 4.4 %collective-permute-done.4.refs_5_ = bf16[1024,256]{1,0:T(8,128)(2,1)S(1)} collective-permute-done((bf16[1024,256]{1,0:T(8,128)(2,1)S(1)}, bf16[1024,256]{1,0:T(8,128)(2,1)S(1)}, u32[]{:S(2)}, u32[]{:S(2)}) %collective-permute-start.4) | collective-permute-done | bytes 524320 | tf_op jit(solution)/shard_map/ppermute | solution.py:209
  84.2 1.4 shard_map.102
  85.6 1.9 %collective-permute-start.8 = (bf16[768,256]{1,0:T(8,128)(2,1)S(1)}, bf16[768,256]{1,0:T(8,128)(2,1)S(1)}, u32[]{:S(2)}, u32[]{:S(2)}) collective-permute-start(bf16[768,256]{1,0:T(8,128)(2,1)S(1)} %get-tuple-element.37), channel_id=1, source_target_pairs={{0,3},{1,0},{2,1},{3,2},{64,65},{65,66},{66,67},{67,64},{128,131},... | collective-permute-start | bytes 1179656 | tf_op jit(solution)/shard_map/ppermute | solution.py:209
  87.6 4.6 %collective-permute-start.7 = (bf16[768,256]{1,0:T(8,128)(2,1)S(1)}, bf16[768,256]{1,0:T(8,128)(2,1)S(1)}, u32[]{:S(2)}, u32[]{:S(2)}) collective-permute-start(bf16[768,256]{1,0:T(8,128)(2,1)S(1)} %add_convert_fusion.1), channel_id=1, source_target_pairs={{0,1},{1,2},{2,3},{3,0},{64,67},{65,64},{66,65},{67,66},{128,129},... | collective-permute-start | bytes 1179656 | tf_op jit(solution)/shard_map/ppermute | solution.py:209
  92.2 3.1 %collective-permute-done.8.refs_1_ = bf16[768,256]{1,0:T(8,128)(2,1)S(1)} collective-permute-done((bf16[768,256]{1,0:T(8,128)(2,1)S(1)}, bf16[768,256]{1,0:T(8,128)(2,1)S(1)}, u32[]{:S(2)}, u32[]{:S(2)}) %collective-permute-start.8) | collective-permute-done | bytes 393248 | tf_op jit(solution)/shard_map/ppermute | solution.py:209
  95.3 4.9 %collective-permute-done.7.refs_0_ = bf16[768,256]{1,0:T(8,128)(2,1)S(1)} collective-permute-done((bf16[768,256]{1,0:T(8,128)(2,1)S(1)}, bf16[768,256]{1,0:T(8,128)(2,1)S(1)}, u32[]{:S(2)}, u32[]{:S(2)}) %collective-permute-start.7) | collective-permute-done | bytes 393248 | tf_op jit(solution)/shard_map/ppermute | solution.py:209
  100.5 12.7 %all-gather = bf16[3072,128]{1,0:T(8,128)(2,1)S(1)} all-gather(bf16[768,128]{1,0:T(8,128)(2,1)S(1)} %shard_map.103), channel_id=2, replica_groups=mesh['expert'=8,'dp'=16,'tensor'=4] {'tensor'}, dimensions={0}, use_global_device_ids=true | all-gather | bytes 983040 | tf_op jit(solution)/shard_map/all_gather | solution.py:365
  113.1 0.6 shard_map.104
  113.7 2.2 %collective-permute-start.9 = (bf16[192,1024]{1,0:T(8,128)(2,1)S(1)}, bf16[192,1024]{1,0:T(8,128)(2,1)S(1)}, u32[]{:S(2)}, u32[]{:S(2)}) collective-permute-start(bf16[192,1024]{1,0:T(8,128)(2,1)S(1)} %get-tuple-element.51), channel_id=1, source_target_pairs={{0,60},{4,0},{8,4},{12,8},{16,12},{20,16},{24,20},{28,24},{32,28},... | collective-permute-start | bytes 1179656 | tf_op jit(solution)/shard_map/ppermute | solution.py:42
  115.9 0.6 shard_map.105
  116.5 4.3 %collective-permute-start.11 = (bf16[192,1024]{1,0:T(8,128)(2,1)S(1)}, bf16[192,1024]{1,0:T(8,128)(2,1)S(1)}, u32[]{:S(2)}, u32[]{:S(2)}) collective-permute-start(bf16[192,1024]{1,0:T(8,128)(2,1)S(1)} %get-tuple-element.52), channel_id=1, source_target_pairs={{0,4},{4,8},{8,12},{12,16},{16,20},{20,24},{24,28},{28,32},{32,36}... | collective-permute-start | bytes 1179656 | tf_op jit(solution)/shard_map/ppermute | solution.py:42
  120.8 2.6 %collective-permute-done.9 = bf16[192,1024]{1,0:T(8,128)(2,1)S(1)} collective-permute-done((bf16[192,1024]{1,0:T(8,128)(2,1)S(1)}, bf16[192,1024]{1,0:T(8,128)(2,1)S(1)}, u32[]{:S(2)}, u32[]{:S(2)}) %collective-permute-start.9) | collective-permute-done | bytes 393248 | tf_op jit(solution)/shard_map/ppermute | solution.py:42
  123.6 2.1 %collective-permute-start.10 = (bf16[192,1024]{1,0:T(8,128)(2,1)S(1)}, bf16[192,1024]{1,0:T(8,128)(2,1)S(1)}, u32[]{:S(2)}, u32[]{:S(2)}) collective-permute-start(bf16[192,1024]{1,0:T(8,128)(2,1)S(1)} %add_convert_fusion), channel_id=1, source_target_pairs={{0,60},{4,0},{8,4},{12,8},{16,12},{20,16},{24,20},{28,24},{32,28},... | collective-permute-start | bytes 1179656 | tf_op jit(solution)/shard_map/ppermute | solution.py:42
  125.7 0.9 shard_map.106
  126.7 2.5 %collective-permute-done.11.refs_1_ = bf16[192,1024]{1,0:T(8,128)(2,1)S(1)} collective-permute-done((bf16[192,1024]{1,0:T(8,128)(2,1)S(1)}, bf16[192,1024]{1,0:T(8,128)(2,1)S(1)}, u32[]{:S(2)}, u32[]{:S(2)}) %collective-permute-start.11) | collective-permute-done | bytes 393248 | tf_op jit(solution)/shard_map/ppermute | solution.py:42
  129.1 5.4 %collective-permute-done.10.refs_0_ = bf16[192,1024]{1,0:T(8,128)(2,1)S(1)} collective-permute-done((bf16[192,1024]{1,0:T(8,128)(2,1)S(1)}, bf16[192,1024]{1,0:T(8,128)(2,1)S(1)}, u32[]{:S(2)}, u32[]{:S(2)}) %collective-permute-start.10) | collective-permute-done | bytes 393248 | tf_op jit(solution)/shard_map/ppermute | solution.py:42
  135.0 37.4 %all_to_all.10.in_ref = bf16[32,48,128]{2,1,0:T(8,128)(2,1)S(1)} all-to-all(bf16[32,48,128]{2,1,0:T(8,128)(2,1)S(1)} %shard_map.107), channel_id=1, replica_groups={{0,16,32,48,64,80,96,112,128,144,160,176,192,208,224,240,256,272,288,30..., dimensions={0} | all-to-all | bytes 786432 | tf_op jit(solution)/shard_map/all_to_all | solution.py:32
  172.4 0.9 shard_map.108
  (31 shorter events, 1.7 us)
Async XLA Ops:
  1.9 42.2 %copy-start.2 = (bf16[384,384]{1,0:T(8,128)(2,1)S(1)}, bf16[384,384]{1,0:T(8,128)(2,1)}, u32[]{:S(2)}) copy-start(bf16[384,384]{1,0:T(8,128)(2,1)} %constant.73.clone.order_ref) | copy-start | bytes 884740
  1.9 49.7 %copy-start.6 = (bf16[1,4096,128]{2,1,0:T(8,128)(2,1)S(1)}, bf16[1,4096,128]{2,1,0:T(8,128)(2,1)}, u32[]{:S(2)}) copy-start(bf16[1,4096,128]{2,1,0:T(8,128)(2,1)} %param.14) | copy-start | bytes 3145732
  1.9 42.2 %all-to-all-start = ((bf16[32,48,128]{2,1,0:T(8,128)(2,1)}), bf16[32,48,128]{2,1,0:T(8,128)(2,1)S(1)}, u32[]{:S(2)}, u32[]{:S(2)}) async-start(bf16[32,48,128]{2,1,0:T(8,128)(2,1)} %get-tuple-element.29), calls=%async_computation | async-start | bytes 786432 | tf_op jit(solution)/shard_map/all_to_all | solution.py:32
  44.6 17.1 %collective-permute-start = (bf16[192,1024]{1,0:T(8,128)(2,1)S(1)}, bf16[192,1024]{1,0:T(8,128)(2,1)S(1)}, u32[]{:S(2)}, u32[]{:S(2)}) collective-permute-start(bf16[192,1024]{1,0:T(8,128)(2,1)S(1)} %shard_map.100.refs_0_), channel_id=1, source_target_pairs={{0,4},{4,8},{8,12},{12,16},{16,20},{20,24},{24,28},{28,32},{32,36}... | collective-permute-start | bytes 1179656 | tf_op jit(solution)/shard_map/ppermute | solution.py:42
  53.0 16.6 %collective-permute-start.3 = (bf16[1024,256]{1,0:T(8,128)(2,1)S(1)}, bf16[1024,256]{1,0:T(8,128)(2,1)S(1)}, u32[]{:S(2)}, u32[]{:S(2)}) collective-permute-start(bf16[1024,256]{1,0:T(8,128)(2,1)S(1)} %pad_maximum_fusion), channel_id=1, source_target_pairs={{0,2},{1,3},{2,0},{3,1},{64,66},{65,67},{66,64},{67,65},{128,130},... | collective-permute-start | bytes 1572872 | tf_op jit(solution)/shard_map/ppermute | solution.py:209
  57.7 12.0 %collective-permute-start.1 = (bf16[192,1024]{1,0:T(8,128)(2,1)S(1)}, bf16[192,1024]{1,0:T(8,128)(2,1)S(1)}, u32[]{:S(2)}, u32[]{:S(2)}) collective-permute-start(bf16[192,1024]{1,0:T(8,128)(2,1)S(1)} %shard_map.100.refs_0_), channel_id=1, source_target_pairs={{0,60},{4,0},{8,4},{12,8},{16,12},{20,16},{24,20},{28,24},{32,28},... | collective-permute-start | bytes 1179656 | tf_op jit(solution)/shard_map/ppermute | solution.py:42
  61.6 10.6 %collective-permute-start.2 = (bf16[192,1024]{1,0:T(8,128)(2,1)S(1)}, bf16[192,1024]{1,0:T(8,128)(2,1)S(1)}, u32[]{:S(2)}, u32[]{:S(2)}) collective-permute-start(bf16[192,1024]{1,0:T(8,128)(2,1)S(1)} %collective-permute-done.refs_1_), channel_id=1, source_target_pairs={{0,4},{4,8},{8,12},{12,16},{16,20},{20,24},{24,28},{28,32},{32,36}... | collective-permute-start | bytes 1179656 | tf_op jit(solution)/shard_map/ppermute | solution.py:42
  64.3 15.5 %collective-permute-start.5 = (bf16[1024,256]{1,0:T(8,128)(2,1)S(1)}, bf16[1024,256]{1,0:T(8,128)(2,1)S(1)}, u32[]{:S(2)}, u32[]{:S(2)}) collective-permute-start(bf16[1024,256]{1,0:T(8,128)(2,1)S(1)} %pad_maximum_fusion.3), channel_id=1, source_target_pairs={{0,1},{1,2},{2,3},{3,0},{64,67},{65,64},{66,65},{67,66},{128,129},... | collective-permute-start | bytes 1572872 | tf_op jit(solution)/shard_map/ppermute | solution.py:209
  67.1 17.0 %collective-permute-start.4 = (bf16[1024,256]{1,0:T(8,128)(2,1)S(1)}, bf16[1024,256]{1,0:T(8,128)(2,1)S(1)}, u32[]{:S(2)}, u32[]{:S(2)}) collective-permute-start(bf16[1024,256]{1,0:T(8,128)(2,1)S(1)} %pad_maximum_fusion.2), channel_id=1, source_target_pairs={{0,3},{1,0},{2,1},{3,2},{64,65},{65,66},{66,67},{67,64},{128,131},... | collective-permute-start | bytes 1572872 | tf_op jit(solution)/shard_map/ppermute | solution.py:209
  72.8 14.7 %collective-permute-start.6 = (bf16[768,256]{1,0:T(8,128)(2,1)S(1)}, bf16[768,256]{1,0:T(8,128)(2,1)S(1)}, u32[]{:S(2)}, u32[]{:S(2)}) collective-permute-start(bf16[768,256]{1,0:T(8,128)(2,1)S(1)} %shard_map.101), channel_id=1, source_target_pairs={{0,1},{1,2},{2,3},{3,0},{64,67},{65,64},{66,65},{67,66},{128,129},... | collective-permute-start | bytes 1179656 | tf_op jit(solution)/shard_map/ppermute | solution.py:209
  85.6 9.7 %collective-permute-start.8 = (bf16[768,256]{1,0:T(8,128)(2,1)S(1)}, bf16[768,256]{1,0:T(8,128)(2,1)S(1)}, u32[]{:S(2)}, u32[]{:S(2)}) collective-permute-start(bf16[768,256]{1,0:T(8,128)(2,1)S(1)} %get-tuple-element.37), channel_id=1, source_target_pairs={{0,3},{1,0},{2,1},{3,2},{64,65},{65,66},{66,67},{67,64},{128,131},... | collective-permute-start | bytes 1179656 | tf_op jit(solution)/shard_map/ppermute | solution.py:209
  87.6 12.6 %collective-permute-start.7 = (bf16[768,256]{1,0:T(8,128)(2,1)S(1)}, bf16[768,256]{1,0:T(8,128)(2,1)S(1)}, u32[]{:S(2)}, u32[]{:S(2)}) collective-permute-start(bf16[768,256]{1,0:T(8,128)(2,1)S(1)} %add_convert_fusion.1), channel_id=1, source_target_pairs={{0,1},{1,2},{2,3},{3,0},{64,67},{65,64},{66,65},{67,66},{128,129},... | collective-permute-start | bytes 1179656 | tf_op jit(solution)/shard_map/ppermute | solution.py:209
  100.2 12.9 %copy-start = (bf16[1,512,1024]{2,1,0:T(8,128)(2,1)S(1)}, bf16[1,512,1024]{2,1,0:T(8,128)(2,1)}, u32[]{:S(2)}) copy-start(bf16[1,512,1024]{2,1,0:T(8,128)(2,1)} %param.15) | copy-start | bytes 3145732
  113.7 9.7 %collective-permute-start.9 = (bf16[192,1024]{1,0:T(8,128)(2,1)S(1)}, bf16[192,1024]{1,0:T(8,128)(2,1)S(1)}, u32[]{:S(2)}, u32[]{:S(2)}) collective-permute-start(bf16[192,1024]{1,0:T(8,128)(2,1)S(1)} %get-tuple-element.51), channel_id=1, source_target_pairs={{0,60},{4,0},{8,4},{12,8},{16,12},{20,16},{24,20},{28,24},{32,28},... | collective-permute-start | bytes 1179656 | tf_op jit(solution)/shard_map/ppermute | solution.py:42
  116.5 12.7 %collective-permute-start.11 = (bf16[192,1024]{1,0:T(8,128)(2,1)S(1)}, bf16[192,1024]{1,0:T(8,128)(2,1)S(1)}, u32[]{:S(2)}, u32[]{:S(2)}) collective-permute-start(bf16[192,1024]{1,0:T(8,128)(2,1)S(1)} %get-tuple-element.52), channel_id=1, source_target_pairs={{0,4},{4,8},{8,12},{12,16},{16,20},{20,24},{24,28},{28,32},{32,36}... | collective-permute-start | bytes 1179656 | tf_op jit(solution)/shard_map/ppermute | solution.py:42
  123.4 2.2 %copy-start.7 = (f32[16,2]{0,1:T(2,128)S(1)}, f32[16,2]{0,1:T(2,128)}, u32[]{:S(2)}) copy-start(f32[16,2]{0,1:T(2,128)} %param.12) | copy-start | bytes 388
  123.4 2.3 %copy-start.3 = (bf16[8,16,1024]{2,1,0:T(8,128)(2,1)S(1)}, bf16[8,16,1024]{2,1,0:T(8,128)(2,1)}, u32[]{:S(2)}) copy-start(bf16[8,16,1024]{2,1,0:T(8,128)(2,1)} %past_ref.1) | copy-start | bytes 786436
  123.4 2.3 %copy-start.4 = (s32[16,2]{0,1:T(2,128)S(1)}, s32[16,2]{0,1:T(2,128)}, u32[]{:S(2)}) copy-start(s32[16,2]{0,1:T(2,128)} %param.11) | copy-start | bytes 388
  123.4 2.3 %copy-start.5 = (f32[9]{0:T(128)S(1)}, f32[9]{0:T(128)}, u32[]{:S(2)}) copy-start(f32[9]{0:T(128)} %dwa_ref.1) | copy-start | bytes 112
  123.5 10.9 %copy-start.1 = (bf16[384,384]{1,0:T(8,128)(2,1)S(1)}, bf16[384,384]{1,0:T(8,128)(2,1)}, u32[]{:S(2)}) copy-start(bf16[384,384]{1,0:T(8,128)(2,1)} %constant.74.clone.order_ref) | copy-start | bytes 884740
  123.6 10.9 %collective-permute-start.10 = (bf16[192,1024]{1,0:T(8,128)(2,1)S(1)}, bf16[192,1024]{1,0:T(8,128)(2,1)S(1)}, u32[]{:S(2)}, u32[]{:S(2)}) collective-permute-start(bf16[192,1024]{1,0:T(8,128)(2,1)S(1)} %add_convert_fusion), channel_id=1, source_target_pairs={{0,60},{4,0},{8,4},{12,8},{16,12},{20,16},{24,20},{28,24},{32,28},... | collective-permute-start | bytes 1179656 | tf_op jit(solution)/shard_map/ppermute | solution.py:42
